TPU v7x, 32 devices: a whole 2x2x4 slice. The times are simulated.
32 devices in a mesh: rep: 2 (over x), stretch: 2 (over core), tp: 8 (over z, y).
Axes of the slice: x: 2, y: 2, z: 4, core: 2. Of those that a mesh axis runs over, the one named last changes fastest.
Arguments:
- query: bfloat16 [4, 512, 3072], P(('rep', 'stretch'), 'tp'), parts along dimension 0, may hold values from -64 to 64
- stretch_kv: bfloat16 [2, 4, 512, 3072], P(None, ('rep', 'stretch'), 'tp'), parts along dimension 1, may hold values from -6 to 6
- history_kv: bfloat16 [2, 4096, 3072], P(None, ('rep', 'tp')), parts along dimension 1, may hold values from -6 to 6
- block_mask: int32 [4, 4, 8], P(('rep', 'stretch')), parts along dimension 0, may hold values from 0 to 1, as said below
- noise_level: int32 [4], P(('rep', 'stretch')), parts along dimension 0, may hold values from 0 to 999
- history_blocks: int32 [2], P('rep'), parts along dimension 0, may hold values from 1 to 16
- out_weight: bfloat16 [3072, 6144], P(None, 'tp'), may hold values from -0.109375 to 0.109375
- gate_table: float32 [1000, 6144], P(None, 'tp'), may hold values from -6 to 6
Outputs:
- mixed: bfloat16 [4, 512, 6144], P(('rep', 'stretch'), None, 'tp'), parts along dimension 0
There are 2 independent parts, one for each index of `rep`. A program takes and returns all parts, laid end to end along the dimension named above; an argument that names none is the same for every part. Nothing has to cross between parts.
Inputs may be any that keep to these rules, and one draw needn't show every extreme that they name: block_mask[c, i, 4 + i] = 1 for every query block i; block_mask[0, i, j] = 0 for j < 4.
All inputs are finite; a program needn't handle non-finite values.
Results may differ from a plain program's by a relative error of at most 0.0049.
Values may be sent and summed in bfloat16 or wider, within the bound.
No kernel may reach another device: no remote copies, remote signals or barrier semaphores. Data moves between devices by JAX's collectives and lax.ppermute only.
A program may use at most 128 MiB of HBM per device.

v0:
```python
import math

import jax
import jax.numpy as jnp
from jax import lax
from jax.sharding import PartitionSpec as P

H = 24
HD = 128
BLK = 128


NEGATIVE = -1e30


def shifted(value, axis, steps):
    count = lax.axis_size(axis)
    first, last = (max(0, -steps), min(count, count - steps))
    return lax.ppermute(value, axis, [(source, source + steps) for source in range(first, last)])


def head_block(queries, key_rows, value_rows, allowed):
    key_count = key_rows.shape[0]
    head_count = queries.shape[1]
    key_heads = key_rows.reshape(key_count, head_count, HD)
    scores = jnp.einsum("qhd,khd->qhk", queries, key_heads, preferred_element_type=jnp.float32) * (
        1.0 / math.sqrt(HD)
    )
    scores = jnp.where(allowed[:, None, :], scores, NEGATIVE)
    row_peak = jnp.max(scores, axis=2)
    weights = jnp.where(allowed[:, None, :], jnp.exp(scores - row_peak[:, :, None]), 0.0)
    weight_sum = jnp.sum(weights, axis=2)
    output = None
    value_heads = value_rows.reshape(key_count, head_count, HD).astype(jnp.float32)
    output = jnp.einsum("qhk,khd->qhd", weights, value_heads, precision=lax.Precision.HIGHEST)
    return (row_peak, weight_sum, output)


def combine(earlier, later):
    row_peak = jnp.maximum(earlier[0], later[0])
    scale_one = jnp.exp(earlier[0] - row_peak)
    scale_two = jnp.exp(later[0] - row_peak)
    weight_sum = earlier[1] * scale_one + later[1] * scale_two
    output = None
    output = earlier[2] * scale_one[:, :, None] + later[2] * scale_two[:, :, None]
    return (row_peak, weight_sum, output)


def column_table(columns, block_count):
    return (columns[:, None] == jnp.arange(2 * block_count, dtype=jnp.int32)[None, :]).astype(
        jnp.float32
    )


def attend_all(
    queries,
    query_positions,
    fresh_keys,
    fresh_values,
    fresh_hot,
    mask_table,
    history_pair,
    history_live,
    span,
):
    row_count = queries.shape[0]
    head_count = queries.shape[1]
    block_count = mask_table.shape[0]
    query_hot = (
        (query_positions // BLK)[:, None] == jnp.arange(block_count, dtype=jnp.int32)[None, :]
    ).astype(jnp.float32)
    fresh_allowed = jnp.dot(jnp.dot(query_hot, mask_table), fresh_hot.T) > 0.5
    base_peak = jnp.full((row_count, head_count), NEGATIVE, jnp.float32)
    skipped = (
        base_peak,
        jnp.zeros((row_count, head_count), jnp.float32),
        jnp.zeros((row_count, head_count, HD), jnp.float32),
    )
    result = head_block(queries, fresh_keys, fresh_values, fresh_allowed)
    for sub_block in range(history_pair.shape[1] // span):
        lower_row = sub_block * span
        key_rows = history_pair[0, lower_row : lower_row + span]
        value_rows = history_pair[1, lower_row : lower_row + span]
        live_rows = history_live[lower_row : lower_row + span]
        allowed = jnp.broadcast_to(live_rows[None, :], (row_count, span))
        block_part = lax.cond(
            jnp.any(live_rows),
            lambda: head_block(queries, key_rows, value_rows, allowed),
            lambda: skipped,
        )
        result = combine(result, block_part)
    return result


def on_device(
    query, stretch_kv, history_kv, block_mask, noise_level, history_blocks, out_weight, gate_table
):
    tp_count = lax.axis_size("tp")
    tp_index = lax.axis_index("tp")
    local_rows = query.shape[1]
    feature_width = query.shape[2]
    history_rows = history_kv.shape[1]
    block_count = block_mask.shape[1]
    own_pair = stretch_kv[:, 0]
    older_pair = shifted(own_pair, "stretch", 1)
    mask_table = block_mask[0].astype(jnp.float32)
    live_limit = history_blocks[0] * BLK
    fresh_keys = jnp.concatenate([older_pair[0], own_pair[0]], 0)
    fresh_values = jnp.concatenate([older_pair[1], own_pair[1]], 0)
    own_positions = tp_index * local_rows + jnp.arange(local_rows, dtype=jnp.int32)
    fresh_hot = column_table(
        jnp.concatenate([own_positions // BLK, block_count + own_positions // BLK], 0), block_count
    )
    history_positions = tp_index * history_rows + jnp.arange(history_rows, dtype=jnp.int32)
    history_live = history_positions < live_limit
    piece = lax.all_gather(query[0], "tp", axis=0, tiled=True)
    row_count = piece.shape[0]
    positions = jnp.arange(row_count, dtype=jnp.int32)
    row_peak, weight_sum, output = attend_all(
        piece.reshape(row_count, H, HD),
        positions,
        fresh_keys,
        fresh_values,
        fresh_hot,
        mask_table,
        history_kv,
        history_live,
        BLK,
    )
    got_outputs, got_peaks, got_sums = (
        lax.all_to_all(
            output.reshape(tp_count, local_rows, H, HD),
            "tp",
            split_axis=0,
            concat_axis=0,
            tiled=True,
        ),
        lax.all_to_all(
            row_peak.reshape(tp_count, local_rows, H), "tp", split_axis=0, concat_axis=0, tiled=True
        ),
        lax.all_to_all(
            weight_sum.reshape(tp_count, local_rows, H),
            "tp",
            split_axis=0,
            concat_axis=0,
            tiled=True,
        ),
    )
    overall = jnp.max(got_peaks, axis=0)
    factor = jnp.exp(got_peaks - overall[None])
    merged_sum = jnp.sum(got_sums * factor, axis=0)
    merged = jnp.sum(got_outputs * factor[:, :, :, None], axis=0) / merged_sum[:, :, None]
    attended = merged.reshape(local_rows, feature_width).astype(jnp.bfloat16)
    projected = jnp.dot(
        lax.all_gather(attended, "tp", axis=0, tiled=True),
        out_weight,
        preferred_element_type=jnp.float32,
    )
    level_hot = (jnp.arange(gate_table.shape[0], dtype=jnp.int32) == noise_level[0]).astype(
        jnp.float32
    )[None, :]
    gate_row = jnp.dot(level_hot, gate_table, precision=lax.Precision.HIGHEST)
    return (projected * gate_row).astype(jnp.bfloat16)[None]


def solution(mesh):
    return jax.shard_map(
        on_device,
        mesh=mesh,
        in_specs=(
            P(("rep", "stretch"), "tp", None),
            P(None, ("rep", "stretch"), "tp", None),
            P(None, ("rep", "tp"), None),
            P(("rep", "stretch"), None, None),
            P(("rep", "stretch")),
            P("rep"),
            P(None, "tp"),
            P(None, "tp"),
        ),
        out_specs=P(("rep", "stretch"), None, "tp"),
        check_vma=False,
    )
```

profile of v0, /device:TPU:0, one launch (start us, length us, event | category | flops | bytes accessed | tf_op | source)
XLA Modules:
  0.0 404.0 jit_solution(16750470983532467193)
XLA Ops:
  6.5 0.0 copy-start
  6.5 0.7 all-gather.6.cloned.1.call-update
  7.3 3.4 collective-permute-start
  11.4 0.1 pad_add_fusion
  11.4 1.2 convolution_compare_fusion
  12.6 0.7 slice_reduce_fusion.1
  14.6 0.2 copy.89
  14.7 1.9 fusion.73
  16.7 0.1 copy.121
  16.7 0.1 copy.91
  16.8 0.0 collective-permute-done
  16.8 1.9 fusion.72
  18.7 0.1 copy.120
  18.8 0.8 copy.90
  19.6 52.7 %all-gather.6.cloned.1.call-done = bf16[1,512,3072]{2,1,0:T(8,128)(2,1)} async-done(((bf16[1,64,3072]{2,1,0:T(8,128)(2,1)}), bf16[1,512,3072]{2,1,0:T(8,128)(2,1)}) %all-gather.6.cloned.1.call-update) | async-done | bytes 3145744 | tf_op jit(solution)/shard_map/all_gather | solution.py:116
  72.3 4.7 %copy.92 = bf16[1,512,3072]{1,2,0:T(8,128)(2,1)} copy(bf16[1,512,3072]{2,1,0:T(8,128)(2,1)} %all-gather.6.cloned.1.call-done) | data formatting | bytes 6291456 | tf_op jit(solution)/shard_map/all_gather | solution.py:116
  77.0 3.4 fusion.37
  80.4 2.7 fusion.38
  83.1 28.6 %conditional.3 = (f32[512,24]{0,1:T(8,128)}, f32[512,24]{0,1:T(8,128)}, f32[512,24,128]{0,2,1:T(8,128)}) conditional(s32[]{:T(128)} %convert_element_type.30, () %tuple.23, (pred[128]{0:T(512)(128)(4,1)S(1)}, bf16[2,256,3072]{2,1,0:T(8,128)(2,1)}, bf16[512,24,128]{0,2,1:T(8,128)(2,1)}) %tuple.60), branch_computations={%region_7.8_spmd, %region_8.11_spmd} | conditional | flops 2837422080 | bytes 52101528 | solution.py:86
  83.1 4.7 %copy.98 = bf16[2,256,3072]{1,2,0:T(8,128)(2,1)} copy(bf16[2,256,3072]{2,1,0:T(8,128)(2,1)} %get-tuple-element.59) | data formatting | bytes 6291456 | tf_op jit(solution)/shard_map
  87.8 1.5 fusion.71
  89.3 4.2 %bitcast_reduce_fusion.1 = (f32[512,24]{0,1:T(8,128)}, f32[24,128,512]{2,1,0:T(8,128)S(1)}) fusion(pred[128]{0:T(512)(128)(4,1)S(1)} %get-tuple-element.28, bf16[128,24,128]{0,2,1:T(8,128)(2,1)S(1)} %bitcast.110, bf16[512,24,128]{0,2,1:T(8,128)(2,1)} %get-tuple-element.60), kind=kOutput, calls=%fused_computation.18 | convolution fusion | flops 407359488 | bytes 10272896 | tf_op jit(solution)/shard_map/cond/branch_1_fun/qhd,khd->qhk/dot_general | solution.py:26
  93.5 3.1 fusion.21
  96.6 8.6 %fusion.28 = f32[512,24,128]{2,0,1:T(8,128)} fusion(bf16[128,24,128]{0,2,1:T(8,128)(2,1)S(1)} %bitcast.112, f32[24,128,512]{2,1,0:T(8,128)S(1)} %get-tuple-element.80, f32[512,24]{0,1:T(8,128)} %get-tuple-element.94, pred[128]{0:T(512)(128)(4,1)S(1)} %get-tuple-element.28), kind=kOutput, calls=%fused_computation.30 | convolution fusion | flops 2422210560 | bytes 13418624 | tf_op jit(solution)/shard_map/cond/branch_1_fun/qhk,khd->qhd/dot_general | solution.py:35
  105.1 6.6 %copy.119 = f32[512,24,128]{0,2,1:T(8,128)} copy(f32[512,24,128]{2,0,1:T(8,128)} %fusion.28) | data formatting | bytes 12582912 | tf_op jit(solution)/shard_map/cond | solution.py:86
  111.7 28.7 %conditional.2 = (f32[512,24]{0,1:T(8,128)}, f32[512,24]{0,1:T(8,128)}, f32[512,24,128]{0,2,1:T(8,128)}) conditional(s32[]{:T(128)} %convert_element_type.29, () %tuple.21, (pred[128]{0:T(512)(128)(4,1)S(1)}, bf16[2,256,3072]{2,1,0:T(8,128)(2,1)}, bf16[512,24,128]{0,2,1:T(8,128)(2,1)}) %tuple.61), branch_computations={%region_2.3_spmd, %region_3.6_spmd} | conditional | flops 2837422080 | bytes 52101528 | solution.py:86
  111.7 4.8 %copy.95 = bf16[2,256,3072]{1,2,0:T(8,128)(2,1)} copy(bf16[2,256,3072]{2,1,0:T(8,128)(2,1)} %get-tuple-element.56) | data formatting | bytes 6291456 | tf_op jit(solution)/shard_map
  116.5 1.5 fusion.70
  118.0 4.2 %bitcast_reduce_fusion = (f32[512,24]{0,1:T(8,128)}, f32[24,128,512]{2,1,0:T(8,128)S(1)}) fusion(pred[128]{0:T(512)(128)(4,1)S(1)} %get-tuple-element.25, bf16[128,24,128]{0,2,1:T(8,128)(2,1)S(1)} %bitcast.111, bf16[512,24,128]{0,2,1:T(8,128)(2,1)} %get-tuple-element.57), kind=kOutput, calls=%fused_computation.1 | convolution fusion | flops 407359488 | bytes 10272896 | tf_op jit(solution)/shard_map/cond/branch_1_fun/qhd,khd->qhk/dot_general | solution.py:26
  122.1 3.1 fusion.4
  125.2 8.6 %fusion.11 = f32[512,24,128]{2,0,1:T(8,128)} fusion(bf16[128,24,128]{0,2,1:T(8,128)(2,1)S(1)} %bitcast.113, f32[24,128,512]{2,1,0:T(8,128)S(1)} %get-tuple-element.76, f32[512,24]{0,1:T(8,128)} %get-tuple-element.100, pred[128]{0:T(512)(128)(4,1)S(1)} %get-tuple-element.25), kind=kOutput, calls=%fused_computation.13 | convolution fusion | flops 2422210560 | bytes 13418624 | tf_op jit(solution)/shard_map/cond/branch_1_fun/qhk,khd->qhd/dot_general | solution.py:35
  133.8 6.6 %copy.117 = f32[512,24,128]{0,2,1:T(8,128)} copy(f32[512,24,128]{2,0,1:T(8,128)} %fusion.11) | data formatting | bytes 12582912 | tf_op jit(solution)/shard_map/cond | solution.py:86
  140.4 1.7 multiply_add_fusion
  142.0 1.5 reshape.73
  143.6 1.5 copy.128
  145.1 1.6 reshape.80
  146.7 4.0 all-to-all-start.1
  150.7 0.0 copy-done.2
  150.7 1.2 copy.88
  151.9 2.2 copy.87
  154.1 0.9 reshape.74
  155.0 0.7 reshape.82
  155.7 1.8 all-to-all-done.1
  157.5 4.1 %all-to-all-start.2 = ((f32[8,1,1536]{2,1,0:T(1,128)}), f32[8,1,1536]{2,1,0:T(1,128)S(1)}, u32[]{:S(2)}, u32[]{:S(2)}) async-start(f32[8,1,1536]{2,1,0:T(1,128)} %reshape.82), calls=%async_computation.2 | async-start | bytes 98304 | tf_op jit(solution)/shard_map/all_to_all | solution.py:141
  161.6 15.7 %fusion.36 = f32[512,24,128]{0,2,1:T(8,128)} fusion(f32[512,24,128]{0,2,1:T(8,128)} %get-tuple-element.62, f32[512,24,128]{0,2,1:T(8,128)} %get-tuple-element.61, f32[512,24]{0,1:T(8,128)} %get-tuple-element.71, f32[512,24]{0,1:T(8,128)} %get-tuple-element.70, f32[512,24]{0,1:T(8,128)} %get-tuple-element.69, f32[512,24]{0,1:T(8,128)} %get-tuple-element.68, ...), kind=kOutput, calls=%fused_computation.37 | convolution fusion | flops 2433220608 | bytes 26263552 | tf_op jit(solution)/shard_map/qhk,khd->qhd/dot_general | solution.py:35
  177.4 6.6 %copy.101 = f32[512,24,128]{2,1,0:T(8,128)} copy(f32[512,24,128]{0,2,1:T(8,128)} %fusion.36) | data formatting | bytes 12582912 | tf_op jit(solution)/shard_map/add | solution.py:45
  184.0 0.0 all-to-all-done.2
  184.0 6.0 %all-to-all-start = ((f32[8,64,24,128]{3,2,1,0:T(8,128)}), f32[8,64,24,128]{3,2,1,0:T(8,128)}, u32[]{:S(2)}, u32[]{:S(2)}) async-start(f32[8,64,24,128]{3,2,1,0:T(8,128)} %bitcast.107), calls=%async_computation | async-start | bytes 12582912 | tf_op jit(solution)/shard_map/all_to_all | solution.py:131
  190.0 0.0 all-gather.4.cloned.1.call-start
  190.0 0.5 broadcast.113
  190.5 1.6 reduce.2
  192.1 0.1 reshape.81
  192.2 0.8 reduce.3
  193.0 0.1 reshape.83
  193.1 0.1 copy.103
  193.2 0.1 copy.105
  193.3 132.3 %all-to-all-done = f32[8,64,24,128]{3,2,1,0:T(8,128)} async-done(((f32[8,64,24,128]{3,2,1,0:T(8,128)}), f32[8,64,24,128]{3,2,1,0:T(8,128)}, u32[]{:S(2)}, u32[]{:S(2)}) %all-to-all-start) | async-done | bytes 6291488 | tf_op jit(solution)/shard_map/all_to_all | solution.py:131
  325.6 4.5 %multiply_reduce_fusion = f32[64,24,128]{2,1,0:T(8,128)S(1)} fusion(f32[8,64,24,128]{3,2,1,0:T(8,128)} %all-to-all-done, f32[8,64,24]{2,1,0:T(8,128)S(1)} %copy.103), kind=kLoop, calls=%fused_computation.39 | loop fusion | flops 2949120 | bytes 7127040 | tf_op jit(solution)/shard_map/reduce_sum | solution.py:152
  330.1 0.3 divide_convert_fusion
  330.4 0.8 copy.126
  331.2 0.0 all-gather.4.cloned.1.call-update
  331.9 1.1 convolution_reduce_fusion
  333.1 57.4 %all-gather.4.cloned.1.call-done = bf16[512,3072]{1,0:T(8,128)(2,1)} async-done(((bf16[64,3072]{1,0:T(8,128)(2,1)}), bf16[512,3072]{1,0:T(8,128)(2,1)}) %all-gather.4.cloned.1.call-update) | async-done | bytes 3145744 | tf_op jit(solution)/shard_map/all_gather | solution.py:155
  390.4 6.8 %fusion.45 = bf16[1,512,768]{2,1,0:T(8,128)(2,1)} fusion(bf16[512,3072]{1,0:T(8,128)(2,1)} %all-gather.4.cloned.1.call-done, bf16[3072,768]{1,0:T(8,128)(2,1)} %param.18, f32[768]{0:T(1024)S(1)} %convolution_reduce_fusion), kind=kOutput, calls=%fused_computation.50 | convolution fusion | flops 2416705536 | bytes 8653824 | tf_op jit(solution)/shard_map/dot_general | solution.py:154
  (15 shorter events, 0.1 us)
Async XLA Ops:
  6.5 325.4 %copy-start = (f32[1000,768]{1,0:T(8,128)S(1)}, f32[1000,768]{1,0:T(8,128)}, u32[]{:S(2)}) copy-start(f32[1000,768]{1,0:T(8,128)} %param.19) | copy-start | bytes 9216004
  6.5 65.8 %all-gather.6.cloned.1.call-start = ((), (), s32[]{:S(2)}) async-start(), calls=%async_computation.4 | async-start | bytes 3538944 | tf_op jit(solution)/shard_map/all_gather | solution.py:116
  7.3 9.5 %collective-permute-start = (bf16[2,64,3072]{2,1,0:T(8,128)(2,1)}, bf16[2,64,3072]{2,1,0:T(8,128)(2,1)}, u32[]{:S(2)}, u32[]{:S(2)}) collective-permute-start(bf16[2,64,3072]{2,1,0:T(8,128)(2,1)} %bitcast.118), channel_id=1, source_target_pairs={{0,8},{1,9},{2,10},{3,11},{4,12},{5,13},{6,14},{7,15},{16,24},{17,... | collective-permute-start | bytes 2359304 | tf_op jit(solution)/shard_map/ppermute | solution.py:19
  80.4 2.7 copy-start.1
  80.4 2.7 copy-start.3
  111.7 39.0 %copy-start.2 = (bf16[1,1,64,3072]{3,2,1,0:T(8,128)(2,1)S(1)}, bf16[1,1,64,3072]{3,2,1,0:T(8,128)(2,1)}, u32[]{:S(2)}) copy-start(bf16[1,1,64,3072]{3,2,1,0:T(8,128)(2,1)} %get-tuple-element.83) | copy-start | bytes 1179652
  146.7 10.8 %all-to-all-start.1 = ((f32[8,1,1536]{2,1,0:T(1,128)}), f32[8,1,1536]{2,1,0:T(1,128)}, u32[]{:S(2)}, u32[]{:S(2)}) async-start(f32[8,1,1536]{2,1,0:T(1,128)} %reshape.80), calls=%async_computation.1 | async-start | bytes 98304 | tf_op jit(solution)/shard_map/all_to_all | solution.py:138
  157.5 26.5 %all-to-all-start.2 = ((f32[8,1,1536]{2,1,0:T(1,128)}), f32[8,1,1536]{2,1,0:T(1,128)S(1)}, u32[]{:S(2)}, u32[]{:S(2)}) async-start(f32[8,1,1536]{2,1,0:T(1,128)} %reshape.82), calls=%async_computation.2 | async-start | bytes 98304 | tf_op jit(solution)/shard_map/all_to_all | solution.py:141
  184.0 141.6 %all-to-all-start = ((f32[8,64,24,128]{3,2,1,0:T(8,128)}), f32[8,64,24,128]{3,2,1,0:T(8,128)}, u32[]{:S(2)}, u32[]{:S(2)}) async-start(f32[8,64,24,128]{3,2,1,0:T(8,128)} %bitcast.107), calls=%async_computation | async-start | bytes 12582912 | tf_op jit(solution)/shard_map/all_to_all | solution.py:131
  190.0 200.5 %all-gather.4.cloned.1.call-start = ((), (), s32[]{:S(2)}) async-start(), calls=%async_computation.3 | async-start | bytes 3538944 | tf_op jit(solution)/shard_map/all_gather | solution.py:155
Sparse Core Ops, SparseCore 0:
  9.5 62.7 all-gather.5
  331.4 59.0 all-gather.3
where the time goes:
time: 406 us; the launch traced here: 404 us
  waiting for transfers between devices  245 us (60%)
  matrix products  53.7 us (13%)
  local copies, waits for them, and re-layouts  53.3 us (13%)
  other arithmetic  18.4 us (5%)
  starting transfers between devices  17.5 us (4%)
  between operations  16.2 us (4%)
    all_to_all x1, waiting for transfers between devices, on_device(): lax.all_to_all(output.reshape(tp_count, local_rows, H, HD), 'tp', split_a...  132 us
    all_gather x1, waiting for transfers between devices, on_device(): lax.all_gather(attended, 'tp', axis=0, tiled=True)  57.4 us
    all_gather x1, waiting for transfers between devices, on_device(): piece = lax.all_gather(query[0], 'tp', axis=0, tiled=True)  52.7 us
    dot_general x3, matrix products, head_block(): jnp.einsum('qhk,khd->qhd', weights, value_heads, precision=lax.Precision....  32.9 us
    cond x2, local copies, waits for them, and re-layouts, attend_all(): lax.cond(jnp.any(live_rows), lambda: head_block(queries, key_rows, value_...  13.1 us
    dot_general x3, matrix products, head_block(): jnp.einsum('qhd,khd->qhk', queries, key_heads, preferred_element_type=jnp...  11.8 us
    another operation x2, local copies, waits for them, and re-layouts  9.51 us
    reduce_sum x3, other arithmetic, head_block(): weight_sum = jnp.sum(weights, axis=2)  8.84 us
  transfers between devices with their start and end apart: 6, of which 4 were waited for; matrix products, arithmetic and copies ran while one was open for 10% of the time, Pallas kernels for 0%

commit v1 on v0

v1 whole, which is shorter than its diff:
```python
import functools
import math

import jax
import jax.numpy as jnp
from jax import lax
from jax.experimental import pallas as pl
from jax.experimental.pallas import tpu as pltpu
from jax.sharding import PartitionSpec as P

HD = 128
BLK = 128
NEGATIVE = -1e30
LOG2_SCALE = math.log2(math.e) / math.sqrt(HD)


def head_groups(head_count, tp_count):
    both = math.gcd(head_count, tp_count)
    return both & -both


def xor_permute(value, group, step):
    count = lax.axis_size("tp")
    pairs = [(t, (t // group) * group + ((t % group) ^ step)) for t in range(count)]
    return lax.ppermute(value, "tp", pairs)


def partner_core(value):
    return lax.ppermute(value, "stretch", [(0, 1), (1, 0)])


def attention_body(place, q_ref, own_ref, other_ref, bias_ref, out_ref, *rest, rows, half, heads):
    stats = rest[:-1]
    q_scr = rest[-1]
    outer, group = q_ref.shape[0], q_ref.shape[1]
    for o in range(outer):
        for t in range(group):
            q_scr[pl.ds((o * group + t) * rows, rows), :] = q_ref[o, place[0] ^ t]
    total_rows = outer * group * rows
    block_count = bias_ref.shape[0]
    q_block = total_rows // block_count

    def flat(ref, low, count, h):
        part = ref[:, low : low + count, h * HD : (h + 1) * HD]
        return part.reshape(group * count, HD)

    for h in range(heads):
        queries = q_scr[:, h * HD : (h + 1) * HD]
        peak = total = acc = None
        column = 0
        for ref, low, count, value_low in (
            (own_ref, 2 * half, rows, 2 * half + rows),
            (other_ref, 2 * half, rows, 2 * half + rows),
            (own_ref, 0, half, half),
            (other_ref, 0, half, half),
        ):
            keys = flat(ref, low, count, h)
            values = flat(ref, value_low, count, h)
            width = keys.shape[0]
            scores = lax.dot_general(
                queries, keys, (((1,), (1,)), ((), ())), preferred_element_type=jnp.float32
            )
            scores = scores.reshape(block_count, q_block, width) * LOG2_SCALE
            scores = scores + bias_ref[:, :, column : column + width]
            scores = scores.reshape(total_rows, width)
            column += width
            top = jnp.max(scores, axis=1, keepdims=True)
            new_peak = top if peak is None else jnp.maximum(peak, top)
            weights = jnp.exp2(scores - new_peak)
            part = jnp.sum(weights, axis=1, keepdims=True)
            product = jnp.dot(
                weights.astype(jnp.bfloat16), values, preferred_element_type=jnp.float32
            )
            if peak is None:
                total, acc = part, product
            else:
                scale = jnp.exp2(peak - new_peak)
                total = total * scale + part
                acc = acc * scale + product
            peak = new_peak
        cols = slice(h * HD, (h + 1) * HD)
        if stats:
            out_ref[:, cols] = acc
            stats[0][:, h : h + 1] = peak
            stats[1][:, h : h + 1] = total
        else:
            out_ref[:, cols] = (acc / total).astype(out_ref.dtype)


def attention(place, q, own, other, bias, rows, half, partial):
    heads = q.shape[-1] // HD
    total_rows = q.shape[0] * q.shape[1] * rows
    wide = jax.ShapeDtypeStruct((total_rows, heads * HD), jnp.float32 if partial else jnp.bfloat16)
    thin = jax.ShapeDtypeStruct((total_rows, heads), jnp.float32)
    vmem = pl.BlockSpec(memory_space=pltpu.VMEM)
    return pl.pallas_call(
        functools.partial(attention_body, rows=rows, half=half, heads=heads),
        out_shape=(wide, thin, thin) if partial else wide,
        in_specs=[pl.BlockSpec(memory_space=pltpu.SMEM)] + [vmem] * 4,
        out_specs=(vmem,) * 3 if partial else vmem,
        scratch_shapes=[pltpu.VMEM((total_rows, heads * HD), jnp.bfloat16)],
        name="attend",
    )(place, q, own, other, bias)


def project_body(place, parts_ref, weight_ref, gate_ref, out_ref):
    group, _, width = parts_ref.shape
    acc = None
    for step in range(group):
        low = pl.multiple_of((place[0] ^ step) * width, width)
        product = jnp.dot(
            parts_ref[step], weight_ref[pl.ds(low, width), :], preferred_element_type=jnp.float32
        )
        acc = product if acc is None else acc + product
    out_ref[...] = (acc * gate_ref[...]).astype(out_ref.dtype)


def project(place, parts, weight, gate_row):
    vmem = pl.BlockSpec(memory_space=pltpu.VMEM)
    return pl.pallas_call(
        project_body,
        out_shape=jax.ShapeDtypeStruct((parts.shape[1], weight.shape[1]), jnp.bfloat16),
        in_specs=[pl.BlockSpec(memory_space=pltpu.SMEM)] + [vmem] * 3,
        out_specs=vmem,
        name="project",
    )(place, parts, weight, gate_row)


def key_bias(block_mask, live_limit, sources, rows, half, history_rows, core):
    block_count = block_mask.shape[0]
    fresh = (sources[:, None] * rows + jnp.arange(rows, dtype=jnp.int32)[None, :]).reshape(-1) // BLK
    hot = fresh[:, None] == jnp.arange(block_count, dtype=jnp.int32)[None, :]
    mask = block_mask > 0

    def fresh_part(columns):
        return jnp.any(hot[None, :, :] & columns[:, None, :], axis=2)

    def history_part(which):
        base = sources[:, None] * history_rows + which * half
        position = (base + jnp.arange(half, dtype=jnp.int32)[None, :]).reshape(-1)
        return jnp.broadcast_to((position < live_limit)[None, :], (block_count, position.shape[0]))

    allowed = jnp.concatenate(
        [
            fresh_part(mask[:, block_count:]),
            fresh_part(mask[:, :block_count]),
            history_part(core),
            history_part(1 - core),
        ],
        axis=1,
    )
    return jnp.where(allowed, 0.0, NEGATIVE).astype(jnp.float32)[:, None, :]


def on_device(
    query, stretch_kv, history_kv, block_mask, noise_level, history_blocks, out_weight, gate_table
):
    tp_count = lax.axis_size("tp")
    tp_index = lax.axis_index("tp")
    core = lax.axis_index("stretch")
    rows = query.shape[1]
    feature_width = query.shape[2]
    history_rows = history_kv.shape[1]
    half = history_rows // 2
    group = head_groups(feature_width // HD, tp_count)
    outer = tp_count // group
    width = feature_width // group
    member = tp_index % group
    base = tp_index - member
    place = member[None].astype(jnp.int32)

    history_half = lax.dynamic_slice_in_dim(history_kv, core * half, half, axis=1)
    stacked = jnp.concatenate(
        [history_half[0], history_half[1], stretch_kv[0, 0], stretch_kv[1, 0], query[0]], axis=0
    )
    kv_rows = 2 * half + 2 * rows

    def block_for(step):
        return lax.dynamic_slice_in_dim(stacked, (member ^ step) * width, width, axis=1)

    order = sorted(range(1, group), reverse=True)
    received = {0: block_for(0)}
    for step in order:
        received[step] = xor_permute(block_for(step), group, step)
    own = jnp.stack([received[step] for step in range(group)])
    other = partner_core(own[:, :kv_rows])
    q = own[None, :, kv_rows:]
    if outer > 1:
        same = [[o * group + m for o in range(outer)] for m in range(group)]
        q = lax.all_gather(q[0], "tp", axis=0, axis_index_groups=same)

    sources = base + (member ^ jnp.arange(group, dtype=jnp.int32))
    bias = key_bias(
        block_mask[0], history_blocks[0] * BLK, sources, rows, half, history_rows, core
    )
    if outer > 1:
        out, peak, total = attention(place, q, own, other, bias, rows, half, True)
        outs = lax.all_gather(out, "tp", axis=0, axis_index_groups=same)
        peaks = lax.all_gather(peak, "tp", axis=0, axis_index_groups=same)
        totals = lax.all_gather(total, "tp", axis=0, axis_index_groups=same)
        factor = jnp.exp2(peaks - jnp.max(peaks, axis=0, keepdims=True))
        total = jnp.sum(totals * factor, axis=0)
        heads = width // HD
        outs = outs.reshape(outer, -1, heads, HD) * factor[..., None]
        attended = (jnp.sum(outs, axis=0) / total[..., None]).astype(jnp.bfloat16)
        attended = attended.reshape(-1, width)
    else:
        attended = attention(place, q, own, other, bias, rows, half, False)

    parts = {0: attended}
    for step in range(group - 2, 0, -2):
        parts[step] = xor_permute(attended, group, step)
    for step in range(0, group, 2):
        parts[step + 1] = xor_permute(parts[step], group, 1)
    gathered = jnp.stack([parts[step] for step in range(group)])
    gate_row = lax.dynamic_slice_in_dim(gate_table, noise_level[0], 1, axis=0)
    return project(place, gathered, out_weight, gate_row)[None]


def solution(mesh):
    return jax.shard_map(
        on_device,
        mesh=mesh,
        in_specs=(
            P(("rep", "stretch"), "tp", None),
            P(None, ("rep", "stretch"), "tp", None),
            P(None, ("rep", "tp"), None),
            P(("rep", "stretch"), None, None),
            P(("rep", "stretch")),
            P("rep"),
            P(None, "tp"),
            P(None, "tp"),
        ),
        out_specs=P(("rep", "stretch"), None, "tp"),
        check_vma=False,
    )
```

time: 406 us -> 150 us (0.37)
  waiting for transfers between devices: 245 us -> 65.7 us
  matrix products: 53.7 us -> 0 us
  local copies, waits for them, and re-layouts: 53.3 us -> 28.6 us
  Pallas kernels: 0 us -> 18 us
  other arithmetic: 18.4 us -> 1.36 us
  starting transfers between devices: 17.5 us -> 33.8 us
  between operations: 16.2 us -> 1.47 us
    all_to_all x3 -> x0, waiting for transfers between devices: 134 us -> none  [the longest x1 132 us: on_device(): lax.all_to_all(output.reshape(tp_count, local_rows, H, HD), 'tp', split_a...]
    all_gather x2 -> x0, waiting for transfers between devices: 110 us -> none  [the longest x1 57.4 us: on_device(): lax.all_gather(attended, 'tp', axis=0, tiled=True)]
    ppermute x1 -> x15, waiting for transfers between devices: 0.01 us -> 65.7 us  [the longest x14 63.2 us: xor_permute(): return lax.ppermute(value, 'tp', pairs)]
    dot_general x9 -> x0, matrix products: 53.7 us -> none  [the longest x3 32.9 us: head_block(): jnp.einsum('qhk,khd->qhd', weights, value_heads, precision=lax.Precision....]
    ppermute x1 -> x15, starting transfers between devices: 3.42 us -> 33.8 us  [the longest x14 33.7 us: xor_permute(): return lax.ppermute(value, 'tp', pairs)]
    unnamed x15 -> x30, local copies, waits for them, and re-layouts: 3.44 us -> 22.1 us
    pallas_call x0 -> x2, Pallas kernels: none -> 18 us  [the longest x1 10.4 us: attention(): pl.pallas_call(functools.partial(attention_body, rows=rows, half=half, he...]
    all_to_all x3 -> x0, starting transfers between devices: 14.1 us -> none  [the longest x1 6 us: on_device(): lax.all_to_all(output.reshape(tp_count, local_rows, H, HD), 'tp', split_a...]
  transfers between devices with their start and end apart: 6 -> 15, of which waited for: 4 -> 9; matrix products, arithmetic and copies ran while one was open for 10% -> 12% of each run, Pallas kernels for 0% -> 0%
where the time goes in v1:
time: 150 us; the launch traced here: 149 us
  waiting for transfers between devices  65.7 us (44%)
  starting transfers between devices  33.8 us (23%)
  local copies, waits for them, and re-layouts  28.6 us (19%)
  Pallas kernels  18 us (12%)
    ppermute x14, waiting for transfers between devices, xor_permute(): return lax.ppermute(value, 'tp', pairs)  63.2 us
    ppermute x14, starting transfers between devices, xor_permute(): return lax.ppermute(value, 'tp', pairs)  33.7 us
    unnamed x30, local copies, waits for them, and re-layouts  22.1 us
    pallas_call x1, Pallas kernels, attention(): pl.pallas_call(functools.partial(attention_body, rows=rows, half=half, he...  10.4 us
    pallas_call x1, Pallas kernels, project(): pl.pallas_call(project_body, out_shape=jax.ShapeDtypeStruct((parts.shape[...  7.63 us
    dynamic_slice x1, local copies, waits for them, and re-layouts, block_for(): lax.dynamic_slice_in_dim(stacked, (member ^ step) * width, width, axis=1)  3.08 us
  transfers between devices with their start and end apart: 15, of which 9 were waited for; matrix products, arithmetic and copies ran while one was open for 12% of the time, Pallas kernels for 0%

profile of v1, /device:TPU:0, one launch (start us, length us, event | category | flops | bytes accessed | tf_op | source)
XLA Modules:
  0.0 149.0 jit_solution(9093016574320657649)
XLA Ops:
  0.0 2.2 %fusion.1 = bf16[448,3072]{1,0:T(8,128)(2,1)} fusion(bf16[2,256,3072]{2,1,0:T(8,128)(2,1)} %param.10, s32[]{:T(128)S(6)} %select_n.58), kind=kLoop, calls=%fused_computation.3 | loop fusion | bytes 1572868
  2.2 2.1 %fusion = bf16[448,3072]{1,0:T(8,128)(2,1)} fusion(bf16[448,3072]{1,0:T(8,128)(2,1)} %fusion.1, bf16[2,256,3072]{2,1,0:T(8,128)(2,1)} %param.10, s32[]{:T(128)S(6)} %add.166, s32[]{:T(128)S(6)} %select_n.58), kind=kLoop, calls=%fused_computation.1 | loop fusion | bytes 1572872
  4.3 0.8 bitcast_dynamic-update-slice_fusion.10
  5.1 0.8 bitcast_dynamic-update-slice_fusion.9
  5.9 0.8 bitcast_dynamic-update-slice_fusion.8
  6.7 3.1 %constant_dynamic-slice_fusion.1 = (bf16[448,384]{1,0:T(8,128)(2,1)}, bf16[448,384]{1,0:T(8,128)(2,1)}, bf16[448,384]{1,0:T(8,128)(2,1)}, bf16[448,384]{1,0:T(8,...) fusion(bf16[448,3072]{1,0:T(8,128)(2,1)} %bitcast_dynamic-update-slice_fusion.8, ...), kind=kLoop, calls=%fused_computation.39 | loop fusion | bytes 4816924 | tf_op jit(solution)/shard_map/dynamic_slice | solution.py:179
  9.8 3.0 %collective-permute-start = (bf16[448,384]{1,0:T(8,128)(2,1)}, bf16[448,384]{1,0:T(8,128)(2,1)}, u32[]{:S(2)}, u32[]{:S(2)}) collective-permute-start(bf16[448,384]{1,0:T(8,128)(2,1)} %get-tuple-element.13), channel_id=1, source_target_pairs={{0,1},{1,0},{2,3},{3,2},{4,5},{5,4},{6,7},{7,6},{8,9},{9,8},{10,11... | collective-permute-start | bytes 1032200 | tf_op jit(solution)/shard_map/ppermute | solution.py:25
  12.8 1.6 %collective-permute-start.1 = (bf16[448,384]{1,0:T(8,128)(2,1)}, bf16[448,384]{1,0:T(8,128)(2,1)}, u32[]{:S(2)}, u32[]{:S(2)}) collective-permute-start(bf16[448,384]{1,0:T(8,128)(2,1)} %get-tuple-element.12), channel_id=1, source_target_pairs={{0,2},{1,3},{2,0},{3,1},{4,6},{5,7},{6,4},{7,5},{8,10},{9,11},{10,... | collective-permute-start | bytes 1032200 | tf_op jit(solution)/shard_map/ppermute | solution.py:25
  14.3 0.0 collective-permute-start.2
  14.3 3.0 %collective-permute-start.3 = (bf16[448,384]{1,0:T(8,128)(2,1)}, bf16[448,384]{1,0:T(8,128)(2,1)}, u32[]{:S(2)}, u32[]{:S(2)}) collective-permute-start(bf16[448,384]{1,0:T(8,128)(2,1)} %get-tuple-element.10), channel_id=1, source_target_pairs={{0,4},{1,5},{2,6},{3,7},{4,0},{5,1},{6,2},{7,3},{8,12},{9,13},{10,... | collective-permute-start | bytes 1032200 | tf_op jit(solution)/shard_map/ppermute | solution.py:25
  17.3 1.3 collective-permute-start.4
  18.6 0.1 iota_add_fusion
  18.7 0.1 add.151
  19.4 0.1 fusion.3
  19.5 0.1 fusion.2
  19.6 1.0 bitcast_dynamic-update-slice_fusion.18
  20.6 0.5 collective-permute-done
  21.1 3.8 %collective-permute-start.5 = (bf16[448,384]{1,0:T(8,128)(2,1)}, bf16[448,384]{1,0:T(8,128)(2,1)S(1)}, u32[]{:S(2)}, u32[]{:S(2)}) collective-permute-start(bf16[448,384]{1,0:T(8,128)(2,1)} %get-tuple-element.8), channel_id=1, source_target_pairs={{0,6},{1,7},{2,4},{3,5},{4,2},{5,3},{6,0},{7,1},{8,14},{9,15},{10,... | collective-permute-start | bytes 1032200 | tf_op jit(solution)/shard_map/ppermute | solution.py:25
  25.0 1.0 bitcast_dynamic-update-slice_fusion.17
  26.0 11.8 %collective-permute-done.1 = bf16[448,384]{1,0:T(8,128)(2,1)} collective-permute-done((bf16[448,384]{1,0:T(8,128)(2,1)}, bf16[448,384]{1,0:T(8,128)(2,1)}, u32[]{:S(2)}, u32[]{:S(2)}) %collective-permute-start.1) | collective-permute-done | bytes 344096 | tf_op jit(solution)/shard_map/ppermute | solution.py:25
  37.9 1.0 collective-permute-start.6
  38.8 1.0 bitcast_dynamic-update-slice_fusion.16
  39.8 3.1 %collective-permute-done.2 = bf16[448,384]{1,0:T(8,128)(2,1)} collective-permute-done((bf16[448,384]{1,0:T(8,128)(2,1)}, bf16[448,384]{1,0:T(8,128)(2,1)}, u32[]{:S(2)}, u32[]{:S(2)}) %collective-permute-start.2) | collective-permute-done | bytes 344096 | tf_op jit(solution)/shard_map/ppermute | solution.py:25
  42.9 1.0 bitcast_dynamic-update-slice_fusion.15
  44.0 0.0 collective-permute-done.3
  44.0 1.0 bitcast_dynamic-update-slice_fusion.14
  45.0 19.6 %collective-permute-done.4 = bf16[448,384]{1,0:T(8,128)(2,1)S(1)} collective-permute-done((bf16[448,384]{1,0:T(8,128)(2,1)}, bf16[448,384]{1,0:T(8,128)(2,1)S(1)}, u32[]{:S(2)}, u32[]{:S(2)}) %collective-permute-start.4) | collective-permute-done | bytes 344096 | tf_op jit(solution)/shard_map/ppermute | solution.py:25
  64.6 0.1 bitcast_dynamic-update-slice_fusion.13
  64.7 0.1 bitcast_dynamic-update-slice_fusion.12
  64.7 0.0 collective-permute-done.6
  64.7 0.1 bitcast_dynamic-update-slice_fusion.11.own_ref
  64.8 0.2 slice.33
  65.1 0.1 collective-permute-start.7
  65.2 0.1 fusion.8
  65.3 0.1 and_reduce_fusion.1
  65.4 1.0 copy_select_fusion.bias_ref
  66.4 0.8 slice_bitcast_fusion.q_ref
  67.2 2.5 %collective-permute-done.7.other_ref = bf16[8,384,384]{2,1,0:T(8,128)(2,1)S(1)} collective-permute-done((bf16[8,384,384]{2,1,0:T(8,128)(2,1)S(1)}, bf16[8,384,384]{2,1,0:T(8,128)(2,1)S(1)}, u32[]{:S(2)}, u32[]{:S(2)}) %collective-permute-start.7) | collective-permute-done | bytes 2359328 | tf_op jit(solution)/shard_map/ppermute | solution.py:29
  69.7 1.4 copy-done.2
  71.1 10.4 %attend.1 = bf16[512,384]{1,0:T(8,128)(2,1)} custom-call(s32[1]{0:T(128)} %bitcast.place, bf16[1,8,64,384]{3,2,1,0:T(8,128)(2,1)} %slice_bitcast_fusion.q_ref, bf16[8,448,384]{2,1,0:T(8,128)(2,1)} %copy-done.1, bf16[8,384,384]{2,1,0:T(8,128)(2,1)} %copy-done.2, f32[4,1,3072]{2,1,0:T(1,128)} %copy_select_fusion.bias_ref), custom_call_target="tpu_custom_call" | custom-call | tf_op jit(solution)/shard_map/attend/pallas_call | solution.py:96
  81.5 13.2 %collective-permute-start.9 = (bf16[512,384]{1,0:T(8,128)(2,1)}, bf16[512,384]{1,0:T(8,128)(2,1)}, u32[]{:S(2)}, u32[]{:S(2)}) collective-permute-start(bf16[512,384]{1,0:T(8,128)(2,1)} %attend.1), channel_id=1, source_target_pairs={{0,2},{1,3},{2,0},{3,1},{4,6},{5,7},{6,4},{7,5},{8,10},{9,11},{10,... | collective-permute-start | bytes 1179656 | tf_op jit(solution)/shard_map/ppermute | solution.py:25
  94.8 2.1 %collective-permute-start.11 = (bf16[512,384]{1,0:T(8,128)(2,1)}, bf16[512,384]{1,0:T(8,128)(2,1)}, u32[]{:S(2)}, u32[]{:S(2)}) collective-permute-start(bf16[512,384]{1,0:T(8,128)(2,1)} %attend.1), channel_id=1, source_target_pairs={{0,4},{1,5},{2,6},{3,7},{4,0},{5,1},{6,2},{7,3},{8,12},{9,13},{10,... | collective-permute-start | bytes 1179656 | tf_op jit(solution)/shard_map/ppermute | solution.py:25
  96.9 1.5 collective-permute-start.13
  98.4 0.5 collective-permute-start.8
  99.5 0.6 constant_dynamic-slice_fusion.gate_ref
  100.1 1.8 %bitcast_dynamic-update-slice_fusion.7 = bf16[8,512,384]{2,1,0:T(8,128)(2,1)} fusion(bf16[512,384]{1,0:T(8,128)(2,1)} %attend.1), kind=kLoop, calls=%fused_computation.12 | loop fusion | bytes 786432
  101.9 11.0 %collective-permute-done.9 = bf16[512,384]{1,0:T(8,128)(2,1)} collective-permute-done((bf16[512,384]{1,0:T(8,128)(2,1)}, bf16[512,384]{1,0:T(8,128)(2,1)}, u32[]{:S(2)}, u32[]{:S(2)}) %collective-permute-start.9) | collective-permute-done | bytes 393248 | tf_op jit(solution)/shard_map/ppermute | solution.py:25
  112.9 0.7 collective-permute-start.10
  113.6 11.2 %collective-permute-done.11 = bf16[512,384]{1,0:T(8,128)(2,1)} collective-permute-done((bf16[512,384]{1,0:T(8,128)(2,1)}, bf16[512,384]{1,0:T(8,128)(2,1)}, u32[]{:S(2)}, u32[]{:S(2)}) %collective-permute-start.11) | collective-permute-done | bytes 393248 | tf_op jit(solution)/shard_map/ppermute | solution.py:25
  124.8 0.9 collective-permute-start.12
  125.7 0.0 collective-permute-done.13
  125.7 1.1 collective-permute-start.14
  126.8 0.0 collective-permute-done.8
  126.9 1.8 %bitcast_dynamic-update-slice_fusion.6 = bf16[8,512,384]{2,1,0:T(8,128)(2,1)} fusion(bf16[8,512,384]{2,1,0:T(8,128)(2,1)} %bitcast_dynamic-update-slice_fusion.7, bf16[512,384]{1,0:T(8,128)(2,1)} %collective-permute-done.8), kind=kLoop, calls=%fused_computation.11 | loop fusion | bytes 786432
  128.6 1.8 %bitcast_dynamic-update-slice_fusion.5 = bf16[8,512,384]{2,1,0:T(8,128)(2,1)} fusion(bf16[8,512,384]{2,1,0:T(8,128)(2,1)} %bitcast_dynamic-update-slice_fusion.6, bf16[512,384]{1,0:T(8,128)(2,1)} %collective-permute-done.9), kind=kLoop, calls=%fused_computation.10 | loop fusion | bytes 786432
  130.4 0.0 collective-permute-done.10
  130.4 0.8 bitcast_dynamic-update-slice_fusion.4
  131.2 1.8 %bitcast_dynamic-update-slice_fusion.3 = bf16[8,512,384]{2,1,0:T(8,128)(2,1)} fusion(bf16[8,512,384]{2,1,0:T(8,128)(2,1)} %bitcast_dynamic-update-slice_fusion.4, bf16[512,384]{1,0:T(8,128)(2,1)} %collective-permute-done.11), kind=kLoop, calls=%fused_computation.8 | loop fusion | bytes 786432
  133.0 3.3 %collective-permute-done.12 = bf16[512,384]{1,0:T(8,128)(2,1)S(1)} collective-permute-done((bf16[512,384]{1,0:T(8,128)(2,1)}, bf16[512,384]{1,0:T(8,128)(2,1)S(1)}, u32[]{:S(2)}, u32[]{:S(2)}) %collective-permute-start.12) | collective-permute-done | bytes 393248 | tf_op jit(solution)/shard_map/ppermute | solution.py:25
  136.3 0.8 bitcast_dynamic-update-slice_fusion.2
  137.1 0.8 bitcast_dynamic-update-slice_fusion.1
  137.9 2.6 %collective-permute-done.14 = bf16[512,384]{1,0:T(8,128)(2,1)S(1)} collective-permute-done((bf16[512,384]{1,0:T(8,128)(2,1)S(1)}, bf16[512,384]{1,0:T(8,128)(2,1)S(1)}, u32[]{:S(2)}, u32[]{:S(2)}) %collective-permute-start.14) | collective-permute-done | bytes 393248 | tf_op jit(solution)/shard_map/ppermute | solution.py:25
  140.5 0.8 bitcast_dynamic-update-slice_fusion.parts_ref
  141.3 7.6 %project.1 = bf16[512,768]{1,0:T(8,128)(2,1)} custom-call(s32[1]{0:T(128)} %bitcast.place, bf16[8,512,384]{2,1,0:T(8,128)(2,1)} %bitcast_dynamic-update-slice_fusion.parts_ref, bf16[3072,768]{1,0:T(8,128)(2,1)} %weight_ref.1, f32[1,768]{1,0:T(1,128)} %constant_dynamic-slice_fusion.gate_ref), custom_call_target="tpu_custom_call" | custom-call | tf_op jit(solution)/shard_map/project/pallas_call | solution.py:120
  (20 shorter events, 0.1 us)
Async XLA Ops:
  0.0 99.5 %copy-start = (f32[1000,768]{1,0:T(8,128)S(1)}, f32[1000,768]{1,0:T(8,128)}, u32[]{:S(2)}) copy-start(f32[1000,768]{1,0:T(8,128)} %param.15) | copy-start | bytes 9216004
  0.0 5.9 %copy-start.4 = (bf16[1,64,3072]{2,1,0:T(8,128)(2,1)S(1)}, bf16[1,64,3072]{2,1,0:T(8,128)(2,1)}, u32[]{:S(2)}) copy-start(bf16[1,64,3072]{2,1,0:T(8,128)(2,1)} %param.8) | copy-start | bytes 1179652
  0.0 4.3 %copy-start.3 = (bf16[2,1,64,3072]{3,2,1,0:T(8,128)(2,1)S(1)}, bf16[2,1,64,3072]{3,2,1,0:T(8,128)(2,1)}, u32[]{:S(2)}) copy-start(bf16[2,1,64,3072]{3,2,1,0:T(8,128)(2,1)} %param.9) | copy-start | bytes 2359300
  5.9 13.7 %copy-start.5 = (s32[1,4,8]{2,1,0:T(4,128)S(1)}, s32[1,4,8]{2,1,0:T(4,128)}, u32[]{:S(2)}) copy-start(s32[1,4,8]{2,1,0:T(4,128)} %param.11) | copy-start | bytes 388
  9.8 11.4 %collective-permute-start = (bf16[448,384]{1,0:T(8,128)(2,1)}, bf16[448,384]{1,0:T(8,128)(2,1)}, u32[]{:S(2)}, u32[]{:S(2)}) collective-permute-start(bf16[448,384]{1,0:T(8,128)(2,1)} %get-tuple-element.13), channel_id=1, source_target_pairs={{0,1},{1,0},{2,3},{3,2},{4,5},{5,4},{6,7},{7,6},{8,9},{9,8},{10,11... | collective-permute-start | bytes 1032200 | tf_op jit(solution)/shard_map/ppermute | solution.py:25
  12.8 25.1 %collective-permute-start.1 = (bf16[448,384]{1,0:T(8,128)(2,1)}, bf16[448,384]{1,0:T(8,128)(2,1)}, u32[]{:S(2)}, u32[]{:S(2)}) collective-permute-start(bf16[448,384]{1,0:T(8,128)(2,1)} %get-tuple-element.12), channel_id=1, source_target_pairs={{0,2},{1,3},{2,0},{3,1},{4,6},{5,7},{6,4},{7,5},{8,10},{9,11},{10,... | collective-permute-start | bytes 1032200 | tf_op jit(solution)/shard_map/ppermute | solution.py:25
  14.3 28.6 %collective-permute-start.2 = (bf16[448,384]{1,0:T(8,128)(2,1)}, bf16[448,384]{1,0:T(8,128)(2,1)}, u32[]{:S(2)}, u32[]{:S(2)}) collective-permute-start(bf16[448,384]{1,0:T(8,128)(2,1)} %get-tuple-element.11), channel_id=1, source_target_pairs={{0,3},{1,2},{2,1},{3,0},{4,7},{5,6},{6,5},{7,4},{8,11},{9,10},{10,... | collective-permute-start | bytes 1032200 | tf_op jit(solution)/shard_map/ppermute | solution.py:25
  14.3 29.6 %collective-permute-start.3 = (bf16[448,384]{1,0:T(8,128)(2,1)}, bf16[448,384]{1,0:T(8,128)(2,1)}, u32[]{:S(2)}, u32[]{:S(2)}) collective-permute-start(bf16[448,384]{1,0:T(8,128)(2,1)} %get-tuple-element.10), channel_id=1, source_target_pairs={{0,4},{1,5},{2,6},{3,7},{4,0},{5,1},{6,2},{7,3},{8,12},{9,13},{10,... | collective-permute-start | bytes 1032200 | tf_op jit(solution)/shard_map/ppermute | solution.py:25
  17.3 47.3 %collective-permute-start.4 = (bf16[448,384]{1,0:T(8,128)(2,1)}, bf16[448,384]{1,0:T(8,128)(2,1)S(1)}, u32[]{:S(2)}, u32[]{:S(2)}) collective-permute-start(bf16[448,384]{1,0:T(8,128)(2,1)} %get-tuple-element.9), channel_id=1, source_target_pairs={{0,5},{1,4},{2,7},{3,6},{4,1},{5,0},{6,3},{7,2},{8,13},{9,12},{10,... | collective-permute-start | bytes 1032200 | tf_op jit(solution)/shard_map/ppermute | solution.py:25
  21.1 43.5 %collective-permute-start.5 = (bf16[448,384]{1,0:T(8,128)(2,1)}, bf16[448,384]{1,0:T(8,128)(2,1)S(1)}, u32[]{:S(2)}, u32[]{:S(2)}) collective-permute-start(bf16[448,384]{1,0:T(8,128)(2,1)} %get-tuple-element.8), channel_id=1, source_target_pairs={{0,6},{1,7},{2,4},{3,5},{4,2},{5,3},{6,0},{7,1},{8,14},{9,15},{10,... | collective-permute-start | bytes 1032200 | tf_op jit(solution)/shard_map/ppermute | solution.py:25
  37.9 26.9 %collective-permute-start.6 = (bf16[448,384]{1,0:T(8,128)(2,1)}, bf16[448,384]{1,0:T(8,128)(2,1)S(1)}, u32[]{:S(2)}, u32[]{:S(2)}) collective-permute-start(bf16[448,384]{1,0:T(8,128)(2,1)} %get-tuple-element.7), channel_id=1, source_target_pairs={{0,7},{1,6},{2,5},{3,4},{4,3},{5,2},{6,1},{7,0},{8,15},{9,14},{10,... | collective-permute-start | bytes 1032200 | tf_op jit(solution)/shard_map/ppermute | solution.py:25
  64.8 2.4 %copy-start.1 = (bf16[8,448,384]{2,1,0:T(8,128)(2,1)}, bf16[8,448,384]{2,1,0:T(8,128)(2,1)S(1)}, u32[]{:S(2)}) copy-start(bf16[8,448,384]{2,1,0:T(8,128)(2,1)S(1)} %bitcast_dynamic-update-slice_fusion.11.own_ref) | copy-start | bytes 8257540
  65.1 4.6 %collective-permute-start.7 = (bf16[8,384,384]{2,1,0:T(8,128)(2,1)S(1)}, bf16[8,384,384]{2,1,0:T(8,128)(2,1)S(1)}, u32[]{:S(2)}, u32[]{:S(2)}) collective-permute-start(bf16[8,384,384]{2,1,0:T(8,128)(2,1)S(1)} %slice.33), channel_id=1, source_target_pairs={{0,8},{8,0},{1,9},{9,1},{2,10},{10,2},{3,11},{11,3},{4,12},{12,4},... | collective-permute-start | bytes 7077896 | tf_op jit(solution)/shard_map/ppermute | solution.py:29
  69.7 1.4 copy-start.2
  81.5 31.4 %collective-permute-start.9 = (bf16[512,384]{1,0:T(8,128)(2,1)}, bf16[512,384]{1,0:T(8,128)(2,1)}, u32[]{:S(2)}, u32[]{:S(2)}) collective-permute-start(bf16[512,384]{1,0:T(8,128)(2,1)} %attend.1), channel_id=1, source_target_pairs={{0,2},{1,3},{2,0},{3,1},{4,6},{5,7},{6,4},{7,5},{8,10},{9,11},{10,... | collective-permute-start | bytes 1179656 | tf_op jit(solution)/shard_map/ppermute | solution.py:25
  94.8 30.1 %collective-permute-start.11 = (bf16[512,384]{1,0:T(8,128)(2,1)}, bf16[512,384]{1,0:T(8,128)(2,1)}, u32[]{:S(2)}, u32[]{:S(2)}) collective-permute-start(bf16[512,384]{1,0:T(8,128)(2,1)} %attend.1), channel_id=1, source_target_pairs={{0,4},{1,5},{2,6},{3,7},{4,0},{5,1},{6,2},{7,3},{8,12},{9,13},{10,... | collective-permute-start | bytes 1179656 | tf_op jit(solution)/shard_map/ppermute | solution.py:25
  96.9 28.8 %collective-permute-start.13 = (bf16[512,384]{1,0:T(8,128)(2,1)}, bf16[512,384]{1,0:T(8,128)(2,1)S(1)}, u32[]{:S(2)}, u32[]{:S(2)}) collective-permute-start(bf16[512,384]{1,0:T(8,128)(2,1)} %attend.1), channel_id=1, source_target_pairs={{0,6},{1,7},{2,4},{3,5},{4,2},{5,3},{6,0},{7,1},{8,14},{9,15},{10,... | collective-permute-start | bytes 1179656 | tf_op jit(solution)/shard_map/ppermute | solution.py:25
  98.4 28.5 %collective-permute-start.8 = (bf16[512,384]{1,0:T(8,128)(2,1)}, bf16[512,384]{1,0:T(8,128)(2,1)}, u32[]{:S(2)}, u32[]{:S(2)}) collective-permute-start(bf16[512,384]{1,0:T(8,128)(2,1)} %attend.1), channel_id=1, source_target_pairs={{0,1},{1,0},{2,3},{3,2},{4,5},{5,4},{6,7},{7,6},{8,9},{9,8},{10,11... | collective-permute-start | bytes 1179656 | tf_op jit(solution)/shard_map/ppermute | solution.py:25
  112.9 17.5 %collective-permute-start.10 = (bf16[512,384]{1,0:T(8,128)(2,1)}, bf16[512,384]{1,0:T(8,128)(2,1)S(1)}, u32[]{:S(2)}, u32[]{:S(2)}) collective-permute-start(bf16[512,384]{1,0:T(8,128)(2,1)} %collective-permute-done.9), channel_id=1, source_target_pairs={{0,1},{1,0},{2,3},{3,2},{4,5},{5,4},{6,7},{7,6},{8,9},{9,8},{10,11... | collective-permute-start | bytes 1179656 | tf_op jit(solution)/shard_map/ppermute | solution.py:25
  124.8 11.5 %collective-permute-start.12 = (bf16[512,384]{1,0:T(8,128)(2,1)}, bf16[512,384]{1,0:T(8,128)(2,1)S(1)}, u32[]{:S(2)}, u32[]{:S(2)}) collective-permute-start(bf16[512,384]{1,0:T(8,128)(2,1)} %collective-permute-done.11), channel_id=1, source_target_pairs={{0,1},{1,0},{2,3},{3,2},{4,5},{5,4},{6,7},{7,6},{8,9},{9,8},{10,11... | collective-permute-start | bytes 1179656 | tf_op jit(solution)/shard_map/ppermute | solution.py:25
  125.7 14.8 %collective-permute-start.14 = (bf16[512,384]{1,0:T(8,128)(2,1)S(1)}, bf16[512,384]{1,0:T(8,128)(2,1)S(1)}, u32[]{:S(2)}, u32[]{:S(2)}) collective-permute-start(bf16[512,384]{1,0:T(8,128)(2,1)S(1)} %collective-permute-done.13), channel_id=1, source_target_pairs={{0,1},{1,0},{2,3},{3,2},{4,5},{5,4},{6,7},{7,6},{8,9},{9,8},{10,11... | collective-permute-start | bytes 1179656 | tf_op jit(solution)/shard_map/ppermute | solution.py:25

commit v2 on v1

v2 whole, which is shorter than its diff:
```python
import functools
import math

import jax
import jax.numpy as jnp
from jax import lax
from jax.experimental import pallas as pl
from jax.experimental.pallas import tpu as pltpu
from jax.sharding import PartitionSpec as P


HD = 128
BLK = 128
NEGATIVE = -1e30
LOG2_SCALE = math.log2(math.e) / math.sqrt(HD)
CHUNKS = 2

VMEM = pl.BlockSpec(memory_space=pltpu.VMEM)
SMEM = pl.BlockSpec(memory_space=pltpu.SMEM)
HBM = pl.BlockSpec(memory_space=pltpu.HBM)


def head_groups(head_count, tp_count):
    both = math.gcd(head_count, tp_count)
    return both & -both


def head_chunks(heads, count):
    count = min(count, heads)
    sizes = [heads // count + (1 if i < heads % count else 0) for i in range(count)]
    return [(sum(sizes[:i]), sizes[i]) for i in range(count)]


def xor_permute(value, group, step, senders=None):
    count = lax.axis_size("tp")
    pairs = [
        (t, (t // group) * group + ((t % group) ^ step))
        for t in range(count)
        if senders is None or t % group in senders
    ]
    return lax.ppermute(value, "tp", pairs)


def spread(value, member, group):
    def send(block, step, senders=None):
        return xor_permute(block, group, step, senders)

    if group == 1:
        return [value], [member]
    line = [(value, member)]
    if group == 8:
        over = send(value, 4)
        line += [(send(value, 2), member ^ 2), (over, member ^ 4)]
        line += [(send(over, 2), member ^ 6)]
    else:
        line += [(send(value, step), member ^ step) for step in range(2, group, 2)]
    across = [(send(block, 1), source ^ 1) for block, source in line]
    blocks, members = zip(*(line + across))
    return list(blocks), list(members)


def partner_core(value):
    return lax.ppermute(value, "stretch", [(0, 1), (1, 0)])


def pack_body(place, query, stretch, history, *rest, half, rows, width, plan):
    count = len(plan)
    blocks, stages = rest[:count], rest[count : 2 * count]
    in_sems, out_sems = rest[2 * count :]
    row = pl.multiple_of(place[1] * half, 8)
    incoming = []
    for index, (step, low, cols) in enumerate(plan):
        column = pl.ds(pl.multiple_of((place[0] ^ step) * width + low, HD), cols)
        parts = (
            (history.at[0, pl.ds(row, half), column], 0, half),
            (history.at[1, pl.ds(row, half), column], half, half),
            (stretch.at[0, :, column], 2 * half, rows),
            (stretch.at[1, :, column], 2 * half + rows, rows),
            (query.at[:, column], 2 * half + 2 * rows, rows),
        )
        copies = [
            pltpu.make_async_copy(
                source, stages[index].at[pl.ds(at, size), :], in_sems.at[index, part]
            )
            for part, (source, at, size) in enumerate(parts)
        ]
        for copy in copies:
            copy.start()
        incoming.append(copies)
    outgoing = []
    for index, copies in enumerate(incoming):
        for copy in copies:
            copy.wait()
        copy = pltpu.make_async_copy(stages[index], blocks[index], out_sems.at[index])
        copy.start()
        outgoing.append(copy)
    for copy in outgoing:
        copy.wait()


def pack(place, query, stretch, history, width, plan):
    rows, half = query.shape[0], history.shape[1] // 2
    shapes = [(2 * half + 3 * rows, cols) for _, _, cols in plan]
    return pl.pallas_call(
        functools.partial(pack_body, half=half, rows=rows, width=width, plan=plan),
        out_shape=tuple(jax.ShapeDtypeStruct(shape, query.dtype) for shape in shapes),
        in_specs=[SMEM, HBM, HBM, HBM],
        out_specs=(HBM,) * len(plan),
        scratch_shapes=[pltpu.VMEM(shape, query.dtype) for shape in shapes]
        + [
            pltpu.SemaphoreType.DMA((len(plan), 5)),
            pltpu.SemaphoreType.DMA((len(plan),)),
        ],
        name="pack",
    )(place, query, stretch, history)


def attention_body(place, bias_ref, *rest, rows, half, heads, low, inner, outer, group, partial):
    kv_rows = 2 * half + 2 * rows
    refs, rest = rest[:group], rest[group:]
    own = [(ref, 0, low if step < inner else 0) for step, ref in enumerate(refs)]
    other = [(rest[0], step * kv_rows, low) for step in range(inner)]
    rest = rest[1:]
    if inner < group:
        other += [(rest[0], step * kv_rows, 0) for step in range(group - inner)]
        rest = rest[1:]
    q_all = None
    if partial:
        q_all, rest = rest[0], rest[1:]
    out_ref, stats, q_scr = rest[0], rest[1:-1], rest[-1]
    for step, (ref, _, base) in enumerate(own):
        member = place[0] ^ step
        for o in range(outer):
            at = pl.multiple_of((o * group + member) * rows, 8)
            if partial:
                q_scr[pl.ds(at, rows), :] = q_all[o, step]
            else:
                q_scr[pl.ds(at, rows), :] = ref[kv_rows:, base : base + heads * HD]
    total_rows = outer * group * rows
    block_count = bias_ref.shape[0]
    q_block = total_rows // block_count

    for h in range(heads):
        cols = slice(h * HD, (h + 1) * HD)
        queries = q_scr[:, cols]

        def flat(sources, first, count):
            pieces = []
            for ref, row, base in sources:
                columns = slice(base + h * HD, base + (h + 1) * HD)
                pieces.append(ref[row + first : row + first + count, columns])
            return jnp.concatenate(pieces, axis=0)

        peak = total = acc = None
        column = 0
        for sources, first, count, value_first in (
            (own, 2 * half, rows, 2 * half + rows),
            (other, 2 * half, rows, 2 * half + rows),
            (own, 0, half, half),
            (other, 0, half, half),
        ):
            keys = flat(sources, first, count)
            values = flat(sources, value_first, count)
            width = keys.shape[0]
            scores = lax.dot_general(
                queries, keys, (((1,), (1,)), ((), ())), preferred_element_type=jnp.float32
            )
            scores = scores.reshape(block_count, q_block, width) * LOG2_SCALE
            scores = scores + bias_ref[:, :, column : column + width]
            scores = scores.reshape(total_rows, width)
            column += width
            top = jnp.max(scores, axis=1, keepdims=True)
            new_peak = top if peak is None else jnp.maximum(peak, top)
            weights = jnp.exp2(scores - new_peak)
            part = jnp.sum(weights, axis=1, keepdims=True)
            product = jnp.dot(
                weights.astype(jnp.bfloat16), values, preferred_element_type=jnp.float32
            )
            if peak is None:
                total, acc = part, product
            else:
                scale = jnp.exp2(peak - new_peak)
                total = total * scale + part
                acc = acc * scale + product
            peak = new_peak
        if partial:
            out_ref[:, cols] = acc
            stats[0][:, h : h + 1] = peak
            stats[1][:, h : h + 1] = total
        else:
            out_ref[:, cols] = (acc / total).astype(out_ref.dtype)


def attention(place, bias, own, others, q_all, rows, half, total_rows, low, cols):
    group = len(own)
    partial = q_all is not None
    wide = jax.ShapeDtypeStruct((total_rows, cols), jnp.float32 if partial else jnp.bfloat16)
    thin = jax.ShapeDtypeStruct((total_rows, cols // HD), jnp.float32)
    body = functools.partial(
        attention_body,
        rows=rows,
        half=half,
        heads=cols // HD,
        low=low,
        inner=max(group // 2, 1),
        outer=total_rows // (group * rows),
        group=group,
        partial=partial,
    )
    operands = (*own, *others) + ((q_all,) if partial else ())
    return pl.pallas_call(
        body,
        out_shape=(wide, thin, thin) if partial else wide,
        in_specs=[SMEM] + [VMEM] * (1 + len(operands)),
        out_specs=(VMEM,) * 3 if partial else VMEM,
        scratch_shapes=[pltpu.VMEM((total_rows, cols), jnp.bfloat16)],
        compiler_params=pltpu.CompilerParams(vmem_limit_bytes=24 << 20),
        name="attend",
    )(place, bias, *operands)


def project_body(starts, place, weight, *rest, group, low, last, first):
    parts, rest = rest[:group], rest[group:]
    cols = parts[0].shape[1]
    left = jnp.concatenate([part[...] for part in parts], axis=1)
    right = jnp.concatenate(
        [
            weight[pl.ds(pl.multiple_of(starts[step] + low, HD), cols), :]
            for step in range(group)
        ],
        axis=0,
    )
    acc = jnp.dot(left, right, preferred_element_type=jnp.float32)
    if not first:
        acc = acc + rest[0][...]
        rest = rest[1:]
    if last:
        gate, out = rest
        acc = acc * gate[pl.ds(place[2] % 8, 1), :]
    else:
        (out,) = rest
    out[...] = acc.astype(out.dtype)


def project(starts, place, parts, weight, before, gate, low):
    group = len(parts)
    first, last = before is None, gate is not None
    operands = [weight, *parts]
    operands += [] if first else [before]
    operands += [gate] if last else []
    shape = (parts[0].shape[0], weight.shape[1])
    return pl.pallas_call(
        functools.partial(
            project_body, group=group, low=low, last=last, first=first
        ),
        out_shape=jax.ShapeDtypeStruct(shape, jnp.bfloat16 if last else jnp.float32),
        in_specs=[SMEM, SMEM] + [VMEM] * len(operands),
        out_specs=VMEM,
        compiler_params=pltpu.CompilerParams(vmem_limit_bytes=24 << 20),
        name="project",
    )(starts, place, *operands)


def pick_body(place, table, out, sem):
    row = pl.multiple_of(place[2] // 8 * 8, 8)
    copy = pltpu.make_async_copy(table.at[pl.ds(row, 8), :], out, sem)
    copy.start()
    copy.wait()


def pick_gate(place, table):
    return pl.pallas_call(
        pick_body,
        out_shape=jax.ShapeDtypeStruct((8, table.shape[1]), table.dtype),
        in_specs=[SMEM, HBM],
        out_specs=VMEM,
        scratch_shapes=[pltpu.SemaphoreType.DMA],
        compiler_params=pltpu.CompilerParams(vmem_limit_bytes=1 << 20),
        name="pick",
    )(place, table)


def key_bias(block_mask, live_limit, sources, rows, half, history_rows, core):
    block_count = block_mask.shape[0]
    fresh = (sources[:, None] * rows + jnp.arange(rows, dtype=jnp.int32)[None, :]).reshape(-1) // BLK
    hot = fresh[:, None] == jnp.arange(block_count, dtype=jnp.int32)[None, :]
    mask = block_mask > 0

    def fresh_part(columns):
        return jnp.any(hot[None, :, :] & columns[:, None, :], axis=2)

    def history_part(which):
        base = sources[:, None] * history_rows + which * half
        position = (base + jnp.arange(half, dtype=jnp.int32)[None, :]).reshape(-1)
        return jnp.broadcast_to((position < live_limit)[None, :], (block_count, position.shape[0]))

    allowed = jnp.concatenate(
        [
            fresh_part(mask[:, block_count:]),
            fresh_part(mask[:, :block_count]),
            history_part(core),
            history_part(1 - core),
        ],
        axis=1,
    )
    return jnp.where(allowed, 0.0, NEGATIVE).astype(jnp.float32)[:, None, :]


def on_device(
    query, stretch_kv, history_kv, block_mask, noise_level, history_blocks, out_weight, gate_table
):
    tp_count = lax.axis_size("tp")
    tp_index = lax.axis_index("tp")
    core = lax.axis_index("stretch")
    rows = query.shape[1]
    feature_width = query.shape[2]
    history_rows = history_kv.shape[1]
    half = history_rows // 2
    group = head_groups(feature_width // HD, tp_count)
    outer = tp_count // group
    width = feature_width // group
    total_rows = tp_count * rows
    member = tp_index % group
    kv_rows = 2 * half + 2 * rows
    place = jnp.stack([member, core, noise_level[0]]).astype(jnp.int32)
    same = [[o * group + m for o in range(outer)] for m in range(group)]
    chunks = [(low * HD, count * HD) for low, count in head_chunks(width // HD, CHUNKS)]

    sources = tp_index - member + (member ^ jnp.arange(group, dtype=jnp.int32))
    bias = key_bias(
        block_mask[0], history_blocks[0] * BLK, sources, rows, half, history_rows, core
    )

    inner = max(group // 2, 1)
    cross = list(range(group - 1, inner - 1, -1))
    plan = [(step, low, cols) for low, cols in chunks[:1] for step in cross]
    plan += [(step, 0, width) for step in range(inner)]
    plan += [(step, low, cols) for low, cols in chunks[1:] for step in cross]
    blocks = pack(place, query[0], stretch_kv[:, 0], history_kv, width, plan)
    sends = [{} for _ in chunks]
    near = {}
    for (step, low, cols), block in zip(plan, blocks):
        if step >= inner:
            index = [first for first, _ in chunks].index(low)
            sends[index][step] = xor_permute(block, group, step)
        elif step == 0:
            near[step] = block
        else:
            near[step] = xor_permute(block, group, step)
    other_near = partner_core(
        jnp.concatenate([near[step][:kv_rows] for step in range(inner)], axis=0)
    )

    gathered = []
    for index, (low, cols) in enumerate(chunks):
        far = sends[index]
        own = [near[step] for step in range(inner)] + [far[step] for step in reversed(cross)]
        others = [other_near]
        if cross:
            others.append(
                partner_core(
                    jnp.concatenate([far[step][:kv_rows] for step in reversed(cross)], axis=0)
                )
            )
        attend = functools.partial(
            attention,
            place,
            bias,
            own,
            others,
            rows=rows,
            half=half,
            total_rows=total_rows,
            low=low,
            cols=cols,
        )
        if outer > 1:
            q = jnp.stack(
                [
                    block[kv_rows:, low : low + cols] if step < inner else block[kv_rows:]
                    for step, block in enumerate(own)
                ]
            )
            q = lax.all_gather(q, "tp", axis=0, axis_index_groups=same)
            out, peak, total = attend(q_all=q)
            outs, peaks, totals = (
                lax.all_gather(value, "tp", axis=0, axis_index_groups=same)
                for value in (out, peak, total)
            )
            factor = jnp.exp2(peaks - jnp.max(peaks, axis=0, keepdims=True))
            total = jnp.sum(totals * factor, axis=0)
            outs = outs.reshape(outer, total_rows, -1, HD) * factor[..., None]
            attended = (jnp.sum(outs, axis=0) / total[..., None]).astype(jnp.bfloat16)
            attended = attended.reshape(total_rows, -1)
        else:
            attended = attend(q_all=None)
        parts, members = spread(attended, member, group)
        gathered.append(parts)
    starts = (jnp.stack(members) * width).astype(jnp.int32)

    gate_rows = pick_gate(place, gate_table)
    result = None
    for index, ((low, _), parts) in enumerate(zip(chunks, gathered)):
        gate = gate_rows if index == len(chunks) - 1 else None
        result = project(starts, place, parts, out_weight, result, gate, low)
    return result[None]


def solution(mesh):
    return jax.shard_map(
        on_device,
        mesh=mesh,
        in_specs=(
            P(("rep", "stretch"), "tp", None),
            P(None, ("rep", "stretch"), "tp", None),
            P(None, ("rep", "tp"), None),
            P(("rep", "stretch"), None, None),
            P(("rep", "stretch")),
            P("rep"),
            P(None, "tp"),
            P(None, "tp"),
        ),
        out_specs=P(("rep", "stretch"), None, "tp"),
        check_vma=False,
    )
```

time: 150 us -> 143 us (0.953)
  local copies, waits for them, and re-layouts: 28.6 us -> 6.4 us
  starting transfers between devices: 33.8 us -> 48.5 us
  Pallas kernels: 18 us -> 20 us
    unnamed x30 -> x36, local copies, waits for them, and re-layouts: 22.1 us -> 4.97 us
    ppermute x14 -> x25, starting transfers between devices: 33.7 us -> 47.9 us  [xor_permute(): return lax.ppermute(value, 'tp', pairs)]
    dynamic_slice x2 -> x0, local copies, waits for them, and re-layouts: 3.68 us -> none  [the longest x1 3.08 us: block_for(): lax.dynamic_slice_in_dim(stacked, (member ^ step) * width, width, axis=1)]
    pallas_call x2 -> x6, Pallas kernels: 18 us -> 20 us  [the longest x2 9.14 us: attention(): pl.pallas_call(body, out_shape=(wide, thin, thin) if partial else wide, i...]
    ppermute x14 -> x25, waiting for transfers between devices: 63.2 us -> 63.5 us  [xor_permute(): return lax.ppermute(value, 'tp', pairs)]
  transfers between devices with their start and end apart: 15 -> 28, of which waited for: 9 -> 11; matrix products, arithmetic and copies ran while one was open for 12% -> 1% of each run, Pallas kernels for 0% -> 9%
where the time goes in v2:
time: 143 us
  waiting for transfers between devices  65.1 us (46%)
  starting transfers between devices  48.5 us (34%)
  Pallas kernels  20 us (14%)
  local copies, waits for them, and re-layouts  6.4 us (4%)
  between operations  1.7 us (1%)
    ppermute x25, waiting for transfers between devices, xor_permute(): return lax.ppermute(value, 'tp', pairs)  63.5 us
    ppermute x25, starting transfers between devices, xor_permute(): return lax.ppermute(value, 'tp', pairs)  47.9 us
    pallas_call x2, Pallas kernels, attention(): pl.pallas_call(body, out_shape=(wide, thin, thin) if partial else wide, i...  9.14 us
    pallas_call x2, Pallas kernels, project(): pl.pallas_call(functools.partial(project_body, group=group, low=low, last...  6.3 us
    unnamed x36, local copies, waits for them, and re-layouts  4.97 us
    pallas_call x1, Pallas kernels, pack(): pl.pallas_call(functools.partial(pack_body, half=half, rows=rows, width=w...  3.99 us
  transfers between devices with their start and end apart: 28, of which 11 were waited for; matrix products, arithmetic and copies ran while one was open for 1% of the time, Pallas kernels for 9%

profile of v2, /device:TPU:0, one launch (start us, length us, event | category | flops | bytes accessed | tf_op | source)
XLA Modules:
  0.0 143.0 jit_solution(3990555666236014747)
XLA Ops:
  0.7 0.6 pad_add_fusion.place
  1.3 4.0 %pack.1 = (bf16[448,256]{1,0:T(8,128)(2,1)}, bf16[448,256]{1,0:T(8,128)(2,1)}, bf16[448,256]{1,0:T(8,128)(2,1)}, bf16[448,256]{1,0:T(8,128)(2,1)}, bf16[448,384]...) custom-call(s32[3]{0:T(128)} %pad_add_fusion.place, ...), custom_call_target="tpu_custom_call" | custom-call | tf_op jit(solution)/shard_map/pack/pallas_call | solution.py:104
  5.3 3.1 %collective-permute-start = (bf16[448,384]{1,0:T(8,128)(2,1)}, bf16[448,384]{1,0:T(8,128)(2,1)S(1)}, u32[]{:S(2)}, u32[]{:S(2)}) collective-permute-start(bf16[448,384]{1,0:T(8,128)(2,1)} %get-tuple-element.18), channel_id=1, source_target_pairs={{0,1},{1,0},{2,3},{3,2},{4,5},{5,4},{6,7},{7,6},{8,9},{9,8},{10,11... | collective-permute-start | bytes 1032200 | tf_op jit(solution)/shard_map/ppermute | solution.py:41
  8.3 1.6 %collective-permute-start.1 = (bf16[448,384]{1,0:T(8,128)(2,1)}, bf16[448,384]{1,0:T(8,128)(2,1)S(1)}, u32[]{:S(2)}, u32[]{:S(2)}) collective-permute-start(bf16[448,384]{1,0:T(8,128)(2,1)} %get-tuple-element.19), channel_id=1, source_target_pairs={{0,2},{1,3},{2,0},{3,1},{4,6},{5,7},{6,4},{7,5},{8,10},{9,11},{10,... | collective-permute-start | bytes 1032200 | tf_op jit(solution)/shard_map/ppermute | solution.py:41
  9.9 3.0 %collective-permute-start.3 = (bf16[448,128]{1,0:T(8,128)(2,1)}, bf16[448,128]{1,0:T(8,128)(2,1)S(1)}, u32[]{:S(2)}, u32[]{:S(2)}) collective-permute-start(bf16[448,128]{1,0:T(8,128)(2,1)} %get-tuple-element.21), channel_id=1, source_target_pairs={{0,4},{1,5},{2,6},{3,7},{4,0},{5,1},{6,2},{7,3},{8,12},{9,13},{10,... | collective-permute-start | bytes 344072 | tf_op jit(solution)/shard_map/ppermute | solution.py:41
  12.9 1.3 collective-permute-start.4
  14.2 0.1 fusion.6
  14.3 0.1 iota_add_fusion
  14.3 0.1 add.112
  15.1 0.1 fusion.1
  15.2 0.1 fusion
  15.3 1.0 slice.44
  16.3 0.1 and_reduce_fusion.1
  16.4 13.7 %collective-permute-done.2.rest_3_ = bf16[448,384]{1,0:T(8,128)(2,1)S(1)} collective-permute-done((bf16[448,384]{1,0:T(8,128)(2,1)}, bf16[448,384]{1,0:T(8,128)(2,1)S(1)}, u32[]{:S(2)}, u32[]{:S(2)}) %collective-permute-start.2) | collective-permute-done | bytes 344096 | tf_op jit(solution)/shard_map/ppermute | solution.py:41
  30.1 3.8 %collective-permute-start.5 = (bf16[448,128]{1,0:T(8,128)(2,1)}, bf16[448,128]{1,0:T(8,128)(2,1)S(1)}, u32[]{:S(2)}, u32[]{:S(2)}) collective-permute-start(bf16[448,128]{1,0:T(8,128)(2,1)} %get-tuple-element.23), channel_id=1, source_target_pairs={{0,6},{1,7},{2,4},{3,5},{4,2},{5,3},{6,0},{7,1},{8,14},{9,15},{10,... | collective-permute-start | bytes 344072 | tf_op jit(solution)/shard_map/ppermute | solution.py:41
  33.9 1.2 collective-permute-start.6
  35.3 0.0 collective-permute-done.rest_1_
  35.3 0.1 collective-permute-start.16
  35.4 0.1 pad_maximum_fusion
  35.5 0.0 collective-permute-done.3.rest_4_
  35.5 0.6 copy-done.15
  36.2 2.2 %collective-permute-start.17 = (bf16[448,256]{1,0:T(8,128)(2,1)S(1)}, bf16[448,256]{1,0:T(8,128)(2,1)S(1)}, u32[]{:S(2)}, u32[]{:S(2)}) collective-permute-start(bf16[448,256]{1,0:T(8,128)(2,1)S(1)} %copy-done.15), channel_id=1, source_target_pairs={{0,5},{1,4},{2,7},{3,6},{4,1},{5,0},{6,3},{7,2},{8,13},{9,12},{10,... | collective-permute-start | bytes 688136 | tf_op jit(solution)/shard_map/ppermute | solution.py:41
  38.3 0.0 collective-permute-done.4.rest_5_
  38.3 3.8 %collective-permute-start.18 = (bf16[448,256]{1,0:T(8,128)(2,1)S(1)}, bf16[448,256]{1,0:T(8,128)(2,1)S(1)}, u32[]{:S(2)}, u32[]{:S(2)}) collective-permute-start(bf16[448,256]{1,0:T(8,128)(2,1)S(1)} %copy-done.16), channel_id=1, source_target_pairs={{0,6},{1,7},{2,4},{3,5},{4,2},{5,3},{6,0},{7,1},{8,14},{9,15},{10,... | collective-permute-start | bytes 688136 | tf_op jit(solution)/shard_map/ppermute | solution.py:41
  42.1 0.0 collective-permute-done.5.rest_6_
  42.1 1.2 collective-permute-start.19
  43.4 16.8 %collective-permute-done.19.rest_7_ = bf16[448,256]{1,0:T(8,128)(2,1)S(1)} collective-permute-done((bf16[448,256]{1,0:T(8,128)(2,1)S(1)}, bf16[448,256]{1,0:T(8,128)(2,1)S(1)}, u32[]{:S(2)}, u32[]{:S(2)}) %collective-permute-start.19) | collective-permute-done | bytes 229408 | tf_op jit(solution)/shard_map/ppermute | solution.py:41
  60.3 0.0 collective-permute-done.18.rest_6_
  60.3 0.0 copy-start.3
  60.3 12.3 %collective-permute-done.17.rest_5_ = bf16[448,256]{1,0:T(8,128)(2,1)S(1)} collective-permute-done((bf16[448,256]{1,0:T(8,128)(2,1)S(1)}, bf16[448,256]{1,0:T(8,128)(2,1)S(1)}, u32[]{:S(2)}, u32[]{:S(2)}) %collective-permute-start.17) | collective-permute-done | bytes 229408 | tf_op jit(solution)/shard_map/ppermute | solution.py:41
  72.7 0.1 pad_maximum_fusion.1
  72.7 0.1 collective-permute-start.20
  72.8 0.6 collective-permute-start.8
  73.4 0.1 copy_select_fusion.bias_ref
  73.5 1.6 %collective-permute-done.20.rest_9_ = bf16[1536,256]{1,0:T(8,128)(2,1)S(1)} collective-permute-done((bf16[1536,256]{1,0:T(8,128)(2,1)S(1)}, bf16[1536,256]{1,0:T(8,128)(2,1)S(1)}, u32[]{:S(2)}, u32[]{:S(2)}) %collective-permute-start.20) | collective-permute-done | bytes 786464 | tf_op jit(solution)/shard_map/ppermute | solution.py:63
  75.1 6.1 %attend.3.rest_0_ = bf16[512,256]{1,0:T(8,128)(2,1)} custom-call(s32[3]{0:T(128)S(1)} %copy-done.12, f32[4,1,3072]{2,1,0:T(1,128)S(1)} %copy_select_fusion.bias_ref, bf16[448,384]{1,0:T(8,128)(2,1)S(1)} %copy-done.3, bf16[448,384]{1,0:T(8,128)(2,1)S(1)} %collective-permute-done.rest_1_, bf16[448,384]{1,0:T(8,128)(2,1)S(1)} %collective-permute-done.1.rest_2_, ...), custom_call_target="tpu_custom_call" | custom-call | tf_op jit(solution)/shard_map/attend/pallas_call | solution.py:211
  81.2 10.2 %collective-permute-start.22 = (bf16[512,256]{1,0:T(8,128)(2,1)}, bf16[512,256]{1,0:T(8,128)(2,1)}, u32[]{:S(2)}, u32[]{:S(2)}) collective-permute-start(bf16[512,256]{1,0:T(8,128)(2,1)} %attend.3.rest_0_), channel_id=1, source_target_pairs={{0,4},{1,5},{2,6},{3,7},{4,0},{5,1},{6,2},{7,3},{8,12},{9,13},{10,... | collective-permute-start | bytes 786440 | tf_op jit(solution)/shard_map/ppermute | solution.py:41
  91.5 1.0 copy-done.5
  92.5 1.0 copy-done.7
  93.4 3.0 %attend.2.rest_0_ = bf16[512,128]{1,0:T(8,128)(2,1)S(1)} custom-call(s32[3]{0:T(128)S(1)} %copy-done.12, f32[4,1,3072]{2,1,0:T(1,128)S(1)} %copy_select_fusion.bias_ref, bf16[448,384]{1,0:T(8,128)(2,1)S(1)} %copy-done.3, bf16[448,384]{1,0:T(8,128)(2,1)S(1)} %collective-permute-done.rest_1_, bf16[448,384]{1,0:T(8,128)(2,1)S(1)} %copy-done.5, ...), custom_call_target="tpu_custom_call" | custom-call | tf_op jit(solution)/shard_map/attend/pallas_call | solution.py:211
  96.5 2.1 %collective-permute-start.9 = (bf16[512,128]{1,0:T(8,128)(2,1)S(1)}, bf16[512,128]{1,0:T(8,128)(2,1)}, u32[]{:S(2)}, u32[]{:S(2)}) collective-permute-start(bf16[512,128]{1,0:T(8,128)(2,1)S(1)} %attend.2.rest_0_), channel_id=1, source_target_pairs={{0,2},{1,3},{2,0},{3,1},{4,6},{5,7},{6,4},{7,5},{8,10},{9,11},{10,... | collective-permute-start | bytes 393224 | tf_op jit(solution)/shard_map/ppermute | solution.py:41
  98.6 5.5 %collective-permute-done.22.rest_2_ = bf16[512,256]{1,0:T(8,128)(2,1)} collective-permute-done((bf16[512,256]{1,0:T(8,128)(2,1)}, bf16[512,256]{1,0:T(8,128)(2,1)}, u32[]{:S(2)}, u32[]{:S(2)}) %collective-permute-start.22) | collective-permute-done | bytes 262176 | tf_op jit(solution)/shard_map/ppermute | solution.py:41
  104.1 0.0 collective-permute-start.23
  104.1 1.5 %collective-permute-start.24 = (bf16[512,256]{1,0:T(8,128)(2,1)}, bf16[512,256]{1,0:T(8,128)(2,1)}, u32[]{:S(2)}, u32[]{:S(2)}) collective-permute-start(bf16[512,256]{1,0:T(8,128)(2,1)} %attend.3.rest_0_), channel_id=1, source_target_pairs={{0,1},{1,0},{2,3},{3,2},{4,5},{5,4},{6,7},{7,6},{8,9},{9,8},{10,11... | collective-permute-start | bytes 786440 | tf_op jit(solution)/shard_map/ppermute | solution.py:41
  105.6 2.2 %collective-permute-start.10 = (bf16[512,128]{1,0:T(8,128)(2,1)S(1)}, bf16[512,128]{1,0:T(8,128)(2,1)}, u32[]{:S(2)}, u32[]{:S(2)}) collective-permute-start(bf16[512,128]{1,0:T(8,128)(2,1)S(1)} %attend.2.rest_0_), channel_id=1, source_target_pairs={{0,4},{1,5},{2,6},{3,7},{4,0},{5,1},{6,2},{7,3},{8,12},{9,13},{10,... | collective-permute-start | bytes 393224 | tf_op jit(solution)/shard_map/ppermute | solution.py:41
  107.8 0.8 collective-permute-start.25
  108.6 1.2 collective-permute-start.26
  109.9 4.6 %collective-permute-done.10.rest_2_ = bf16[512,128]{1,0:T(8,128)(2,1)} collective-permute-done((bf16[512,128]{1,0:T(8,128)(2,1)S(1)}, bf16[512,128]{1,0:T(8,128)(2,1)}, u32[]{:S(2)}, u32[]{:S(2)}) %collective-permute-start.10) | collective-permute-done | bytes 131104 | tf_op jit(solution)/shard_map/ppermute | solution.py:41
  114.4 3.1 %collective-permute-start.11 = (bf16[512,128]{1,0:T(8,128)(2,1)}, bf16[512,128]{1,0:T(8,128)(2,1)}, u32[]{:S(2)}, u32[]{:S(2)}) collective-permute-start(bf16[512,128]{1,0:T(8,128)(2,1)} %collective-permute-done.10.rest_2_), channel_id=1, source_target_pairs={{0,2},{1,3},{2,0},{3,1},{4,6},{5,7},{6,4},{7,5},{8,10},{9,11},{10,... | collective-permute-start | bytes 393224 | tf_op jit(solution)/shard_map/ppermute | solution.py:41
  117.5 1.2 collective-permute-start.27
  118.7 0.6 pick.1.rest_9_
  119.3 0.1 stack.42
  119.4 0.9 collective-permute-start.12
  120.3 0.5 collective-permute-done.11.rest_3_
  120.8 1.2 collective-permute-start.14
  122.0 0.8 collective-permute-start.13
  122.8 2.0 %collective-permute-done.26.rest_6_ = bf16[512,256]{1,0:T(8,128)(2,1)} collective-permute-done((bf16[512,256]{1,0:T(8,128)(2,1)}, bf16[512,256]{1,0:T(8,128)(2,1)}, u32[]{:S(2)}, u32[]{:S(2)}) %collective-permute-start.26) | collective-permute-done | bytes 262176 | tf_op jit(solution)/shard_map/ppermute | solution.py:41
  124.8 1.5 %collective-permute-start.15 = (bf16[512,128]{1,0:T(8,128)(2,1)}, bf16[512,128]{1,0:T(8,128)(2,1)S(1)}, u32[]{:S(2)}, u32[]{:S(2)}) collective-permute-start(bf16[512,128]{1,0:T(8,128)(2,1)} %collective-permute-done.11.rest_3_), channel_id=1, source_target_pairs={{0,1},{1,0},{2,3},{3,2},{4,5},{5,4},{6,7},{7,6},{8,9},{9,8},{10,11... | collective-permute-start | bytes 393224 | tf_op jit(solution)/shard_map/ppermute | solution.py:41
  126.3 4.1 %collective-permute-done.27.rest_7_ = bf16[512,256]{1,0:T(8,128)(2,1)} collective-permute-done((bf16[512,256]{1,0:T(8,128)(2,1)S(1)}, bf16[512,256]{1,0:T(8,128)(2,1)}, u32[]{:S(2)}, u32[]{:S(2)}) %collective-permute-start.27) | collective-permute-done | bytes 262176 | tf_op jit(solution)/shard_map/ppermute | solution.py:41
  130.4 2.3 %copy-done = bf16[3072,768]{1,0:T(8,128)(2,1)S(1)} copy-done((bf16[3072,768]{1,0:T(8,128)(2,1)S(1)}, bf16[3072,768]{1,0:T(8,128)(2,1)}, u32[]{:S(2)}) %copy-start) | copy-done | bytes 4718616
  132.8 3.4 %project.2.rest_8_ = f32[512,768]{1,0:T(8,128)S(1)} custom-call(s32[8]{0:T(128)S(1)} %broadcast_multiply_fusion.starts, s32[3]{0:T(128)S(1)} %copy-done.12, bf16[3072,768]{1,0:T(8,128)(2,1)S(1)} %copy-done, bf16[512,256]{1,0:T(8,128)(2,1)} %attend.3.rest_0_, bf16[512,256]{1,0:T(8,128)(2,1)} %collective-permute-done.21.rest_1_, ...), custom_call_target="tpu_custom_call" | custom-call | tf_op jit(solution)/shard_map/project/pallas_call | solution.py:252
  136.2 2.5 %collective-permute-done.13.rest_5_ = bf16[512,128]{1,0:T(8,128)(2,1)S(1)} collective-permute-done((bf16[512,128]{1,0:T(8,128)(2,1)}, bf16[512,128]{1,0:T(8,128)(2,1)S(1)}, u32[]{:S(2)}, u32[]{:S(2)}) %collective-permute-start.13) | collective-permute-done | bytes 131104 | tf_op jit(solution)/shard_map/ppermute | solution.py:41
  138.7 1.4 collective-permute-done.15.rest_7_
  140.1 2.9 %project.3 = bf16[512,768]{1,0:T(8,128)(2,1)} custom-call(s32[8]{0:T(128)S(1)} %broadcast_multiply_fusion.starts, s32[3]{0:T(128)S(1)} %copy-done.12, bf16[3072,768]{1,0:T(8,128)(2,1)S(1)} %copy-done.1, bf16[512,128]{1,0:T(8,128)(2,1)S(1)} %attend.2.rest_0_, bf16[512,128]{1,0:T(8,128)(2,1)} %collective-permute-done.9.rest_1_, ...), custom_call_target="tpu_custom_call" | custom-call | tf_op jit(solution)/shard_map/project/pallas_call | solution.py:252
  (67 shorter events, 0.4 us)
Async XLA Ops:
  1.3 12.9 %copy-start.13 = (s32[1,4,8]{2,1,0:T(4,128)S(1)}, s32[1,4,8]{2,1,0:T(4,128)}, u32[]{:S(2)}) copy-start(s32[1,4,8]{2,1,0:T(4,128)} %param.11) | copy-start | bytes 388
  5.3 30.0 %copy-start.14 = (bf16[448,256]{1,0:T(8,128)(2,1)S(1)}, bf16[448,256]{1,0:T(8,128)(2,1)}, u32[]{:S(2)}) copy-start(bf16[448,256]{1,0:T(8,128)(2,1)} %get-tuple-element.25) | copy-start | bytes 688132
  5.3 30.0 %collective-permute-start = (bf16[448,384]{1,0:T(8,128)(2,1)}, bf16[448,384]{1,0:T(8,128)(2,1)S(1)}, u32[]{:S(2)}, u32[]{:S(2)}) collective-permute-start(bf16[448,384]{1,0:T(8,128)(2,1)} %get-tuple-element.18), channel_id=1, source_target_pairs={{0,1},{1,0},{2,3},{3,2},{4,5},{5,4},{6,7},{7,6},{8,9},{9,8},{10,11... | collective-permute-start | bytes 1032200 | tf_op jit(solution)/shard_map/ppermute | solution.py:41
  8.3 25.6 %collective-permute-start.1 = (bf16[448,384]{1,0:T(8,128)(2,1)}, bf16[448,384]{1,0:T(8,128)(2,1)S(1)}, u32[]{:S(2)}, u32[]{:S(2)}) collective-permute-start(bf16[448,384]{1,0:T(8,128)(2,1)} %get-tuple-element.19), channel_id=1, source_target_pairs={{0,2},{1,3},{2,0},{3,1},{4,6},{5,7},{6,4},{7,5},{8,10},{9,11},{10,... | collective-permute-start | bytes 1032200 | tf_op jit(solution)/shard_map/ppermute | solution.py:41
  9.9 20.2 %collective-permute-start.2 = (bf16[448,384]{1,0:T(8,128)(2,1)}, bf16[448,384]{1,0:T(8,128)(2,1)S(1)}, u32[]{:S(2)}, u32[]{:S(2)}) collective-permute-start(bf16[448,384]{1,0:T(8,128)(2,1)} %get-tuple-element.20), channel_id=1, source_target_pairs={{0,3},{1,2},{2,1},{3,0},{4,7},{5,6},{6,5},{7,4},{8,11},{9,10},{10,... | collective-permute-start | bytes 1032200 | tf_op jit(solution)/shard_map/ppermute | solution.py:41
  9.9 25.6 %collective-permute-start.3 = (bf16[448,128]{1,0:T(8,128)(2,1)}, bf16[448,128]{1,0:T(8,128)(2,1)S(1)}, u32[]{:S(2)}, u32[]{:S(2)}) collective-permute-start(bf16[448,128]{1,0:T(8,128)(2,1)} %get-tuple-element.21), channel_id=1, source_target_pairs={{0,4},{1,5},{2,6},{3,7},{4,0},{5,1},{6,2},{7,3},{8,12},{9,13},{10,... | collective-permute-start | bytes 344072 | tf_op jit(solution)/shard_map/ppermute | solution.py:41
  12.9 25.4 %collective-permute-start.4 = (bf16[448,128]{1,0:T(8,128)(2,1)}, bf16[448,128]{1,0:T(8,128)(2,1)S(1)}, u32[]{:S(2)}, u32[]{:S(2)}) collective-permute-start(bf16[448,128]{1,0:T(8,128)(2,1)} %get-tuple-element.22), channel_id=1, source_target_pairs={{0,5},{1,4},{2,7},{3,6},{4,1},{5,0},{6,3},{7,2},{8,13},{9,12},{10,... | collective-permute-start | bytes 344072 | tf_op jit(solution)/shard_map/ppermute | solution.py:41
  30.1 45.0 %copy-start.6 = (bf16[448,384]{1,0:T(8,128)(2,1)}, bf16[448,384]{1,0:T(8,128)(2,1)S(1)}, u32[]{:S(2)}) copy-start(bf16[448,384]{1,0:T(8,128)(2,1)S(1)} %collective-permute-done.2.rest_3_) | copy-start | bytes 1032196
  30.1 12.0 %collective-permute-start.5 = (bf16[448,128]{1,0:T(8,128)(2,1)}, bf16[448,128]{1,0:T(8,128)(2,1)S(1)}, u32[]{:S(2)}, u32[]{:S(2)}) collective-permute-start(bf16[448,128]{1,0:T(8,128)(2,1)} %get-tuple-element.23), channel_id=1, source_target_pairs={{0,6},{1,7},{2,4},{3,5},{4,2},{5,3},{6,0},{7,1},{8,14},{9,15},{10,... | collective-permute-start | bytes 344072 | tf_op jit(solution)/shard_map/ppermute | solution.py:41
  33.9 41.2 %copy-start.4 = (bf16[448,384]{1,0:T(8,128)(2,1)}, bf16[448,384]{1,0:T(8,128)(2,1)S(1)}, u32[]{:S(2)}) copy-start(bf16[448,384]{1,0:T(8,128)(2,1)S(1)} %collective-permute-done.1.rest_2_) | copy-start | bytes 1032196
  33.9 9.4 %collective-permute-start.6 = (bf16[448,128]{1,0:T(8,128)(2,1)}, bf16[448,128]{1,0:T(8,128)(2,1)S(1)}, u32[]{:S(2)}, u32[]{:S(2)}) collective-permute-start(bf16[448,128]{1,0:T(8,128)(2,1)} %get-tuple-element.24), channel_id=1, source_target_pairs={{0,7},{1,6},{2,5},{3,4},{4,3},{5,2},{6,1},{7,0},{8,15},{9,14},{10,... | collective-permute-start | bytes 344072 | tf_op jit(solution)/shard_map/ppermute | solution.py:41
  35.2 0.9 copy-start.15
  35.2 3.1 %copy-start.16 = (bf16[448,256]{1,0:T(8,128)(2,1)S(1)}, bf16[448,256]{1,0:T(8,128)(2,1)}, u32[]{:S(2)}) copy-start(bf16[448,256]{1,0:T(8,128)(2,1)} %get-tuple-element.27) | copy-start | bytes 688132
  35.2 6.9 %copy-start.17 = (bf16[448,256]{1,0:T(8,128)(2,1)S(1)}, bf16[448,256]{1,0:T(8,128)(2,1)}, u32[]{:S(2)}) copy-start(bf16[448,256]{1,0:T(8,128)(2,1)} %get-tuple-element.28) | copy-start | bytes 688132
  35.3 37.3 %collective-permute-start.16 = (bf16[448,256]{1,0:T(8,128)(2,1)S(1)}, bf16[448,256]{1,0:T(8,128)(2,1)S(1)}, u32[]{:S(2)}, u32[]{:S(2)}) collective-permute-start(bf16[448,256]{1,0:T(8,128)(2,1)S(1)} %copy-done.14), channel_id=1, source_target_pairs={{0,4},{1,5},{2,6},{3,7},{4,0},{5,1},{6,2},{7,3},{8,12},{9,13},{10,... | collective-permute-start | bytes 688136 | tf_op jit(solution)/shard_map/ppermute | solution.py:41
  35.5 37.2 %copy-start.8 = (bf16[448,128]{1,0:T(8,128)(2,1)}, bf16[448,128]{1,0:T(8,128)(2,1)S(1)}, u32[]{:S(2)}) copy-start(bf16[448,128]{1,0:T(8,128)(2,1)S(1)} %collective-permute-done.3.rest_4_) | copy-start | bytes 344068
  36.2 36.4 %collective-permute-start.17 = (bf16[448,256]{1,0:T(8,128)(2,1)S(1)}, bf16[448,256]{1,0:T(8,128)(2,1)S(1)}, u32[]{:S(2)}, u32[]{:S(2)}) collective-permute-start(bf16[448,256]{1,0:T(8,128)(2,1)S(1)} %copy-done.15), channel_id=1, source_target_pairs={{0,5},{1,4},{2,7},{3,6},{4,1},{5,0},{6,3},{7,2},{8,13},{9,12},{10,... | collective-permute-start | bytes 688136 | tf_op jit(solution)/shard_map/ppermute | solution.py:41
  38.3 34.4 %copy-start.10 = (bf16[448,128]{1,0:T(8,128)(2,1)}, bf16[448,128]{1,0:T(8,128)(2,1)S(1)}, u32[]{:S(2)}) copy-start(bf16[448,128]{1,0:T(8,128)(2,1)S(1)} %collective-permute-done.4.rest_5_) | copy-start | bytes 344068
  38.3 22.0 %collective-permute-start.18 = (bf16[448,256]{1,0:T(8,128)(2,1)S(1)}, bf16[448,256]{1,0:T(8,128)(2,1)S(1)}, u32[]{:S(2)}, u32[]{:S(2)}) collective-permute-start(bf16[448,256]{1,0:T(8,128)(2,1)S(1)} %copy-done.16), channel_id=1, source_target_pairs={{0,6},{1,7},{2,4},{3,5},{4,2},{5,3},{6,0},{7,1},{8,14},{9,15},{10,... | collective-permute-start | bytes 688136 | tf_op jit(solution)/shard_map/ppermute | solution.py:41
  42.1 18.1 %collective-permute-start.19 = (bf16[448,256]{1,0:T(8,128)(2,1)S(1)}, bf16[448,256]{1,0:T(8,128)(2,1)S(1)}, u32[]{:S(2)}, u32[]{:S(2)}) collective-permute-start(bf16[448,256]{1,0:T(8,128)(2,1)S(1)} %copy-done.17), channel_id=1, source_target_pairs={{0,7},{1,6},{2,5},{3,4},{4,3},{5,2},{6,1},{7,0},{8,15},{9,14},{10,... | collective-permute-start | bytes 688136 | tf_op jit(solution)/shard_map/ppermute | solution.py:41
  43.3 31.8 %collective-permute-start.7 = (bf16[1536,384]{1,0:T(8,128)(2,1)S(1)}, bf16[1536,384]{1,0:T(8,128)(2,1)S(1)}, u32[]{:S(2)}, u32[]{:S(2)}) collective-permute-start(bf16[1536,384]{1,0:T(8,128)(2,1)S(1)} %pad_maximum_fusion), channel_id=1, source_target_pairs={{0,8},{8,0},{1,9},{9,1},{2,10},{10,2},{3,11},{11,3},{4,12},{12,4},... | collective-permute-start | bytes 3538952 | tf_op jit(solution)/shard_map/ppermute | solution.py:63
  60.3 14.8 %copy-start.3 = (bf16[448,384]{1,0:T(8,128)(2,1)S(1)}, bf16[448,384]{1,0:T(8,128)(2,1)}, u32[]{:S(2)}) copy-start(bf16[448,384]{1,0:T(8,128)(2,1)} %get-tuple-element.17.rest_0_) | copy-start | bytes 1032196
  60.3 14.8 %copy-start.12 = (s32[3]{0:T(128)S(1)}, s32[3]{0:T(128)}, u32[]{:S(2)}) copy-start(s32[3]{0:T(128)} %pad_add_fusion.place) | copy-start | bytes 40
  72.7 2.4 %collective-permute-start.20 = (bf16[1536,256]{1,0:T(8,128)(2,1)S(1)}, bf16[1536,256]{1,0:T(8,128)(2,1)S(1)}, u32[]{:S(2)}, u32[]{:S(2)}) collective-permute-start(bf16[1536,256]{1,0:T(8,128)(2,1)S(1)} %pad_maximum_fusion.1), channel_id=1, source_target_pairs={{0,8},{8,0},{1,9},{9,1},{2,10},{10,2},{3,11},{11,3},{4,12},{12,4},... | collective-permute-start | bytes 2359304 | tf_op jit(solution)/shard_map/ppermute | solution.py:63
  72.8 18.6 %collective-permute-start.8 = (bf16[1536,128]{1,0:T(8,128)(2,1)S(1)}, bf16[1536,128]{1,0:T(8,128)(2,1)S(1)}, u32[]{:S(2)}, u32[]{:S(2)}) collective-permute-start(bf16[1536,128]{1,0:T(8,128)(2,1)S(1)} %pad_maximum_fusion.2), channel_id=1, source_target_pairs={{0,8},{8,0},{1,9},{9,1},{2,10},{10,2},{3,11},{11,3},{4,12},{12,4},... | collective-permute-start | bytes 1179656 | tf_op jit(solution)/shard_map/ppermute | solution.py:63
  73.5 18.0 %copy-start.9 = (bf16[448,128]{1,0:T(8,128)(2,1)S(1)}, bf16[448,128]{1,0:T(8,128)(2,1)}, u32[]{:S(2)}) copy-start(bf16[448,128]{1,0:T(8,128)(2,1)} %copy-done.8) | copy-start | bytes 344068
  73.5 18.0 %copy-start.11 = (bf16[448,128]{1,0:T(8,128)(2,1)S(1)}, bf16[448,128]{1,0:T(8,128)(2,1)}, u32[]{:S(2)}) copy-start(bf16[448,128]{1,0:T(8,128)(2,1)} %copy-done.10) | copy-start | bytes 344068
  81.2 37.5 %copy-start.2 = (f32[1000,768]{1,0:T(8,128)S(1)}, f32[1000,768]{1,0:T(8,128)}, u32[]{:S(2)}) copy-start(f32[1000,768]{1,0:T(8,128)} %table.1) | copy-start | bytes 9216004
  81.2 22.9 %collective-permute-start.22 = (bf16[512,256]{1,0:T(8,128)(2,1)}, bf16[512,256]{1,0:T(8,128)(2,1)}, u32[]{:S(2)}, u32[]{:S(2)}) collective-permute-start(bf16[512,256]{1,0:T(8,128)(2,1)} %attend.3.rest_0_), channel_id=1, source_target_pairs={{0,4},{1,5},{2,6},{3,7},{4,0},{5,1},{6,2},{7,3},{8,12},{9,13},{10,... | collective-permute-start | bytes 786440 | tf_op jit(solution)/shard_map/ppermute | solution.py:41
  91.4 16.4 %collective-permute-start.21 = (bf16[512,256]{1,0:T(8,128)(2,1)}, bf16[512,256]{1,0:T(8,128)(2,1)}, u32[]{:S(2)}, u32[]{:S(2)}) collective-permute-start(bf16[512,256]{1,0:T(8,128)(2,1)} %attend.3.rest_0_), channel_id=1, source_target_pairs={{0,2},{1,3},{2,0},{3,1},{4,6},{5,7},{6,4},{7,5},{8,10},{9,11},{10,... | collective-permute-start | bytes 786440 | tf_op jit(solution)/shard_map/ppermute | solution.py:41
  91.5 1.0 copy-start.5
  92.5 1.0 copy-start.7
  96.5 12.1 %collective-permute-start.9 = (bf16[512,128]{1,0:T(8,128)(2,1)S(1)}, bf16[512,128]{1,0:T(8,128)(2,1)}, u32[]{:S(2)}, u32[]{:S(2)}) collective-permute-start(bf16[512,128]{1,0:T(8,128)(2,1)S(1)} %attend.2.rest_0_), channel_id=1, source_target_pairs={{0,2},{1,3},{2,0},{3,1},{4,6},{5,7},{6,4},{7,5},{8,10},{9,11},{10,... | collective-permute-start | bytes 393224 | tf_op jit(solution)/shard_map/ppermute | solution.py:41
  104.1 13.4 %collective-permute-start.23 = (bf16[512,256]{1,0:T(8,128)(2,1)}, bf16[512,256]{1,0:T(8,128)(2,1)S(1)}, u32[]{:S(2)}, u32[]{:S(2)}) collective-permute-start(bf16[512,256]{1,0:T(8,128)(2,1)} %collective-permute-done.22.rest_2_), channel_id=1, source_target_pairs={{0,2},{1,3},{2,0},{3,1},{4,6},{5,7},{6,4},{7,5},{8,10},{9,11},{10,... | collective-permute-start | bytes 786440 | tf_op jit(solution)/shard_map/ppermute | solution.py:41
  104.1 15.3 %collective-permute-start.24 = (bf16[512,256]{1,0:T(8,128)(2,1)}, bf16[512,256]{1,0:T(8,128)(2,1)}, u32[]{:S(2)}, u32[]{:S(2)}) collective-permute-start(bf16[512,256]{1,0:T(8,128)(2,1)} %attend.3.rest_0_), channel_id=1, source_target_pairs={{0,1},{1,0},{2,3},{3,2},{4,5},{5,4},{6,7},{7,6},{8,9},{9,8},{10,11... | collective-permute-start | bytes 786440 | tf_op jit(solution)/shard_map/ppermute | solution.py:41
  105.6 8.8 %collective-permute-start.10 = (bf16[512,128]{1,0:T(8,128)(2,1)S(1)}, bf16[512,128]{1,0:T(8,128)(2,1)}, u32[]{:S(2)}, u32[]{:S(2)}) collective-permute-start(bf16[512,128]{1,0:T(8,128)(2,1)S(1)} %attend.2.rest_0_), channel_id=1, source_target_pairs={{0,4},{1,5},{2,6},{3,7},{4,0},{5,1},{6,2},{7,3},{8,12},{9,13},{10,... | collective-permute-start | bytes 393224 | tf_op jit(solution)/shard_map/ppermute | solution.py:41
  107.8 14.2 %collective-permute-start.25 = (bf16[512,256]{1,0:T(8,128)(2,1)}, bf16[512,256]{1,0:T(8,128)(2,1)}, u32[]{:S(2)}, u32[]{:S(2)}) collective-permute-start(bf16[512,256]{1,0:T(8,128)(2,1)} %collective-permute-done.21.rest_1_), channel_id=1, source_target_pairs={{0,1},{1,0},{2,3},{3,2},{4,5},{5,4},{6,7},{7,6},{8,9},{9,8},{10,11... | collective-permute-start | bytes 786440 | tf_op jit(solution)/shard_map/ppermute | solution.py:41
  108.6 16.2 %collective-permute-start.26 = (bf16[512,256]{1,0:T(8,128)(2,1)}, bf16[512,256]{1,0:T(8,128)(2,1)}, u32[]{:S(2)}, u32[]{:S(2)}) collective-permute-start(bf16[512,256]{1,0:T(8,128)(2,1)} %collective-permute-done.22.rest_2_), channel_id=1, source_target_pairs={{0,1},{1,0},{2,3},{3,2},{4,5},{5,4},{6,7},{7,6},{8,9},{9,8},{10,11... | collective-permute-start | bytes 786440 | tf_op jit(solution)/shard_map/ppermute | solution.py:41
  114.4 6.3 %collective-permute-start.11 = (bf16[512,128]{1,0:T(8,128)(2,1)}, bf16[512,128]{1,0:T(8,128)(2,1)}, u32[]{:S(2)}, u32[]{:S(2)}) collective-permute-start(bf16[512,128]{1,0:T(8,128)(2,1)} %collective-permute-done.10.rest_2_), channel_id=1, source_target_pairs={{0,2},{1,3},{2,0},{3,1},{4,6},{5,7},{6,4},{7,5},{8,10},{9,11},{10,... | collective-permute-start | bytes 393224 | tf_op jit(solution)/shard_map/ppermute | solution.py:41
  117.5 12.9 %collective-permute-start.27 = (bf16[512,256]{1,0:T(8,128)(2,1)S(1)}, bf16[512,256]{1,0:T(8,128)(2,1)}, u32[]{:S(2)}, u32[]{:S(2)}) collective-permute-start(bf16[512,256]{1,0:T(8,128)(2,1)S(1)} %collective-permute-done.23.rest_3_), channel_id=1, source_target_pairs={{0,1},{1,0},{2,3},{3,2},{4,5},{5,4},{6,7},{7,6},{8,9},{9,8},{10,11... | collective-permute-start | bytes 786440 | tf_op jit(solution)/shard_map/ppermute | solution.py:41
  119.4 16.7 %collective-permute-start.12 = (bf16[512,128]{1,0:T(8,128)(2,1)S(1)}, bf16[512,128]{1,0:T(8,128)(2,1)S(1)}, u32[]{:S(2)}, u32[]{:S(2)}) collective-permute-start(bf16[512,128]{1,0:T(8,128)(2,1)S(1)} %attend.2.rest_0_), channel_id=1, source_target_pairs={{0,1},{1,0},{2,3},{3,2},{4,5},{5,4},{6,7},{7,6},{8,9},{9,8},{10,11... | collective-permute-start | bytes 393224 | tf_op jit(solution)/shard_map/ppermute | solution.py:41
  120.8 17.9 %collective-permute-start.14 = (bf16[512,128]{1,0:T(8,128)(2,1)}, bf16[512,128]{1,0:T(8,128)(2,1)S(1)}, u32[]{:S(2)}, u32[]{:S(2)}) collective-permute-start(bf16[512,128]{1,0:T(8,128)(2,1)} %collective-permute-done.10.rest_2_), channel_id=1, source_target_pairs={{0,1},{1,0},{2,3},{3,2},{4,5},{5,4},{6,7},{7,6},{8,9},{9,8},{10,11... | collective-permute-start | bytes 393224 | tf_op jit(solution)/shard_map/ppermute | solution.py:41
  122.0 16.7 %collective-permute-start.13 = (bf16[512,128]{1,0:T(8,128)(2,1)}, bf16[512,128]{1,0:T(8,128)(2,1)S(1)}, u32[]{:S(2)}, u32[]{:S(2)}) collective-permute-start(bf16[512,128]{1,0:T(8,128)(2,1)} %collective-permute-done.9.rest_1_), channel_id=1, source_target_pairs={{0,1},{1,0},{2,3},{3,2},{4,5},{5,4},{6,7},{7,6},{8,9},{9,8},{10,11... | collective-permute-start | bytes 393224 | tf_op jit(solution)/shard_map/ppermute | solution.py:41
  124.8 15.3 %collective-permute-start.15 = (bf16[512,128]{1,0:T(8,128)(2,1)}, bf16[512,128]{1,0:T(8,128)(2,1)S(1)}, u32[]{:S(2)}, u32[]{:S(2)}) collective-permute-start(bf16[512,128]{1,0:T(8,128)(2,1)} %collective-permute-done.11.rest_3_), channel_id=1, source_target_pairs={{0,1},{1,0},{2,3},{3,2},{4,5},{5,4},{6,7},{7,6},{8,9},{9,8},{10,11... | collective-permute-start | bytes 393224 | tf_op jit(solution)/shard_map/ppermute | solution.py:41
  130.4 2.3 %copy-start = (bf16[3072,768]{1,0:T(8,128)(2,1)S(1)}, bf16[3072,768]{1,0:T(8,128)(2,1)}, u32[]{:S(2)}) copy-start(bf16[3072,768]{1,0:T(8,128)(2,1)} %weight.3) | copy-start | bytes 14155780
  132.8 7.3 %copy-start.1 = (bf16[3072,768]{1,0:T(8,128)(2,1)S(1)}, bf16[3072,768]{1,0:T(8,128)(2,1)}, u32[]{:S(2)}) copy-start(bf16[3072,768]{1,0:T(8,128)(2,1)} %weight.3) | copy-start | bytes 14155780

commit v3 on v2

--- a/solution.py
+++ b/solution.py
@@ -14,6 +14,7 @@
 NEGATIVE = -1e30
 LOG2_SCALE = math.log2(math.e) / math.sqrt(HD)
 CHUNKS = 2
+VMEM_LIMIT = 12 << 20
 
 VMEM = pl.BlockSpec(memory_space=pltpu.VMEM)
 SMEM = pl.BlockSpec(memory_space=pltpu.SMEM)
@@ -41,30 +42,48 @@
     return lax.ppermute(value, "tp", pairs)
 
 
-def spread(value, member, group):
-    def send(block, step, senders=None):
-        return xor_permute(block, group, step, senders)
+def spread(value, heads, group):
+    def send(block, step):
+        return xor_permute(block, group, step)
+
+    def both(block, step):
+        return [(block, step), (send(block, 1), step ^ 1)]
 
     if group == 1:
-        return [value], [member]
-    line = [(value, member)]
+        return [(value, 0)], [[] for _ in heads]
+    near = both(value, 0)
     if group == 8:
-        over = send(value, 4)
-        line += [(send(value, 2), member ^ 2), (over, member ^ 4)]
-        line += [(send(over, 2), member ^ 6)]
-    else:
-        line += [(send(value, step), member ^ step) for step in range(2, group, 2)]
-    across = [(send(block, 1), source ^ 1) for block, source in line]
-    blocks, members = zip(*(line + across))
-    return list(blocks), list(members)
+        near += both(send(value, 2), 2)
+    far = []
+    for block in heads:
+        pieces = []
+        if group == 8:
+            over = send(block, 4)
+            pieces += both(over, 4)
+            pieces += both(send(over, 2), 6)
+        else:
+            for step in range(2, group, 2):
+                moved = send(block, step)
+                pieces += both(moved, step)
+        far.append(pieces)
+    return near, far
 
 
 def partner_core(value):
     return lax.ppermute(value, "stretch", [(0, 1), (1, 0)])
 
 
-def pack_body(place, query, stretch, history, *rest, half, rows, width, plan):
+def pack_body(place, *rest, half, rows, width, plan, gated):
+    if gated:
+        table, rest = rest[0], rest[1:]
+    query, stretch, history, rest = *rest[:3], rest[3:]
     count = len(plan)
+    if gated:
+        gate_out, rest = rest[0], rest[1:]
+        gate_sem, rest = rest[-1], rest[:-1]
+        gate_row = pl.multiple_of(place[2] // 8 * 8, 8)
+        gate_copy = pltpu.make_async_copy(table.at[pl.ds(gate_row, 8), :], gate_out, gate_sem)
+        gate_copy.start()
     blocks, stages = rest[:count], rest[count : 2 * count]
     in_sems, out_sems = rest[2 * count :]
     row = pl.multiple_of(place[1] * half, 8)
@@ -96,26 +115,54 @@
         outgoing.append(copy)
     for copy in outgoing:
         copy.wait()
-
-
-def pack(place, query, stretch, history, width, plan):
+    if gated:
+        gate_copy.wait()
+
+
+def pack(place, query, stretch, history, width, plan, table=None):
+    gated = table is not None
     rows, half = query.shape[0], history.shape[1] // 2
     shapes = [(2 * half + 3 * rows, cols) for _, _, cols in plan]
+    outs = [jax.ShapeDtypeStruct(shape, query.dtype) for shape in shapes]
+    scratch = [pltpu.VMEM(shape, query.dtype) for shape in shapes]
+    scratch += [pltpu.SemaphoreType.DMA((len(plan), 5)), pltpu.SemaphoreType.DMA((len(plan),))]
+    operands = [query, stretch, history]
+    out_specs = [HBM] * len(plan)
+    if gated:
+        outs = [jax.ShapeDtypeStruct((8, table.shape[1]), table.dtype)] + outs
+        out_specs = [VMEM] + out_specs
+        scratch.append(pltpu.SemaphoreType.DMA)
+        operands = [table] + operands
     return pl.pallas_call(
-        functools.partial(pack_body, half=half, rows=rows, width=width, plan=plan),
-        out_shape=tuple(jax.ShapeDtypeStruct(shape, query.dtype) for shape in shapes),
-        in_specs=[SMEM, HBM, HBM, HBM],
-        out_specs=(HBM,) * len(plan),
-        scratch_shapes=[pltpu.VMEM(shape, query.dtype) for shape in shapes]
-        + [
-            pltpu.SemaphoreType.DMA((len(plan), 5)),
-            pltpu.SemaphoreType.DMA((len(plan),)),
-        ],
+        functools.partial(
+            pack_body, half=half, rows=rows, width=width, plan=plan, gated=gated
+        ),
+        out_shape=tuple(outs),
+        in_specs=[SMEM] + [HBM] * len(operands),
+        out_specs=tuple(out_specs),
+        scratch_shapes=scratch,
         name="pack",
-    )(place, query, stretch, history)
-
-
-def attention_body(place, bias_ref, *rest, rows, half, heads, low, inner, outer, group, partial):
+    )(place, *operands)
+
+
+def stage_body(_, out):
+    out[...] = jnp.zeros(out.shape, out.dtype)
+
+
+def stage(value):
+    return pl.pallas_call(
+        stage_body,
+        out_shape=jax.ShapeDtypeStruct((8, HD), jnp.float32),
+        in_specs=[VMEM],
+        out_specs=VMEM,
+        compiler_params=pltpu.CompilerParams(vmem_limit_bytes=VMEM_LIMIT),
+        name="stage",
+    )(value)
+
+
+def attention_body(
+    place, bias_ref, *rest, rows, half, heads, low, inner, outer, group, partial, held
+):
     kv_rows = 2 * half + 2 * rows
     refs, rest = rest[:group], rest[group:]
     own = [(ref, 0, low if step < inner else 0) for step, ref in enumerate(refs)]
@@ -127,7 +174,9 @@
     q_all = None
     if partial:
         q_all, rest = rest[0], rest[1:]
+    rest = rest[held:]
     out_ref, stats, q_scr = rest[0], rest[1:-1], rest[-1]
+    singles = () if partial else stats
     for step, (ref, _, base) in enumerate(own):
         member = place[0] ^ step
         for o in range(outer):
@@ -188,10 +237,13 @@
             stats[0][:, h : h + 1] = peak
             stats[1][:, h : h + 1] = total
         else:
-            out_ref[:, cols] = (acc / total).astype(out_ref.dtype)
-
-
-def attention(place, bias, own, others, q_all, rows, half, total_rows, low, cols):
+            result = (acc / total).astype(out_ref.dtype)
+            out_ref[:, cols] = result
+            if singles:
+                singles[h][...] = result
+
+
+def attention(place, bias, own, others, q_all, held, rows, half, total_rows, low, cols):
     group = len(own)
     partial = q_all is not None
     wide = jax.ShapeDtypeStruct((total_rows, cols), jnp.float32 if partial else jnp.bfloat16)
@@ -206,27 +258,31 @@
         outer=total_rows // (group * rows),
         group=group,
         partial=partial,
+        held=len(held),
     )
-    operands = (*own, *others) + ((q_all,) if partial else ())
+    operands = (*own, *others) + ((q_all,) if partial else ()) + held
+    single = jax.ShapeDtypeStruct((total_rows, HD), jnp.bfloat16)
+    heads = cols // HD
+    outs = (wide, thin, thin) if partial else (wide,) + (single,) * (heads if heads > 1 else 0)
     return pl.pallas_call(
         body,
-        out_shape=(wide, thin, thin) if partial else wide,
+        out_shape=outs,
         in_specs=[SMEM] + [VMEM] * (1 + len(operands)),
-        out_specs=(VMEM,) * 3 if partial else VMEM,
+        out_specs=(VMEM,) * len(outs),
         scratch_shapes=[pltpu.VMEM((total_rows, cols), jnp.bfloat16)],
-        compiler_params=pltpu.CompilerParams(vmem_limit_bytes=24 << 20),
+        compiler_params=pltpu.CompilerParams(vmem_limit_bytes=VMEM_LIMIT),
         name="attend",
     )(place, bias, *operands)
 
 
-def project_body(starts, place, weight, *rest, group, low, last, first):
-    parts, rest = rest[:group], rest[group:]
-    cols = parts[0].shape[1]
+def project_body(place, weight, *rest, rows, last, first):
+    count = len(rows)
+    parts, rest = rest[:count], rest[count:]
     left = jnp.concatenate([part[...] for part in parts], axis=1)
     right = jnp.concatenate(
         [
-            weight[pl.ds(pl.multiple_of(starts[step] + low, HD), cols), :]
-            for step in range(group)
+            weight[pl.ds(pl.multiple_of((place[0] ^ step) * width + low, HD), part.shape[1]), :]
+            for part, (step, low, width) in zip(parts, rows)
         ],
         axis=0,
     )
@@ -242,68 +298,67 @@
     out[...] = acc.astype(out.dtype)
 
 
-def project(starts, place, parts, weight, before, gate, low):
-    group = len(parts)
+def project(place, entries, weight, before, gate, width):
+    parts = [part for part, _, _ in entries]
+    rows = tuple((step, low, width) for _, step, low in entries)
     first, last = before is None, gate is not None
     operands = [weight, *parts]
     operands += [] if first else [before]
     operands += [gate] if last else []
     shape = (parts[0].shape[0], weight.shape[1])
     return pl.pallas_call(
+        functools.partial(project_body, rows=rows, last=last, first=first),
+        out_shape=jax.ShapeDtypeStruct(shape, jnp.bfloat16 if last else jnp.float32),
+        in_specs=[SMEM] + [VMEM] * len(operands),
+        out_specs=VMEM,
+        compiler_params=pltpu.CompilerParams(vmem_limit_bytes=VMEM_LIMIT),
+        name="project",
+    )(place, *operands)
+
+
+def bias_body(place, mask, out, *, group, rows, half, history_rows):
+    block_count = out.shape[0]
+    fresh, history = group * rows, group * half
+    member, core, base, live_limit = place[0], place[1], place[3], place[4]
+
+    def positions(count, size, offset):
+        column = lax.broadcasted_iota(jnp.int32, (1, count * group), 1)
+        position = column
+        for step in range(group):
+            start = (base + (member ^ step)) * size + offset - step * count
+            position = jnp.where(column >= step * count, column + start, position)
+        return position
+
+    def put(row, low, allowed):
+        out[row, :, low : low + allowed.shape[1]] = jnp.where(allowed > 0, 0.0, NEGATIVE)
+
+    position = positions(rows, rows, 0)
+    for row in range(block_count):
+        for low, first in ((0, block_count), (fresh, 0)):
+            allowed = jnp.zeros(position.shape, jnp.int32)
+            for block in range(block_count):
+                within = (position >= block * BLK) & (position < (block + 1) * BLK)
+                allowed = jnp.where(within, mask[row, first + block], allowed)
+            put(row, low, allowed)
+    for low, which in ((2 * fresh, core), (2 * fresh + history, 1 - core)):
+        position = positions(half, history_rows, which * half)
+        allowed = jnp.where(position < live_limit, 1, 0)
+        for row in range(block_count):
+            put(row, low, allowed)
+
+
+def key_bias(place, block_mask, group, rows, half, history_rows):
+    keys = 2 * group * (rows + half)
+    return pl.pallas_call(
         functools.partial(
-            project_body, group=group, low=low, last=last, first=first
+            bias_body, group=group, rows=rows, half=half, history_rows=history_rows
         ),
-        out_shape=jax.ShapeDtypeStruct(shape, jnp.bfloat16 if last else jnp.float32),
-        in_specs=[SMEM, SMEM] + [VMEM] * len(operands),
+        out_shape=jax.ShapeDtypeStruct((block_mask.shape[0], 1, keys), jnp.float32),
+        in_specs=[SMEM, SMEM],
         out_specs=VMEM,
-        compiler_params=pltpu.CompilerParams(vmem_limit_bytes=24 << 20),
-        name="project",
-    )(starts, place, *operands)
-
-
-def pick_body(place, table, out, sem):
-    row = pl.multiple_of(place[2] // 8 * 8, 8)
-    copy = pltpu.make_async_copy(table.at[pl.ds(row, 8), :], out, sem)
-    copy.start()
-    copy.wait()
-
-
-def pick_gate(place, table):
-    return pl.pallas_call(
-        pick_body,
-        out_shape=jax.ShapeDtypeStruct((8, table.shape[1]), table.dtype),
-        in_specs=[SMEM, HBM],
-        out_specs=VMEM,
-        scratch_shapes=[pltpu.SemaphoreType.DMA],
-        compiler_params=pltpu.CompilerParams(vmem_limit_bytes=1 << 20),
-        name="pick",
-    )(place, table)
-
-
-def key_bias(block_mask, live_limit, sources, rows, half, history_rows, core):
-    block_count = block_mask.shape[0]
-    fresh = (sources[:, None] * rows + jnp.arange(rows, dtype=jnp.int32)[None, :]).reshape(-1) // BLK
-    hot = fresh[:, None] == jnp.arange(block_count, dtype=jnp.int32)[None, :]
-    mask = block_mask > 0
-
-    def fresh_part(columns):
-        return jnp.any(hot[None, :, :] & columns[:, None, :], axis=2)
-
-    def history_part(which):
-        base = sources[:, None] * history_rows + which * half
-        position = (base + jnp.arange(half, dtype=jnp.int32)[None, :]).reshape(-1)
-        return jnp.broadcast_to((position < live_limit)[None, :], (block_count, position.shape[0]))
-
-    allowed = jnp.concatenate(
-        [
-            fresh_part(mask[:, block_count:]),
-            fresh_part(mask[:, :block_count]),
-            history_part(core),
-            history_part(1 - core),
-        ],
-        axis=1,
-    )
-    return jnp.where(allowed, 0.0, NEGATIVE).astype(jnp.float32)[:, None, :]
+        compiler_params=pltpu.CompilerParams(vmem_limit_bytes=VMEM_LIMIT),
+        name="bias",
+    )(place, block_mask)
 
 
 def on_device(
@@ -322,21 +377,23 @@
     total_rows = tp_count * rows
     member = tp_index % group
     kv_rows = 2 * half + 2 * rows
-    place = jnp.stack([member, core, noise_level[0]]).astype(jnp.int32)
+    place = [member, core, noise_level[0], tp_index - member, history_blocks[0] * BLK]
+    place = jnp.stack(place).astype(jnp.int32)
     same = [[o * group + m for o in range(outer)] for m in range(group)]
     chunks = [(low * HD, count * HD) for low, count in head_chunks(width // HD, CHUNKS)]
 
-    sources = tp_index - member + (member ^ jnp.arange(group, dtype=jnp.int32))
-    bias = key_bias(
-        block_mask[0], history_blocks[0] * BLK, sources, rows, half, history_rows, core
-    )
+    bias = key_bias(place, block_mask[0], group, rows, half, history_rows)
 
     inner = max(group // 2, 1)
     cross = list(range(group - 1, inner - 1, -1))
+    arrays = (query[0], stretch_kv[:, 0], history_kv)
     plan = [(step, low, cols) for low, cols in chunks[:1] for step in cross]
-    plan += [(step, 0, width) for step in range(inner)]
-    plan += [(step, low, cols) for low, cols in chunks[1:] for step in cross]
-    blocks = pack(place, query[0], stretch_kv[:, 0], history_kv, width, plan)
+    blocks = pack(place, *arrays, width, plan) if plan else ()
+    rest = [(step, 0, width) for step in range(inner)]
+    rest += [(step, low, cols) for low, cols in chunks[1:] for step in cross]
+    gate_rows, *others = pack(place, *arrays, width, rest, gate_table)
+    blocks = list(blocks) + others
+    plan += rest
     sends = [{} for _ in chunks]
     near = {}
     for (step, low, cols), block in zip(plan, blocks):
@@ -351,7 +408,8 @@
         jnp.concatenate([near[step][:kv_rows] for step in range(inner)], axis=0)
     )
 
-    gathered = []
+    held = (out_weight, stage(out_weight))
+    groups = [[] for _ in range(len(chunks) + 1)]
     for index, (low, cols) in enumerate(chunks):
         far = sends[index]
         own = [near[step] for step in range(inner)] + [far[step] for step in reversed(cross)]
@@ -368,6 +426,7 @@
             bias,
             own,
             others,
+            held=held,
             rows=rows,
             half=half,
             total_rows=total_rows,
@@ -392,17 +451,21 @@
             outs = outs.reshape(outer, total_rows, -1, HD) * factor[..., None]
             attended = (jnp.sum(outs, axis=0) / total[..., None]).astype(jnp.bfloat16)
             attended = attended.reshape(total_rows, -1)
+            singles = [attended[:, at : at + HD] for at in range(0, cols, HD)]
         else:
-            attended = attend(q_all=None)
-        parts, members = spread(attended, member, group)
-        gathered.append(parts)
-    starts = (jnp.stack(members) * width).astype(jnp.int32)
-
-    gate_rows = pick_gate(place, gate_table)
+            attended, *singles = attend(q_all=None)
+            singles = singles or [attended]
+        close, distant = spread(attended, singles, group)
+        groups[index] += [(value, step, low) for value, step in close]
+        for head, pieces in enumerate(distant):
+            late = min(index + (1 if head < len(distant) - 1 else 2), len(chunks))
+            groups[late] += [(value, step, low + head * HD) for value, step in pieces]
+
+    groups = [entries for entries in groups if entries]
     result = None
-    for index, ((low, _), parts) in enumerate(zip(chunks, gathered)):
-        gate = gate_rows if index == len(chunks) - 1 else None
-        result = project(starts, place, parts, out_weight, result, gate, low)
+    for index, entries in enumerate(groups):
+        gate = gate_rows if index == len(groups) - 1 else None
+        result = project(place, entries, out_weight, result, gate, width)
     return result[None]
 
 

time: 143 us -> 141 us (0.986)
  starting transfers between devices: 48.5 us -> 58.6 us
  waiting for transfers between devices: 65.1 us -> 58.3 us
  local copies, waits for them, and re-layouts: 6.4 us -> 0.86 us
    ppermute x25 -> x29, starting transfers between devices: 47.9 us -> 58.4 us  [xor_permute(): return lax.ppermute(value, 'tp', pairs)]
    ppermute x25 -> x29, waiting for transfers between devices: 63.5 us -> 58.3 us  [xor_permute(): return lax.ppermute(value, 'tp', pairs)]
    unnamed x36 -> x18, local copies, waits for them, and re-layouts: 4.97 us -> 0.04 us
    pallas_call x1 -> x2, Pallas kernels: 3.99 us -> 6.7 us  [pack(): pl.pallas_call(functools.partial(pack_body, half=half, rows=rows, width=w...]
    ppermute x3, waiting for transfers between devices: 1.6 us -> 0.01 us  [partner_core(): return lax.ppermute(value, 'stretch', [(0, 1), (1, 0)])]
    pallas_call x5 -> x7, Pallas kernels: 16 us -> 14.5 us  [the longest x2 8.39 us: attention(): pl.pallas_call(body, out_shape=outs, in_specs=[SMEM] + [VMEM] * (1 + len(...]
  transfers between devices with their start and end apart: 28 -> 32, of which waited for: 11 -> 16; matrix products, arithmetic and copies ran while one was open for 1% -> 0% of each run, Pallas kernels for 9% -> 11%
where the time goes in v3:
time: 141 us
  starting transfers between devices  58.6 us (42%)
  waiting for transfers between devices  58.3 us (41%)
  Pallas kernels  21.2 us (15%)
  between operations  1.64 us (1%)
    ppermute x29, starting transfers between devices, xor_permute(): return lax.ppermute(value, 'tp', pairs)  58.4 us
    ppermute x29, waiting for transfers between devices, xor_permute(): return lax.ppermute(value, 'tp', pairs)  58.3 us
    pallas_call x2, Pallas kernels, attention(): pl.pallas_call(body, out_shape=outs, in_specs=[SMEM] + [VMEM] * (1 + len(...  8.39 us
    pallas_call x2, Pallas kernels, pack(): pl.pallas_call(functools.partial(pack_body, half=half, rows=rows, width=w...  6.7 us
    pallas_call x3, Pallas kernels, project(): pl.pallas_call(functools.partial(project_body, rows=rows, last=last, firs...  5.49 us
  transfers between devices with their start and end apart: 32, of which 16 were waited for; matrix products, arithmetic and copies ran while one was open for 0% of the time, Pallas kernels for 11%

profile of v3, /device:TPU:0, one launch (start us, length us, event | category | flops | bytes accessed | tf_op | source)
XLA Modules:
  0.0 140.9 jit_solution(4202739441838687617)
XLA Ops:
  1.3 0.6 stack.16.place
  1.9 3.9 %pack.2 = (f32[8,768]{1,0:T(8,128)}, bf16[448,384]{1,0:T(8,128)(2,1)}, bf16[448,384]{1,0:T(8,128)(2,1)}, bf16[448,384]{1,0:T(8,128)(2,1)}, bf16[448,384]{1,0:T(8...) custom-call(s32[5]{0:T(128)} %stack.16.place, ...), custom_call_target="tpu_custom_call" | custom-call | tf_op jit(solution)/shard_map/pack/pallas_call | solution.py:136
  5.9 4.1 %collective-permute-start.2 = (bf16[448,384]{1,0:T(8,128)(2,1)}, bf16[448,384]{1,0:T(8,128)(2,1)S(1)}, u32[]{:S(2)}, u32[]{:S(2)}) collective-permute-start(bf16[448,384]{1,0:T(8,128)(2,1)} %get-tuple-element.24), channel_id=1, source_target_pairs={{0,3},{1,2},{2,1},{3,0},{4,7},{5,6},{6,5},{7,4},{8,11},{9,10},{10,... | collective-permute-start | bytes 1032200 | tf_op jit(solution)/shard_map/ppermute | solution.py:42
  9.9 0.4 collective-permute-start.1
  10.4 0.2 collective-permute-start
  10.6 2.8 %pack.3 = (bf16[448,256]{1,0:T(8,128)(2,1)}, bf16[448,256]{1,0:T(8,128)(2,1)}, bf16[448,256]{1,0:T(8,128)(2,1)}, bf16[448,256]{1,0:T(8,128)(2,1)}) custom-call(s32[5]{0:T(128)} %stack.16.place, bf16[64,3072]{1,0:T(8,128)(2,1)} %bitcast.11, bf16[2,64,3072]{2,1,0:T(8,128)(2,1)} %bitcast.9, bf16[2,256,3072]{2,1,0:T(8,128)(2,1)} %rest_2_.1), custom_call_target="tpu_custom_call" | custom-call | tf_op jit(solution)/shard_map/pack/pallas_call | solution.py:136
  13.3 3.0 %collective-permute-start.3 = (bf16[448,256]{1,0:T(8,128)(2,1)}, bf16[448,256]{1,0:T(8,128)(2,1)S(1)}, u32[]{:S(2)}, u32[]{:S(2)}) collective-permute-start(bf16[448,256]{1,0:T(8,128)(2,1)} %get-tuple-element.25), channel_id=1, source_target_pairs={{0,4},{1,5},{2,6},{3,7},{4,0},{5,1},{6,2},{7,3},{8,12},{9,13},{10,... | collective-permute-start | bytes 688136 | tf_op jit(solution)/shard_map/ppermute | solution.py:42
  16.3 1.3 collective-permute-start.4
  17.6 10.4 %collective-permute-done.2.rest_3_ = bf16[448,384]{1,0:T(8,128)(2,1)S(1)} collective-permute-done((bf16[448,384]{1,0:T(8,128)(2,1)}, bf16[448,384]{1,0:T(8,128)(2,1)S(1)}, u32[]{:S(2)}, u32[]{:S(2)}) %collective-permute-start.2) | collective-permute-done | bytes 344096 | tf_op jit(solution)/shard_map/ppermute | solution.py:42
  28.1 3.1 %collective-permute-start.5 = (bf16[448,256]{1,0:T(8,128)(2,1)}, bf16[448,256]{1,0:T(8,128)(2,1)S(1)}, u32[]{:S(2)}, u32[]{:S(2)}) collective-permute-start(bf16[448,256]{1,0:T(8,128)(2,1)} %get-tuple-element.27), channel_id=1, source_target_pairs={{0,6},{1,7},{2,4},{3,5},{4,2},{5,3},{6,0},{7,1},{8,14},{9,15},{10,... | collective-permute-start | bytes 688136 | tf_op jit(solution)/shard_map/ppermute | solution.py:42
  31.2 4.5 %collective-permute-done.1.rest_2_ = bf16[448,384]{1,0:T(8,128)(2,1)S(1)} collective-permute-done((bf16[448,384]{1,0:T(8,128)(2,1)}, bf16[448,384]{1,0:T(8,128)(2,1)S(1)}, u32[]{:S(2)}, u32[]{:S(2)}) %collective-permute-start.1) | collective-permute-done | bytes 344096 | tf_op jit(solution)/shard_map/ppermute | solution.py:42
  35.7 1.7 %collective-permute-start.6 = (bf16[448,256]{1,0:T(8,128)(2,1)}, bf16[448,256]{1,0:T(8,128)(2,1)S(1)}, u32[]{:S(2)}, u32[]{:S(2)}) collective-permute-start(bf16[448,256]{1,0:T(8,128)(2,1)} %get-tuple-element.28), channel_id=1, source_target_pairs={{0,7},{1,6},{2,5},{3,4},{4,3},{5,2},{6,1},{7,0},{8,15},{9,14},{10,... | collective-permute-start | bytes 688136 | tf_op jit(solution)/shard_map/ppermute | solution.py:42
  37.4 0.0 collective-permute-done.rest_1_
  37.5 0.1 pad_maximum_fusion
  37.6 0.1 collective-permute-start.7
  37.7 9.8 %collective-permute-done.6.rest_7_ = bf16[448,256]{1,0:T(8,128)(2,1)S(1)} collective-permute-done((bf16[448,256]{1,0:T(8,128)(2,1)}, bf16[448,256]{1,0:T(8,128)(2,1)S(1)}, u32[]{:S(2)}, u32[]{:S(2)}) %collective-permute-start.6) | collective-permute-done | bytes 229408 | tf_op jit(solution)/shard_map/ppermute | solution.py:42
  47.5 0.0 collective-permute-done.5.rest_6_
  47.6 1.3 collective-permute-done.4.rest_5_
  48.9 0.0 copy-start.4
  48.9 0.1 pad_maximum_fusion.1
  49.0 0.1 collective-permute-start.8
  49.1 2.3 %collective-permute-start.16 = (bf16[448,128]{1,0:T(8,128)(2,1)S(1)}, bf16[448,128]{1,0:T(8,128)(2,1)S(1)}, u32[]{:S(2)}, u32[]{:S(2)}) collective-permute-start(bf16[448,128]{1,0:T(8,128)(2,1)S(1)} %copy-done.8), channel_id=1, source_target_pairs={{0,7},{1,6},{2,5},{3,4},{4,3},{5,2},{6,1},{7,0},{8,15},{9,14},{10,... | collective-permute-start | bytes 344072 | tf_op jit(solution)/shard_map/ppermute | solution.py:42
  51.4 1.4 %collective-permute-start.15 = (bf16[448,128]{1,0:T(8,128)(2,1)S(1)}, bf16[448,128]{1,0:T(8,128)(2,1)S(1)}, u32[]{:S(2)}, u32[]{:S(2)}) collective-permute-start(bf16[448,128]{1,0:T(8,128)(2,1)S(1)} %copy-done.7), channel_id=1, source_target_pairs={{0,6},{1,7},{2,4},{3,5},{4,2},{5,3},{6,0},{7,1},{8,14},{9,15},{10,... | collective-permute-start | bytes 344072 | tf_op jit(solution)/shard_map/ppermute | solution.py:42
  52.8 14.8 %collective-permute-start.14 = (bf16[448,128]{1,0:T(8,128)(2,1)S(1)}, bf16[448,128]{1,0:T(8,128)(2,1)S(1)}, u32[]{:S(2)}, u32[]{:S(2)}) collective-permute-start(bf16[448,128]{1,0:T(8,128)(2,1)S(1)} %copy-done.6), channel_id=1, source_target_pairs={{0,5},{1,4},{2,7},{3,6},{4,1},{5,0},{6,3},{7,2},{8,13},{9,12},{10,... | collective-permute-start | bytes 344072 | tf_op jit(solution)/shard_map/ppermute | solution.py:42
  67.7 6.4 %collective-permute-start.13 = (bf16[448,128]{1,0:T(8,128)(2,1)S(1)}, bf16[448,128]{1,0:T(8,128)(2,1)S(1)}, u32[]{:S(2)}, u32[]{:S(2)}) collective-permute-start(bf16[448,128]{1,0:T(8,128)(2,1)S(1)} %copy-done.5), channel_id=1, source_target_pairs={{0,4},{1,5},{2,6},{3,7},{4,0},{5,1},{6,2},{7,3},{8,12},{9,13},{10,... | collective-permute-start | bytes 344072 | tf_op jit(solution)/shard_map/ppermute | solution.py:42
  74.1 3.7 %collective-permute-done.14.rest_5_ = bf16[448,128]{1,0:T(8,128)(2,1)S(1)} collective-permute-done((bf16[448,128]{1,0:T(8,128)(2,1)S(1)}, bf16[448,128]{1,0:T(8,128)(2,1)S(1)}, u32[]{:S(2)}, u32[]{:S(2)}) %collective-permute-start.14) | collective-permute-done | bytes 114720 | tf_op jit(solution)/shard_map/ppermute | solution.py:42
  77.8 3.4 %collective-permute-done.13.rest_4_ = bf16[448,128]{1,0:T(8,128)(2,1)S(1)} collective-permute-done((bf16[448,128]{1,0:T(8,128)(2,1)S(1)}, bf16[448,128]{1,0:T(8,128)(2,1)S(1)}, u32[]{:S(2)}, u32[]{:S(2)}) %collective-permute-start.13) | collective-permute-done | bytes 114720 | tf_op jit(solution)/shard_map/ppermute | solution.py:42
  81.3 0.1 collective-permute-start.17
  81.4 0.6 bias.1.bias_ref
  82.1 0.0 collective-permute-done.8.rest_9_
  82.1 5.4 %attend.2 = (bf16[512,256]{1,0:T(8,128)(2,1)S(1)}, bf16[512,128]{1,0:T(8,128)(2,1)S(1)}, bf16[512,128]{1,0:T(8,128)(2,1)S(1)}) custom-call(s32[5]{0:T(128)S(1)} %copy-done.2, f32[4,1,3072]{2,1,0:T(1,128)S(1)} %bias.1.bias_ref, bf16[448,384]{1,0:T(8,128)(2,1)S(1)} %copy-done.1, bf16[448,384]{1,0:T(8,128)(2,1)S(1)} %collective-permute-done.rest_1_, ...), custom_call_target="tpu_custom_call" | custom-call | tf_op jit(solution)/shard_map/attend/pallas_call | solution.py:267
  87.4 0.1 collective-permute-start.30
  87.5 2.6 %collective-permute-start.9 = (bf16[512,128]{1,0:T(8,128)(2,1)S(1)}, bf16[512,128]{1,0:T(8,128)(2,1)S(1)}, u32[]{:S(2)}, u32[]{:S(2)}) collective-permute-start(bf16[512,128]{1,0:T(8,128)(2,1)S(1)} %get-tuple-element.29), channel_id=1, source_target_pairs={{0,4},{1,5},{2,6},{3,7},{4,0},{5,1},{6,2},{7,3},{8,12},{9,13},{10,... | collective-permute-start | bytes 393224 | tf_op jit(solution)/shard_map/ppermute | solution.py:42
  90.2 0.0 collective-permute-done.17.rest_9_
  90.2 3.0 %attend.3.rest_4_ = bf16[512,128]{1,0:T(8,128)(2,1)S(1)} custom-call(s32[5]{0:T(128)S(1)} %copy-done.2, f32[4,1,3072]{2,1,0:T(1,128)S(1)} %bias.1.bias_ref, bf16[448,384]{1,0:T(8,128)(2,1)S(1)} %copy-done.1, bf16[448,384]{1,0:T(8,128)(2,1)S(1)} %collective-permute-done.rest_1_, bf16[448,384]{1,0:T(8,128)(2,1)S(1)} %collective-permute-done.1.rest_2_, ...), custom_call_target="tpu_custom_call" | custom-call | tf_op jit(solution)/shard_map/attend/pallas_call | solution.py:267
  93.2 0.4 collective-permute-start.18
  93.6 1.3 collective-permute-start.29
  94.9 2.8 %collective-permute-start.22 = (bf16[512,128]{1,0:T(8,128)(2,1)S(1)}, bf16[512,128]{1,0:T(8,128)(2,1)S(1)}, u32[]{:S(2)}, u32[]{:S(2)}) collective-permute-start(bf16[512,128]{1,0:T(8,128)(2,1)S(1)} %get-tuple-element.34), channel_id=1, source_target_pairs={{0,4},{1,5},{2,6},{3,7},{4,0},{5,1},{6,2},{7,3},{8,12},{9,13},{10,... | collective-permute-start | bytes 393224 | tf_op jit(solution)/shard_map/ppermute | solution.py:42
  97.7 0.5 collective-permute-start.26
  98.2 9.6 %collective-permute-done.18.rest_4_ = bf16[512,128]{1,0:T(8,128)(2,1)S(1)} collective-permute-done((bf16[512,128]{1,0:T(8,128)(2,1)S(1)}, bf16[512,128]{1,0:T(8,128)(2,1)S(1)}, u32[]{:S(2)}, u32[]{:S(2)}) %collective-permute-start.18) | collective-permute-done | bytes 131104 | tf_op jit(solution)/shard_map/ppermute | solution.py:42
  107.9 2.7 %collective-permute-done.22.rest_0_ = bf16[512,128]{1,0:T(8,128)(2,1)S(1)} collective-permute-done((bf16[512,128]{1,0:T(8,128)(2,1)S(1)}, bf16[512,128]{1,0:T(8,128)(2,1)S(1)}, u32[]{:S(2)}, u32[]{:S(2)}) %collective-permute-start.22) | collective-permute-done | bytes 131104 | tf_op jit(solution)/shard_map/ppermute | solution.py:42
  110.6 0.0 collective-permute-start.11
  110.6 0.0 collective-permute-done.30.rest_2_
  110.6 1.5 %collective-permute-start.31 = (bf16[512,256]{1,0:T(8,128)(2,1)S(1)}, bf16[512,256]{1,0:T(8,128)(2,1)S(1)}, u32[]{:S(2)}, u32[]{:S(2)}) collective-permute-start(bf16[512,256]{1,0:T(8,128)(2,1)S(1)} %collective-permute-done.30.rest_2_), channel_id=1, source_target_pairs={{0,1},{1,0},{2,3},{3,2},{4,5},{5,4},{6,7},{7,6},{8,9},{9,8},{10,11... | collective-permute-start | bytes 786440 | tf_op jit(solution)/shard_map/ppermute | solution.py:42
  112.1 2.0 %collective-permute-start.20 = (bf16[512,128]{1,0:T(8,128)(2,1)S(1)}, bf16[512,128]{1,0:T(8,128)(2,1)S(1)}, u32[]{:S(2)}, u32[]{:S(2)}) collective-permute-start(bf16[512,128]{1,0:T(8,128)(2,1)S(1)} %collective-permute-done.18.rest_4_), channel_id=1, source_target_pairs={{0,2},{1,3},{2,0},{3,1},{4,6},{5,7},{6,4},{7,5},{8,10},{9,11},{10,... | collective-permute-start | bytes 393224 | tf_op jit(solution)/shard_map/ppermute | solution.py:42
  114.1 0.1 collective-permute-start.24
  114.2 0.9 collective-permute-start.23
  115.1 1.8 %collective-permute-done.11.rest_2_ = bf16[512,128]{1,0:T(8,128)(2,1)S(1)} collective-permute-done((bf16[512,128]{1,0:T(8,128)(2,1)S(1)}, bf16[512,128]{1,0:T(8,128)(2,1)S(1)}, u32[]{:S(2)}, u32[]{:S(2)}) %collective-permute-start.11) | collective-permute-done | bytes 131104 | tf_op jit(solution)/shard_map/ppermute | solution.py:42
  117.0 1.5 %collective-permute-start.28 = (bf16[512,128]{1,0:T(8,128)(2,1)S(1)}, bf16[512,128]{1,0:T(8,128)(2,1)S(1)}, u32[]{:S(2)}, u32[]{:S(2)}) collective-permute-start(bf16[512,128]{1,0:T(8,128)(2,1)S(1)} %collective-permute-done.27.rest_6_), channel_id=1, source_target_pairs={{0,1},{1,0},{2,3},{3,2},{4,5},{5,4},{6,7},{7,6},{8,9},{9,8},{10,11... | collective-permute-start | bytes 393224 | tf_op jit(solution)/shard_map/ppermute | solution.py:42
  118.5 1.3 collective-permute-done.20.rest_6_
  119.8 1.5 %collective-permute-start.10 = (bf16[512,128]{1,0:T(8,128)(2,1)S(1)}, bf16[512,128]{1,0:T(8,128)(2,1)S(1)}, u32[]{:S(2)}, u32[]{:S(2)}) collective-permute-start(bf16[512,128]{1,0:T(8,128)(2,1)S(1)} %collective-permute-done.9.rest_0_), channel_id=1, source_target_pairs={{0,1},{1,0},{2,3},{3,2},{4,5},{5,4},{6,7},{7,6},{8,9},{9,8},{10,11... | collective-permute-start | bytes 393224 | tf_op jit(solution)/shard_map/ppermute | solution.py:42
  121.3 0.5 collective-permute-done.24.rest_2_
  121.8 1.5 %collective-permute-start.25 = (bf16[512,128]{1,0:T(8,128)(2,1)S(1)}, bf16[512,128]{1,0:T(8,128)(2,1)S(1)}, u32[]{:S(2)}, u32[]{:S(2)}) collective-permute-start(bf16[512,128]{1,0:T(8,128)(2,1)S(1)} %collective-permute-done.24.rest_2_), channel_id=1, source_target_pairs={{0,1},{1,0},{2,3},{3,2},{4,5},{5,4},{6,7},{7,6},{8,9},{9,8},{10,11... | collective-permute-start | bytes 393224 | tf_op jit(solution)/shard_map/ppermute | solution.py:42
  123.3 0.8 collective-permute-start.19
  124.1 1.3 collective-permute-done.28.rest_7_
  125.4 1.5 %collective-permute-start.12 = (bf16[512,128]{1,0:T(8,128)(2,1)S(1)}, bf16[512,128]{1,0:T(8,128)(2,1)S(1)}, u32[]{:S(2)}, u32[]{:S(2)}) collective-permute-start(bf16[512,128]{1,0:T(8,128)(2,1)S(1)} %collective-permute-done.11.rest_2_), channel_id=1, source_target_pairs={{0,1},{1,0},{2,3},{3,2},{4,5},{5,4},{6,7},{7,6},{8,9},{9,8},{10,11... | collective-permute-start | bytes 393224 | tf_op jit(solution)/shard_map/ppermute | solution.py:42
  126.9 0.5 collective-permute-start.21
  127.4 1.5 %project.3.rest_8_ = f32[512,768]{1,0:T(8,128)S(1)} custom-call(s32[5]{0:T(128)S(1)} %copy-done.2, bf16[3072,768]{1,0:T(8,128)(2,1)S(1)} %copy-done, bf16[512,256]{1,0:T(8,128)(2,1)S(1)} %get-tuple-element.35.rest_0_, bf16[512,256]{1,0:T(8,128)(2,1)S(1)} %collective-permute-done.29.rest_1_, bf16[512,256]{1,0:T(8,128)(2,1)S(1)} %collective-permute-done.30.rest_2_, ...), custom_call_target="tpu_custom_call" | custom-call | tf_op jit(solution)/shard_map/project/pallas_call | solution.py:309
  129.0 2.0 %collective-permute-done.25.rest_3_ = bf16[512,128]{1,0:T(8,128)(2,1)S(1)} collective-permute-done((bf16[512,128]{1,0:T(8,128)(2,1)S(1)}, bf16[512,128]{1,0:T(8,128)(2,1)S(1)}, u32[]{:S(2)}, u32[]{:S(2)}) %collective-permute-start.25) | collective-permute-done | bytes 131104 | tf_op jit(solution)/shard_map/ppermute | solution.py:42
  131.0 1.5 %project.4.rest_8_ = f32[512,768]{1,0:T(8,128)S(1)} custom-call(s32[5]{0:T(128)S(1)} %copy-done.2, bf16[3072,768]{1,0:T(8,128)(2,1)S(1)} %copy-done, bf16[512,128]{1,0:T(8,128)(2,1)S(1)} %collective-permute-done.22.rest_0_, bf16[512,128]{1,0:T(8,128)(2,1)S(1)} %collective-permute-done.23.rest_1_, bf16[512,128]{1,0:T(8,128)(2,1)S(1)} %collective-permute-done.24.rest_2_, ...), custom_call_target="tpu_custom_call" | custom-call | tf_op jit(solution)/shard_map/project/pallas_call | solution.py:309
  132.6 1.2 collective-permute-done.19.rest_5_
  133.8 2.8 %collective-permute-done.12.rest_3_ = bf16[512,128]{1,0:T(8,128)(2,1)S(1)} collective-permute-done((bf16[512,128]{1,0:T(8,128)(2,1)S(1)}, bf16[512,128]{1,0:T(8,128)(2,1)S(1)}, u32[]{:S(2)}, u32[]{:S(2)}) %collective-permute-start.12) | collective-permute-done | bytes 131104 | tf_op jit(solution)/shard_map/ppermute | solution.py:42
  136.6 1.8 %collective-permute-done.21.rest_7_ = bf16[512,128]{1,0:T(8,128)(2,1)S(1)} collective-permute-done((bf16[512,128]{1,0:T(8,128)(2,1)S(1)}, bf16[512,128]{1,0:T(8,128)(2,1)S(1)}, u32[]{:S(2)}, u32[]{:S(2)}) %collective-permute-start.21) | collective-permute-done | bytes 131104 | tf_op jit(solution)/shard_map/ppermute | solution.py:42
  138.4 2.4 %project.5 = bf16[512,768]{1,0:T(8,128)(2,1)} custom-call(s32[5]{0:T(128)S(1)} %copy-done.2, bf16[3072,768]{1,0:T(8,128)(2,1)S(1)} %copy-done, bf16[512,128]{1,0:T(8,128)(2,1)S(1)} %collective-permute-done.9.rest_0_, bf16[512,128]{1,0:T(8,128)(2,1)S(1)} %collective-permute-done.10.rest_1_, bf16[512,128]{1,0:T(8,128)(2,1)S(1)} %collective-permute-done.11.rest_2_, ...), custom_call_target="tpu_custom_call" | custom-call | tf_op jit(solution)/shard_map/project/pallas_call | solution.py:309
  (43 shorter events, 0.3 us)
Async XLA Ops:
  5.9 22.2 %collective-permute-start.2 = (bf16[448,384]{1,0:T(8,128)(2,1)}, bf16[448,384]{1,0:T(8,128)(2,1)S(1)}, u32[]{:S(2)}, u32[]{:S(2)}) collective-permute-start(bf16[448,384]{1,0:T(8,128)(2,1)} %get-tuple-element.24), channel_id=1, source_target_pairs={{0,3},{1,2},{2,1},{3,0},{4,7},{5,6},{6,5},{7,4},{8,11},{9,10},{10,... | collective-permute-start | bytes 1032200 | tf_op jit(solution)/shard_map/ppermute | solution.py:42
  9.9 25.7 %collective-permute-start.1 = (bf16[448,384]{1,0:T(8,128)(2,1)}, bf16[448,384]{1,0:T(8,128)(2,1)S(1)}, u32[]{:S(2)}, u32[]{:S(2)}) collective-permute-start(bf16[448,384]{1,0:T(8,128)(2,1)} %get-tuple-element.23), channel_id=1, source_target_pairs={{0,2},{1,3},{2,0},{3,1},{4,6},{5,7},{6,4},{7,5},{8,10},{9,11},{10,... | collective-permute-start | bytes 1032200 | tf_op jit(solution)/shard_map/ppermute | solution.py:42
  10.4 7.2 %copy-start.1 = (bf16[448,384]{1,0:T(8,128)(2,1)S(1)}, bf16[448,384]{1,0:T(8,128)(2,1)}, u32[]{:S(2)}) copy-start(bf16[448,384]{1,0:T(8,128)(2,1)} %get-tuple-element.21.rest_0_) | copy-start | bytes 1032196
  10.4 27.0 %collective-permute-start = (bf16[448,384]{1,0:T(8,128)(2,1)}, bf16[448,384]{1,0:T(8,128)(2,1)S(1)}, u32[]{:S(2)}, u32[]{:S(2)}) collective-permute-start(bf16[448,384]{1,0:T(8,128)(2,1)} %get-tuple-element.22), channel_id=1, source_target_pairs={{0,1},{1,0},{2,3},{3,2},{4,5},{5,4},{6,7},{7,6},{8,9},{9,8},{10,11... | collective-permute-start | bytes 1032200 | tf_op jit(solution)/shard_map/ppermute | solution.py:42
  13.3 35.5 %collective-permute-start.3 = (bf16[448,256]{1,0:T(8,128)(2,1)}, bf16[448,256]{1,0:T(8,128)(2,1)S(1)}, u32[]{:S(2)}, u32[]{:S(2)}) collective-permute-start(bf16[448,256]{1,0:T(8,128)(2,1)} %get-tuple-element.25), channel_id=1, source_target_pairs={{0,4},{1,5},{2,6},{3,7},{4,0},{5,1},{6,2},{7,3},{8,12},{9,13},{10,... | collective-permute-start | bytes 688136 | tf_op jit(solution)/shard_map/ppermute | solution.py:42
  16.3 32.5 %collective-permute-start.4 = (bf16[448,256]{1,0:T(8,128)(2,1)}, bf16[448,256]{1,0:T(8,128)(2,1)S(1)}, u32[]{:S(2)}, u32[]{:S(2)}) collective-permute-start(bf16[448,256]{1,0:T(8,128)(2,1)} %get-tuple-element.26), channel_id=1, source_target_pairs={{0,5},{1,4},{2,7},{3,6},{4,1},{5,0},{6,3},{7,2},{8,13},{9,12},{10,... | collective-permute-start | bytes 688136 | tf_op jit(solution)/shard_map/ppermute | solution.py:42
  28.1 19.5 %collective-permute-start.5 = (bf16[448,256]{1,0:T(8,128)(2,1)}, bf16[448,256]{1,0:T(8,128)(2,1)S(1)}, u32[]{:S(2)}, u32[]{:S(2)}) collective-permute-start(bf16[448,256]{1,0:T(8,128)(2,1)} %get-tuple-element.27), channel_id=1, source_target_pairs={{0,6},{1,7},{2,4},{3,5},{4,2},{5,3},{6,0},{7,1},{8,14},{9,15},{10,... | collective-permute-start | bytes 688136 | tf_op jit(solution)/shard_map/ppermute | solution.py:42
  35.7 11.9 %collective-permute-start.6 = (bf16[448,256]{1,0:T(8,128)(2,1)}, bf16[448,256]{1,0:T(8,128)(2,1)S(1)}, u32[]{:S(2)}, u32[]{:S(2)}) collective-permute-start(bf16[448,256]{1,0:T(8,128)(2,1)} %get-tuple-element.28), channel_id=1, source_target_pairs={{0,7},{1,6},{2,5},{3,4},{4,3},{5,2},{6,1},{7,0},{8,15},{9,14},{10,... | collective-permute-start | bytes 688136 | tf_op jit(solution)/shard_map/ppermute | solution.py:42
  37.5 11.6 %copy-start.8 = (bf16[448,128]{1,0:T(8,128)(2,1)S(1)}, bf16[448,128]{1,0:T(8,128)(2,1)}, u32[]{:S(2)}) copy-start(bf16[448,128]{1,0:T(8,128)(2,1)} %get-tuple-element.33) | copy-start | bytes 344068
  37.5 13.9 %copy-start.7 = (bf16[448,128]{1,0:T(8,128)(2,1)S(1)}, bf16[448,128]{1,0:T(8,128)(2,1)}, u32[]{:S(2)}) copy-start(bf16[448,128]{1,0:T(8,128)(2,1)} %get-tuple-element.32) | copy-start | bytes 344068
  37.5 15.4 %copy-start.6 = (bf16[448,128]{1,0:T(8,128)(2,1)S(1)}, bf16[448,128]{1,0:T(8,128)(2,1)}, u32[]{:S(2)}) copy-start(bf16[448,128]{1,0:T(8,128)(2,1)} %get-tuple-element.31) | copy-start | bytes 344068
  37.5 30.2 %copy-start.5 = (bf16[448,128]{1,0:T(8,128)(2,1)S(1)}, bf16[448,128]{1,0:T(8,128)(2,1)}, u32[]{:S(2)}) copy-start(bf16[448,128]{1,0:T(8,128)(2,1)} %get-tuple-element.30) | copy-start | bytes 344068
  37.6 44.4 %collective-permute-start.7 = (bf16[1536,384]{1,0:T(8,128)(2,1)S(1)}, bf16[1536,384]{1,0:T(8,128)(2,1)S(1)}, u32[]{:S(2)}, u32[]{:S(2)}) collective-permute-start(bf16[1536,384]{1,0:T(8,128)(2,1)S(1)} %pad_maximum_fusion), channel_id=1, source_target_pairs={{0,8},{8,0},{1,9},{9,1},{2,10},{10,2},{3,11},{11,3},{4,12},{12,4},... | collective-permute-start | bytes 3538952 | tf_op jit(solution)/shard_map/ppermute | solution.py:73
  47.5 34.5 %copy-start = (bf16[3072,768]{1,0:T(8,128)(2,1)S(1)}, bf16[3072,768]{1,0:T(8,128)(2,1)}, u32[]{:S(2)}) copy-start(bf16[3072,768]{1,0:T(8,128)(2,1)} %weight.5) | copy-start | bytes 14155780
  48.9 32.5 %copy-start.2 = (s32[5]{0:T(128)S(1)}, s32[5]{0:T(128)}, u32[]{:S(2)}) copy-start(s32[5]{0:T(128)} %stack.16.place) | copy-start | bytes 64
  48.9 32.5 %copy-start.4 = (s32[1,4,8]{2,1,0:T(4,128)S(1)}, s32[1,4,8]{2,1,0:T(4,128)}, u32[]{:S(2)}) copy-start(s32[1,4,8]{2,1,0:T(4,128)} %param.11) | copy-start | bytes 388
  49.0 33.1 %collective-permute-start.8 = (bf16[1536,256]{1,0:T(8,128)(2,1)S(1)}, bf16[1536,256]{1,0:T(8,128)(2,1)S(1)}, u32[]{:S(2)}, u32[]{:S(2)}) collective-permute-start(bf16[1536,256]{1,0:T(8,128)(2,1)S(1)} %pad_maximum_fusion.1), channel_id=1, source_target_pairs={{0,8},{8,0},{1,9},{9,1},{2,10},{10,2},{3,11},{11,3},{4,12},{12,4},... | collective-permute-start | bytes 2359304 | tf_op jit(solution)/shard_map/ppermute | solution.py:73
  49.1 18.6 %collective-permute-start.16 = (bf16[448,128]{1,0:T(8,128)(2,1)S(1)}, bf16[448,128]{1,0:T(8,128)(2,1)S(1)}, u32[]{:S(2)}, u32[]{:S(2)}) collective-permute-start(bf16[448,128]{1,0:T(8,128)(2,1)S(1)} %copy-done.8), channel_id=1, source_target_pairs={{0,7},{1,6},{2,5},{3,4},{4,3},{5,2},{6,1},{7,0},{8,15},{9,14},{10,... | collective-permute-start | bytes 344072 | tf_op jit(solution)/shard_map/ppermute | solution.py:42
  51.4 22.7 %collective-permute-start.15 = (bf16[448,128]{1,0:T(8,128)(2,1)S(1)}, bf16[448,128]{1,0:T(8,128)(2,1)S(1)}, u32[]{:S(2)}, u32[]{:S(2)}) collective-permute-start(bf16[448,128]{1,0:T(8,128)(2,1)S(1)} %copy-done.7), channel_id=1, source_target_pairs={{0,6},{1,7},{2,4},{3,5},{4,2},{5,3},{6,0},{7,1},{8,14},{9,15},{10,... | collective-permute-start | bytes 344072 | tf_op jit(solution)/shard_map/ppermute | solution.py:42
  52.8 25.0 %collective-permute-start.14 = (bf16[448,128]{1,0:T(8,128)(2,1)S(1)}, bf16[448,128]{1,0:T(8,128)(2,1)S(1)}, u32[]{:S(2)}, u32[]{:S(2)}) collective-permute-start(bf16[448,128]{1,0:T(8,128)(2,1)S(1)} %copy-done.6), channel_id=1, source_target_pairs={{0,5},{1,4},{2,7},{3,6},{4,1},{5,0},{6,3},{7,2},{8,13},{9,12},{10,... | collective-permute-start | bytes 344072 | tf_op jit(solution)/shard_map/ppermute | solution.py:42
  67.7 13.6 %collective-permute-start.13 = (bf16[448,128]{1,0:T(8,128)(2,1)S(1)}, bf16[448,128]{1,0:T(8,128)(2,1)S(1)}, u32[]{:S(2)}, u32[]{:S(2)}) collective-permute-start(bf16[448,128]{1,0:T(8,128)(2,1)S(1)} %copy-done.5), channel_id=1, source_target_pairs={{0,4},{1,5},{2,6},{3,7},{4,0},{5,1},{6,2},{7,3},{8,12},{9,13},{10,... | collective-permute-start | bytes 344072 | tf_op jit(solution)/shard_map/ppermute | solution.py:42
  81.3 8.9 %collective-permute-start.17 = (bf16[1536,128]{1,0:T(8,128)(2,1)S(1)}, bf16[1536,128]{1,0:T(8,128)(2,1)S(1)}, u32[]{:S(2)}, u32[]{:S(2)}) collective-permute-start(bf16[1536,128]{1,0:T(8,128)(2,1)S(1)} %pad_maximum_fusion.2), channel_id=1, source_target_pairs={{0,8},{8,0},{1,9},{9,1},{2,10},{10,2},{3,11},{11,3},{4,12},{12,4},... | collective-permute-start | bytes 1179656 | tf_op jit(solution)/shard_map/ppermute | solution.py:73
  87.4 23.1 %collective-permute-start.30 = (bf16[512,256]{1,0:T(8,128)(2,1)S(1)}, bf16[512,256]{1,0:T(8,128)(2,1)S(1)}, u32[]{:S(2)}, u32[]{:S(2)}) collective-permute-start(bf16[512,256]{1,0:T(8,128)(2,1)S(1)} %get-tuple-element.35.rest_0_), channel_id=1, source_target_pairs={{0,2},{1,3},{2,0},{3,1},{4,6},{5,7},{6,4},{7,5},{8,10},{9,11},{10,... | collective-permute-start | bytes 786440 | tf_op jit(solution)/shard_map/ppermute | solution.py:42
  87.5 10.2 %collective-permute-start.9 = (bf16[512,128]{1,0:T(8,128)(2,1)S(1)}, bf16[512,128]{1,0:T(8,128)(2,1)S(1)}, u32[]{:S(2)}, u32[]{:S(2)}) collective-permute-start(bf16[512,128]{1,0:T(8,128)(2,1)S(1)} %get-tuple-element.29), channel_id=1, source_target_pairs={{0,4},{1,5},{2,6},{3,7},{4,0},{5,1},{6,2},{7,3},{8,12},{9,13},{10,... | collective-permute-start | bytes 393224 | tf_op jit(solution)/shard_map/ppermute | solution.py:42
  93.2 14.7 %collective-permute-start.18 = (bf16[512,128]{1,0:T(8,128)(2,1)S(1)}, bf16[512,128]{1,0:T(8,128)(2,1)S(1)}, u32[]{:S(2)}, u32[]{:S(2)}) collective-permute-start(bf16[512,128]{1,0:T(8,128)(2,1)S(1)} %attend.3.rest_4_), channel_id=1, source_target_pairs={{0,4},{1,5},{2,6},{3,7},{4,0},{5,1},{6,2},{7,3},{8,12},{9,13},{10,... | collective-permute-start | bytes 393224 | tf_op jit(solution)/shard_map/ppermute | solution.py:42
  93.6 20.6 %collective-permute-start.29 = (bf16[512,256]{1,0:T(8,128)(2,1)S(1)}, bf16[512,256]{1,0:T(8,128)(2,1)S(1)}, u32[]{:S(2)}, u32[]{:S(2)}) collective-permute-start(bf16[512,256]{1,0:T(8,128)(2,1)S(1)} %get-tuple-element.35.rest_0_), channel_id=1, source_target_pairs={{0,1},{1,0},{2,3},{3,2},{4,5},{5,4},{6,7},{7,6},{8,9},{9,8},{10,11... | collective-permute-start | bytes 786440 | tf_op jit(solution)/shard_map/ppermute | solution.py:42
  94.9 15.7 %collective-permute-start.22 = (bf16[512,128]{1,0:T(8,128)(2,1)S(1)}, bf16[512,128]{1,0:T(8,128)(2,1)S(1)}, u32[]{:S(2)}, u32[]{:S(2)}) collective-permute-start(bf16[512,128]{1,0:T(8,128)(2,1)S(1)} %get-tuple-element.34), channel_id=1, source_target_pairs={{0,4},{1,5},{2,6},{3,7},{4,0},{5,1},{6,2},{7,3},{8,12},{9,13},{10,... | collective-permute-start | bytes 393224 | tf_op jit(solution)/shard_map/ppermute | solution.py:42
  97.7 14.4 %collective-permute-start.26 = (bf16[512,128]{1,0:T(8,128)(2,1)S(1)}, bf16[512,128]{1,0:T(8,128)(2,1)S(1)}, u32[]{:S(2)}, u32[]{:S(2)}) collective-permute-start(bf16[512,128]{1,0:T(8,128)(2,1)S(1)} %attend.3.rest_4_), channel_id=1, source_target_pairs={{0,1},{1,0},{2,3},{3,2},{4,5},{5,4},{6,7},{7,6},{8,9},{9,8},{10,11... | collective-permute-start | bytes 393224 | tf_op jit(solution)/shard_map/ppermute | solution.py:42
  107.9 6.3 %collective-permute-start.27 = (bf16[512,128]{1,0:T(8,128)(2,1)S(1)}, bf16[512,128]{1,0:T(8,128)(2,1)S(1)}, u32[]{:S(2)}, u32[]{:S(2)}) collective-permute-start(bf16[512,128]{1,0:T(8,128)(2,1)S(1)} %attend.3.rest_4_), channel_id=1, source_target_pairs={{0,2},{1,3},{2,0},{3,1},{4,6},{5,7},{6,4},{7,5},{8,10},{9,11},{10,... | collective-permute-start | bytes 393224 | tf_op jit(solution)/shard_map/ppermute | solution.py:42
  110.6 6.4 %collective-permute-start.11 = (bf16[512,128]{1,0:T(8,128)(2,1)S(1)}, bf16[512,128]{1,0:T(8,128)(2,1)S(1)}, u32[]{:S(2)}, u32[]{:S(2)}) collective-permute-start(bf16[512,128]{1,0:T(8,128)(2,1)S(1)} %collective-permute-done.9.rest_0_), channel_id=1, source_target_pairs={{0,2},{1,3},{2,0},{3,1},{4,6},{5,7},{6,4},{7,5},{8,10},{9,11},{10,... | collective-permute-start | bytes 393224 | tf_op jit(solution)/shard_map/ppermute | solution.py:42
  110.6 16.3 %collective-permute-start.31 = (bf16[512,256]{1,0:T(8,128)(2,1)S(1)}, bf16[512,256]{1,0:T(8,128)(2,1)S(1)}, u32[]{:S(2)}, u32[]{:S(2)}) collective-permute-start(bf16[512,256]{1,0:T(8,128)(2,1)S(1)} %collective-permute-done.30.rest_2_), channel_id=1, source_target_pairs={{0,1},{1,0},{2,3},{3,2},{4,5},{5,4},{6,7},{7,6},{8,9},{9,8},{10,11... | collective-permute-start | bytes 786440 | tf_op jit(solution)/shard_map/ppermute | solution.py:42
  112.1 7.6 %collective-permute-start.20 = (bf16[512,128]{1,0:T(8,128)(2,1)S(1)}, bf16[512,128]{1,0:T(8,128)(2,1)S(1)}, u32[]{:S(2)}, u32[]{:S(2)}) collective-permute-start(bf16[512,128]{1,0:T(8,128)(2,1)S(1)} %collective-permute-done.18.rest_4_), channel_id=1, source_target_pairs={{0,2},{1,3},{2,0},{3,1},{4,6},{5,7},{6,4},{7,5},{8,10},{9,11},{10,... | collective-permute-start | bytes 393224 | tf_op jit(solution)/shard_map/ppermute | solution.py:42
  114.1 7.7 %collective-permute-start.24 = (bf16[512,128]{1,0:T(8,128)(2,1)S(1)}, bf16[512,128]{1,0:T(8,128)(2,1)S(1)}, u32[]{:S(2)}, u32[]{:S(2)}) collective-permute-start(bf16[512,128]{1,0:T(8,128)(2,1)S(1)} %collective-permute-done.22.rest_0_), channel_id=1, source_target_pairs={{0,2},{1,3},{2,0},{3,1},{4,6},{5,7},{6,4},{7,5},{8,10},{9,11},{10,... | collective-permute-start | bytes 393224 | tf_op jit(solution)/shard_map/ppermute | solution.py:42
  114.2 9.1 %collective-permute-start.23 = (bf16[512,128]{1,0:T(8,128)(2,1)S(1)}, bf16[512,128]{1,0:T(8,128)(2,1)S(1)}, u32[]{:S(2)}, u32[]{:S(2)}) collective-permute-start(bf16[512,128]{1,0:T(8,128)(2,1)S(1)} %collective-permute-done.22.rest_0_), channel_id=1, source_target_pairs={{0,1},{1,0},{2,3},{3,2},{4,5},{5,4},{6,7},{7,6},{8,9},{9,8},{10,11... | collective-permute-start | bytes 393224 | tf_op jit(solution)/shard_map/ppermute | solution.py:42
  117.0 8.4 %collective-permute-start.28 = (bf16[512,128]{1,0:T(8,128)(2,1)S(1)}, bf16[512,128]{1,0:T(8,128)(2,1)S(1)}, u32[]{:S(2)}, u32[]{:S(2)}) collective-permute-start(bf16[512,128]{1,0:T(8,128)(2,1)S(1)} %collective-permute-done.27.rest_6_), channel_id=1, source_target_pairs={{0,1},{1,0},{2,3},{3,2},{4,5},{5,4},{6,7},{7,6},{8,9},{9,8},{10,11... | collective-permute-start | bytes 393224 | tf_op jit(solution)/shard_map/ppermute | solution.py:42
  119.8 12.8 %collective-permute-start.10 = (bf16[512,128]{1,0:T(8,128)(2,1)S(1)}, bf16[512,128]{1,0:T(8,128)(2,1)S(1)}, u32[]{:S(2)}, u32[]{:S(2)}) collective-permute-start(bf16[512,128]{1,0:T(8,128)(2,1)S(1)} %collective-permute-done.9.rest_0_), channel_id=1, source_target_pairs={{0,1},{1,0},{2,3},{3,2},{4,5},{5,4},{6,7},{7,6},{8,9},{9,8},{10,11... | collective-permute-start | bytes 393224 | tf_op jit(solution)/shard_map/ppermute | solution.py:42
  121.8 9.2 %collective-permute-start.25 = (bf16[512,128]{1,0:T(8,128)(2,1)S(1)}, bf16[512,128]{1,0:T(8,128)(2,1)S(1)}, u32[]{:S(2)}, u32[]{:S(2)}) collective-permute-start(bf16[512,128]{1,0:T(8,128)(2,1)S(1)} %collective-permute-done.24.rest_2_), channel_id=1, source_target_pairs={{0,1},{1,0},{2,3},{3,2},{4,5},{5,4},{6,7},{7,6},{8,9},{9,8},{10,11... | collective-permute-start | bytes 393224 | tf_op jit(solution)/shard_map/ppermute | solution.py:42
  123.3 10.5 %collective-permute-start.19 = (bf16[512,128]{1,0:T(8,128)(2,1)S(1)}, bf16[512,128]{1,0:T(8,128)(2,1)S(1)}, u32[]{:S(2)}, u32[]{:S(2)}) collective-permute-start(bf16[512,128]{1,0:T(8,128)(2,1)S(1)} %collective-permute-done.18.rest_4_), channel_id=1, source_target_pairs={{0,1},{1,0},{2,3},{3,2},{4,5},{5,4},{6,7},{7,6},{8,9},{9,8},{10,11... | collective-permute-start | bytes 393224 | tf_op jit(solution)/shard_map/ppermute | solution.py:42
  125.4 11.2 %collective-permute-start.12 = (bf16[512,128]{1,0:T(8,128)(2,1)S(1)}, bf16[512,128]{1,0:T(8,128)(2,1)S(1)}, u32[]{:S(2)}, u32[]{:S(2)}) collective-permute-start(bf16[512,128]{1,0:T(8,128)(2,1)S(1)} %collective-permute-done.11.rest_2_), channel_id=1, source_target_pairs={{0,1},{1,0},{2,3},{3,2},{4,5},{5,4},{6,7},{7,6},{8,9},{9,8},{10,11... | collective-permute-start | bytes 393224 | tf_op jit(solution)/shard_map/ppermute | solution.py:42
  126.9 11.5 %collective-permute-start.21 = (bf16[512,128]{1,0:T(8,128)(2,1)S(1)}, bf16[512,128]{1,0:T(8,128)(2,1)S(1)}, u32[]{:S(2)}, u32[]{:S(2)}) collective-permute-start(bf16[512,128]{1,0:T(8,128)(2,1)S(1)} %collective-permute-done.20.rest_6_), channel_id=1, source_target_pairs={{0,1},{1,0},{2,3},{3,2},{4,5},{5,4},{6,7},{7,6},{8,9},{9,8},{10,11... | collective-permute-start | bytes 393224 | tf_op jit(solution)/shard_map/ppermute | solution.py:42
  128.9 9.5 %copy-start.3 = (f32[8,768]{1,0:T(8,128)S(1)}, f32[8,768]{1,0:T(8,128)}, u32[]{:S(2)}) copy-start(f32[8,768]{1,0:T(8,128)} %get-tuple-element.36.rest_9_) | copy-start | bytes 73732

commit v4 on v3

--- a/solution.py
+++ b/solution.py
@@ -42,7 +42,7 @@
     return lax.ppermute(value, "tp", pairs)
 
 
-def spread(value, heads, group):
+def spread(value, heads, group, across_first):
     def send(block, step):
         return xor_permute(block, group, step)
 
@@ -53,14 +53,25 @@
         return [(value, 0)], [[] for _ in heads]
     near = both(value, 0)
     if group == 8:
-        near += both(send(value, 2), 2)
+        pair = send(value, 2)
+        if across_first:
+            near += [(pair, 2), (send(near[1][0], 2), 3)]
+        else:
+            near += both(pair, 2)
     far = []
-    for block in heads:
+    for head, block in enumerate(heads):
         pieces = []
         if group == 8:
             over = send(block, 4)
-            pieces += both(over, 4)
-            pieces += both(send(over, 2), 6)
+            if across_first:
+                crossed = near[1][0][:, head * HD : (head + 1) * HD]
+                crossed_over = send(crossed, 4)
+                pieces += [(over, 4), (crossed_over, 5)]
+                pieces += [(send(over, 2), 6)]
+                pieces += [(send(crossed_over, 2), 7)]
+            else:
+                pieces += both(over, 4)
+                pieces += both(send(over, 2), 6)
         else:
             for step in range(2, group, 2):
                 moved = send(block, step)
@@ -73,9 +84,10 @@
     return lax.ppermute(value, "stretch", [(0, 1), (1, 0)])
 
 
-def pack_body(place, *rest, half, rows, width, plan, gated):
+def pack_body(*rest, half, rows, width, plan, gated, group):
+    member, core = lax.axis_index("tp") % group, lax.axis_index("stretch")
     if gated:
-        table, rest = rest[0], rest[1:]
+        place, table, rest = rest[0], rest[1], rest[2:]
     query, stretch, history, rest = *rest[:3], rest[3:]
     count = len(plan)
     if gated:
@@ -86,10 +98,10 @@
         gate_copy.start()
     blocks, stages = rest[:count], rest[count : 2 * count]
     in_sems, out_sems = rest[2 * count :]
-    row = pl.multiple_of(place[1] * half, 8)
+    row = pl.multiple_of(core * half, 8)
     incoming = []
     for index, (step, low, cols) in enumerate(plan):
-        column = pl.ds(pl.multiple_of((place[0] ^ step) * width + low, HD), cols)
+        column = pl.ds(pl.multiple_of((member ^ step) * width + low, HD), cols)
         parts = (
             (history.at[0, pl.ds(row, half), column], 0, half),
             (history.at[1, pl.ds(row, half), column], half, half),
@@ -119,7 +131,7 @@
         gate_copy.wait()
 
 
-def pack(place, query, stretch, history, width, plan, table=None):
+def pack(query, stretch, history, width, plan, group, place=None, table=None):
     gated = table is not None
     rows, half = query.shape[0], history.shape[1] // 2
     shapes = [(2 * half + 3 * rows, cols) for _, _, cols in plan]
@@ -132,17 +144,17 @@
         outs = [jax.ShapeDtypeStruct((8, table.shape[1]), table.dtype)] + outs
         out_specs = [VMEM] + out_specs
         scratch.append(pltpu.SemaphoreType.DMA)
-        operands = [table] + operands
+        operands = [place, table] + operands
     return pl.pallas_call(
         functools.partial(
-            pack_body, half=half, rows=rows, width=width, plan=plan, gated=gated
+            pack_body, half=half, rows=rows, width=width, plan=plan, gated=gated, group=group
         ),
         out_shape=tuple(outs),
-        in_specs=[SMEM] + [HBM] * len(operands),
+        in_specs=([SMEM, HBM] if gated else []) + [HBM] * 3,
         out_specs=tuple(out_specs),
         scratch_shapes=scratch,
         name="pack",
-    )(place, *operands)
+    )(*operands)
 
 
 def stage_body(_, out):
@@ -388,10 +400,10 @@
     cross = list(range(group - 1, inner - 1, -1))
     arrays = (query[0], stretch_kv[:, 0], history_kv)
     plan = [(step, low, cols) for low, cols in chunks[:1] for step in cross]
-    blocks = pack(place, *arrays, width, plan) if plan else ()
+    blocks = pack(*arrays, width, plan, group) if plan else ()
     rest = [(step, 0, width) for step in range(inner)]
     rest += [(step, low, cols) for low, cols in chunks[1:] for step in cross]
-    gate_rows, *others = pack(place, *arrays, width, rest, gate_table)
+    gate_rows, *others = pack(*arrays, width, rest, group, place, gate_table)
     blocks = list(blocks) + others
     plan += rest
     sends = [{} for _ in chunks]
@@ -455,7 +467,7 @@
         else:
             attended, *singles = attend(q_all=None)
             singles = singles or [attended]
-        close, distant = spread(attended, singles, group)
+        close, distant = spread(attended, singles, group, index == len(chunks) - 1)
         groups[index] += [(value, step, low) for value, step in close]
         for head, pieces in enumerate(distant):
             late = min(index + (1 if head < len(distant) - 1 else 2), len(chunks))

time: 141 us -> 135 us (0.957)
  waiting for transfers between devices: 58.3 us -> 43.8 us
  starting transfers between devices: 58.6 us -> 67.2 us
    ppermute x29, waiting for transfers between devices: 58.3 us -> 43.7 us  [xor_permute(): return lax.ppermute(value, 'tp', pairs)]
    ppermute x29, starting transfers between devices: 58.4 us -> 67 us  [xor_permute(): return lax.ppermute(value, 'tp', pairs)]
  transfers between devices with their start and end apart: 32 -> 32, of which waited for: 16 -> 12; matrix products, arithmetic and copies ran while one was open for 0% -> 0% of each run, Pallas kernels for 11% -> 11%
where the time goes in v4:
time: 135 us; the launch traced here: 134 us
  starting transfers between devices  67.2 us (50%)
  waiting for transfers between devices  43.8 us (32%)
  Pallas kernels  20.6 us (15%)
  between operations  1.67 us (1%)
    ppermute x29, starting transfers between devices, xor_permute(): return lax.ppermute(value, 'tp', pairs)  67 us
    ppermute x29, waiting for transfers between devices, xor_permute(): return lax.ppermute(value, 'tp', pairs)  43.7 us
    pallas_call x2, Pallas kernels, attention(): pl.pallas_call(body, out_shape=outs, in_specs=[SMEM] + [VMEM] * (1 + len(...  8.4 us
    pallas_call x2, Pallas kernels, pack(): pl.pallas_call(functools.partial(pack_body, half=half, rows=rows, width=w...  6.04 us
    pallas_call x3, Pallas kernels, project(): pl.pallas_call(functools.partial(project_body, rows=rows, last=last, firs...  5.51 us
  transfers between devices with their start and end apart: 32, of which 12 were waited for; matrix products, arithmetic and copies ran while one was open for 0% of the time, Pallas kernels for 11%

profile of v4, /device:TPU:0, one launch (start us, length us, event | category | flops | bytes accessed | tf_op | source)
XLA Modules:
  0.0 134.3 jit_solution(15208922827945319498)
XLA Ops:
  1.3 0.6 stack.16.place.rest_0_
  1.9 4.0 %pack.2 = (f32[8,768]{1,0:T(8,128)}, bf16[448,384]{1,0:T(8,128)(2,1)}, bf16[448,384]{1,0:T(8,128)(2,1)}, bf16[448,384]{1,0:T(8,128)(2,1)}, bf16[448,384]{1,0:T(8...) custom-call(s32[5]{0:T(128)} %stack.16.place.rest_0_, ...), custom_call_target="tpu_custom_call" | custom-call | tf_op jit(solution)/shard_map/pack/pallas_call | solution.py:148
  5.9 4.1 %collective-permute-start.2 = (bf16[448,384]{1,0:T(8,128)(2,1)}, bf16[448,384]{1,0:T(8,128)(2,1)S(1)}, u32[]{:S(2)}, u32[]{:S(2)}) collective-permute-start(bf16[448,384]{1,0:T(8,128)(2,1)} %get-tuple-element.24), channel_id=1, source_target_pairs={{0,3},{1,2},{2,1},{3,0},{4,7},{5,6},{6,5},{7,4},{8,11},{9,10},{10,... | collective-permute-start | bytes 1032200 | tf_op jit(solution)/shard_map/ppermute | solution.py:42
  9.9 0.4 collective-permute-start.1
  10.4 0.2 collective-permute-start
  10.6 2.1 %pack.3 = (bf16[448,256]{1,0:T(8,128)(2,1)}, bf16[448,256]{1,0:T(8,128)(2,1)}, bf16[448,256]{1,0:T(8,128)(2,1)}, bf16[448,256]{1,0:T(8,128)(2,1)}) custom-call(bf16[64,3072]{1,0:T(8,128)(2,1)} %bitcast.11, bf16[2,64,3072]{2,1,0:T(8,128)(2,1)} %bitcast.9, bf16[2,256,3072]{2,1,0:T(8,128)(2,1)} %rest_2_.1), custom_call_target="tpu_custom_call" | custom-call | tf_op jit(solution)/shard_map/pack/pallas_call | solution.py:148
  12.7 3.0 %collective-permute-start.3 = (bf16[448,256]{1,0:T(8,128)(2,1)}, bf16[448,256]{1,0:T(8,128)(2,1)S(1)}, u32[]{:S(2)}, u32[]{:S(2)}) collective-permute-start(bf16[448,256]{1,0:T(8,128)(2,1)} %get-tuple-element.25), channel_id=1, source_target_pairs={{0,4},{1,5},{2,6},{3,7},{4,0},{5,1},{6,2},{7,3},{8,12},{9,13},{10,... | collective-permute-start | bytes 688136 | tf_op jit(solution)/shard_map/ppermute | solution.py:42
  15.7 1.3 collective-permute-start.4
  17.0 12.0 %collective-permute-done.2.rest_3_ = bf16[448,384]{1,0:T(8,128)(2,1)S(1)} collective-permute-done((bf16[448,384]{1,0:T(8,128)(2,1)}, bf16[448,384]{1,0:T(8,128)(2,1)S(1)}, u32[]{:S(2)}, u32[]{:S(2)}) %collective-permute-start.2) | collective-permute-done | bytes 344096 | tf_op jit(solution)/shard_map/ppermute | solution.py:42
  29.0 3.0 %collective-permute-start.5 = (bf16[448,256]{1,0:T(8,128)(2,1)}, bf16[448,256]{1,0:T(8,128)(2,1)S(1)}, u32[]{:S(2)}, u32[]{:S(2)}) collective-permute-start(bf16[448,256]{1,0:T(8,128)(2,1)} %get-tuple-element.27), channel_id=1, source_target_pairs={{0,6},{1,7},{2,4},{3,5},{4,2},{5,3},{6,0},{7,1},{8,14},{9,15},{10,... | collective-permute-start | bytes 688136 | tf_op jit(solution)/shard_map/ppermute | solution.py:42
  32.0 3.6 %collective-permute-done.1.rest_2_ = bf16[448,384]{1,0:T(8,128)(2,1)S(1)} collective-permute-done((bf16[448,384]{1,0:T(8,128)(2,1)}, bf16[448,384]{1,0:T(8,128)(2,1)S(1)}, u32[]{:S(2)}, u32[]{:S(2)}) %collective-permute-start.1) | collective-permute-done | bytes 344096 | tf_op jit(solution)/shard_map/ppermute | solution.py:42
  35.7 2.9 %collective-permute-start.6 = (bf16[448,256]{1,0:T(8,128)(2,1)}, bf16[448,256]{1,0:T(8,128)(2,1)S(1)}, u32[]{:S(2)}, u32[]{:S(2)}) collective-permute-start(bf16[448,256]{1,0:T(8,128)(2,1)} %get-tuple-element.28), channel_id=1, source_target_pairs={{0,7},{1,6},{2,5},{3,4},{4,3},{5,2},{6,1},{7,0},{8,15},{9,14},{10,... | collective-permute-start | bytes 688136 | tf_op jit(solution)/shard_map/ppermute | solution.py:42
  38.7 0.1 pad_maximum_fusion
  38.8 0.1 collective-permute-start.7
  38.9 8.6 %collective-permute-done.6.rest_7_ = bf16[448,256]{1,0:T(8,128)(2,1)S(1)} collective-permute-done((bf16[448,256]{1,0:T(8,128)(2,1)}, bf16[448,256]{1,0:T(8,128)(2,1)S(1)}, u32[]{:S(2)}, u32[]{:S(2)}) %collective-permute-start.6) | collective-permute-done | bytes 229408 | tf_op jit(solution)/shard_map/ppermute | solution.py:42
  47.6 0.0 collective-permute-done.4.rest_5_
  47.6 0.0 collective-permute-done.3.rest_4_
  47.7 0.0 copy-start.4
  47.7 0.1 pad_maximum_fusion.1
  47.7 0.1 collective-permute-start.8
  47.8 2.5 %collective-permute-start.16 = (bf16[448,128]{1,0:T(8,128)(2,1)S(1)}, bf16[448,128]{1,0:T(8,128)(2,1)S(1)}, u32[]{:S(2)}, u32[]{:S(2)}) collective-permute-start(bf16[448,128]{1,0:T(8,128)(2,1)S(1)} %copy-done.8), channel_id=1, source_target_pairs={{0,7},{1,6},{2,5},{3,4},{4,3},{5,2},{6,1},{7,0},{8,15},{9,14},{10,... | collective-permute-start | bytes 344072 | tf_op jit(solution)/shard_map/ppermute | solution.py:42
  50.3 8.3 %collective-permute-start.15 = (bf16[448,128]{1,0:T(8,128)(2,1)S(1)}, bf16[448,128]{1,0:T(8,128)(2,1)S(1)}, u32[]{:S(2)}, u32[]{:S(2)}) collective-permute-start(bf16[448,128]{1,0:T(8,128)(2,1)S(1)} %copy-done.7), channel_id=1, source_target_pairs={{0,6},{1,7},{2,4},{3,5},{4,2},{5,3},{6,0},{7,1},{8,14},{9,15},{10,... | collective-permute-start | bytes 344072 | tf_op jit(solution)/shard_map/ppermute | solution.py:42
  58.6 4.5 %collective-permute-start.14 = (bf16[448,128]{1,0:T(8,128)(2,1)S(1)}, bf16[448,128]{1,0:T(8,128)(2,1)S(1)}, u32[]{:S(2)}, u32[]{:S(2)}) collective-permute-start(bf16[448,128]{1,0:T(8,128)(2,1)S(1)} %copy-done.6), channel_id=1, source_target_pairs={{0,5},{1,4},{2,7},{3,6},{4,1},{5,0},{6,3},{7,2},{8,13},{9,12},{10,... | collective-permute-start | bytes 344072 | tf_op jit(solution)/shard_map/ppermute | solution.py:42
  63.1 0.0 collective-permute-done.16.rest_7_
  63.1 10.2 %collective-permute-start.13 = (bf16[448,128]{1,0:T(8,128)(2,1)S(1)}, bf16[448,128]{1,0:T(8,128)(2,1)S(1)}, u32[]{:S(2)}, u32[]{:S(2)}) collective-permute-start(bf16[448,128]{1,0:T(8,128)(2,1)S(1)} %copy-done.5), channel_id=1, source_target_pairs={{0,4},{1,5},{2,6},{3,7},{4,0},{5,1},{6,2},{7,3},{8,12},{9,13},{10,... | collective-permute-start | bytes 344072 | tf_op jit(solution)/shard_map/ppermute | solution.py:42
  73.3 5.5 %collective-permute-done.14.rest_5_ = bf16[448,128]{1,0:T(8,128)(2,1)S(1)} collective-permute-done((bf16[448,128]{1,0:T(8,128)(2,1)S(1)}, bf16[448,128]{1,0:T(8,128)(2,1)S(1)}, u32[]{:S(2)}, u32[]{:S(2)}) %collective-permute-start.14) | collective-permute-done | bytes 114720 | tf_op jit(solution)/shard_map/ppermute | solution.py:42
  78.7 0.7 collective-permute-done.13.rest_4_
  79.5 0.1 collective-permute-start.17
  79.6 0.6 bias.1.bias_ref
  80.2 0.0 collective-permute-done.8.rest_9_
  80.3 0.0 collective-permute-done.7.rest_8_
  80.3 5.4 %attend.2 = (bf16[512,256]{1,0:T(8,128)(2,1)S(1)}, bf16[512,128]{1,0:T(8,128)(2,1)S(1)}, bf16[512,128]{1,0:T(8,128)(2,1)S(1)}) custom-call(s32[5]{0:T(128)S(1)} %copy-done.2, f32[4,1,3072]{2,1,0:T(1,128)S(1)} %bias.1.bias_ref, bf16[448,384]{1,0:T(8,128)(2,1)S(1)} %copy-done.1, bf16[448,384]{1,0:T(8,128)(2,1)S(1)} %collective-permute-done.rest_1_, ...), custom_call_target="tpu_custom_call" | custom-call | tf_op jit(solution)/shard_map/attend/pallas_call | solution.py:279
  85.6 0.1 collective-permute-start.30
  85.7 2.7 %collective-permute-start.9 = (bf16[512,128]{1,0:T(8,128)(2,1)S(1)}, bf16[512,128]{1,0:T(8,128)(2,1)S(1)}, u32[]{:S(2)}, u32[]{:S(2)}) collective-permute-start(bf16[512,128]{1,0:T(8,128)(2,1)S(1)} %get-tuple-element.29), channel_id=1, source_target_pairs={{0,4},{1,5},{2,6},{3,7},{4,0},{5,1},{6,2},{7,3},{8,12},{9,13},{10,... | collective-permute-start | bytes 393224 | tf_op jit(solution)/shard_map/ppermute | solution.py:42
  88.4 0.0 collective-permute-done.17.rest_9_
  88.4 3.0 %attend.3.rest_4_ = bf16[512,128]{1,0:T(8,128)(2,1)S(1)} custom-call(s32[5]{0:T(128)S(1)} %copy-done.2, f32[4,1,3072]{2,1,0:T(1,128)S(1)} %bias.1.bias_ref, bf16[448,384]{1,0:T(8,128)(2,1)S(1)} %copy-done.1, bf16[448,384]{1,0:T(8,128)(2,1)S(1)} %collective-permute-done.rest_1_, bf16[448,384]{1,0:T(8,128)(2,1)S(1)} %collective-permute-done.1.rest_2_, ...), custom_call_target="tpu_custom_call" | custom-call | tf_op jit(solution)/shard_map/attend/pallas_call | solution.py:279
  91.4 0.4 collective-permute-start.18
  91.8 2.4 %collective-permute-start.29 = (bf16[512,256]{1,0:T(8,128)(2,1)S(1)}, bf16[512,256]{1,0:T(8,128)(2,1)S(1)}, u32[]{:S(2)}, u32[]{:S(2)}) collective-permute-start(bf16[512,256]{1,0:T(8,128)(2,1)S(1)} %get-tuple-element.35.rest_0_), channel_id=1, source_target_pairs={{0,1},{1,0},{2,3},{3,2},{4,5},{5,4},{6,7},{7,6},{8,9},{9,8},{10,11... | collective-permute-start | bytes 786440 | tf_op jit(solution)/shard_map/ppermute | solution.py:42
  94.2 0.1 collective-permute-start.19
  94.3 1.0 collective-permute-done.9.rest_0_
  95.2 3.4 %collective-permute-start.23 = (bf16[512,128]{1,0:T(8,128)(2,1)S(1)}, bf16[512,128]{1,0:T(8,128)(2,1)S(1)}, u32[]{:S(2)}, u32[]{:S(2)}) collective-permute-start(bf16[512,128]{1,0:T(8,128)(2,1)S(1)} %get-tuple-element.34), channel_id=1, source_target_pairs={{0,4},{1,5},{2,6},{3,7},{4,0},{5,1},{6,2},{7,3},{8,12},{9,13},{10,... | collective-permute-start | bytes 393224 | tf_op jit(solution)/shard_map/ppermute | solution.py:42
  98.7 7.4 %collective-permute-done.18.rest_4_ = bf16[512,128]{1,0:T(8,128)(2,1)S(1)} collective-permute-done((bf16[512,128]{1,0:T(8,128)(2,1)S(1)}, bf16[512,128]{1,0:T(8,128)(2,1)S(1)}, u32[]{:S(2)}, u32[]{:S(2)}) %collective-permute-start.18) | collective-permute-done | bytes 131104 | tf_op jit(solution)/shard_map/ppermute | solution.py:42
  106.1 0.0 collective-permute-start.27
  106.1 0.0 collective-permute-done.19.rest_5_
  106.1 2.0 %collective-permute-start.11 = (bf16[512,128]{1,0:T(8,128)(2,1)S(1)}, bf16[512,128]{1,0:T(8,128)(2,1)S(1)}, u32[]{:S(2)}, u32[]{:S(2)}) collective-permute-start(bf16[512,128]{1,0:T(8,128)(2,1)S(1)} %collective-permute-done.9.rest_0_), channel_id=1, source_target_pairs={{0,2},{1,3},{2,0},{3,1},{4,6},{5,7},{6,4},{7,5},{8,10},{9,11},{10,... | collective-permute-start | bytes 393224 | tf_op jit(solution)/shard_map/ppermute | solution.py:42
  108.1 2.7 %collective-permute-start.31 = (bf16[512,256]{1,0:T(8,128)(2,1)S(1)}, bf16[512,256]{1,0:T(8,128)(2,1)S(1)}, u32[]{:S(2)}, u32[]{:S(2)}) collective-permute-start(bf16[512,256]{1,0:T(8,128)(2,1)S(1)} %collective-permute-done.30.rest_2_), channel_id=1, source_target_pairs={{0,1},{1,0},{2,3},{3,2},{4,5},{5,4},{6,7},{7,6},{8,9},{9,8},{10,11... | collective-permute-start | bytes 786440 | tf_op jit(solution)/shard_map/ppermute | solution.py:42
  110.8 0.0 collective-permute-done.23.rest_0_
  110.8 0.0 collective-permute-start.20
  110.8 1.7 %collective-permute-done.27.rest_6_ = bf16[512,128]{1,0:T(8,128)(2,1)S(1)} collective-permute-done((bf16[512,128]{1,0:T(8,128)(2,1)S(1)}, bf16[512,128]{1,0:T(8,128)(2,1)S(1)}, u32[]{:S(2)}, u32[]{:S(2)}) %collective-permute-start.27) | collective-permute-done | bytes 131104 | tf_op jit(solution)/shard_map/ppermute | solution.py:42
  112.4 0.2 collective-permute-start.25
  112.7 0.0 collective-permute-done.29.rest_1_
  112.7 3.3 %collective-permute-start.24 = (bf16[512,128]{1,0:T(8,128)(2,1)S(1)}, bf16[512,128]{1,0:T(8,128)(2,1)S(1)}, u32[]{:S(2)}, u32[]{:S(2)}) collective-permute-start(bf16[512,128]{1,0:T(8,128)(2,1)S(1)} %collective-permute-done.23.rest_0_), channel_id=1, source_target_pairs={{0,1},{1,0},{2,3},{3,2},{4,5},{5,4},{6,7},{7,6},{8,9},{9,8},{10,11... | collective-permute-start | bytes 393224 | tf_op jit(solution)/shard_map/ppermute | solution.py:42
  115.9 0.3 collective-permute-done.11.rest_2_
  116.2 1.8 %collective-permute-start.28 = (bf16[512,128]{1,0:T(8,128)(2,1)S(1)}, bf16[512,128]{1,0:T(8,128)(2,1)S(1)}, u32[]{:S(2)}, u32[]{:S(2)}) collective-permute-start(bf16[512,128]{1,0:T(8,128)(2,1)S(1)} %collective-permute-done.19.rest_5_), channel_id=1, source_target_pairs={{0,2},{1,3},{2,0},{3,1},{4,6},{5,7},{6,4},{7,5},{8,10},{9,11},{10,... | collective-permute-start | bytes 393224 | tf_op jit(solution)/shard_map/ppermute | solution.py:42
  118.0 1.0 collective-permute-done.20.rest_5_
  119.0 1.7 %collective-permute-start.10 = (bf16[512,128]{1,0:T(8,128)(2,1)S(1)}, bf16[512,128]{1,0:T(8,128)(2,1)S(1)}, u32[]{:S(2)}, u32[]{:S(2)}) collective-permute-start(bf16[512,128]{1,0:T(8,128)(2,1)S(1)} %collective-permute-done.9.rest_0_), channel_id=1, source_target_pairs={{0,1},{1,0},{2,3},{3,2},{4,5},{5,4},{6,7},{7,6},{8,9},{9,8},{10,11... | collective-permute-start | bytes 393224 | tf_op jit(solution)/shard_map/ppermute | solution.py:42
  120.7 0.1 collective-permute-done.25.rest_2_
  120.9 2.7 %collective-permute-start.26 = (bf16[512,128]{1,0:T(8,128)(2,1)S(1)}, bf16[512,128]{1,0:T(8,128)(2,1)S(1)}, u32[]{:S(2)}, u32[]{:S(2)}) collective-permute-start(bf16[512,128]{1,0:T(8,128)(2,1)S(1)} %collective-permute-done.25.rest_2_), channel_id=1, source_target_pairs={{0,1},{1,0},{2,3},{3,2},{4,5},{5,4},{6,7},{7,6},{8,9},{9,8},{10,11... | collective-permute-start | bytes 393224 | tf_op jit(solution)/shard_map/ppermute | solution.py:42
  123.5 0.0 collective-permute-start.21
  123.6 3.3 %collective-permute-start.12 = (bf16[512,128]{1,0:T(8,128)(2,1)S(1)}, bf16[512,128]{1,0:T(8,128)(2,1)S(1)}, u32[]{:S(2)}, u32[]{:S(2)}) collective-permute-start(bf16[512,128]{1,0:T(8,128)(2,1)S(1)} %collective-permute-done.11.rest_2_), channel_id=1, source_target_pairs={{0,1},{1,0},{2,3},{3,2},{4,5},{5,4},{6,7},{7,6},{8,9},{9,8},{10,11... | collective-permute-start | bytes 393224 | tf_op jit(solution)/shard_map/ppermute | solution.py:42
  126.9 1.5 %project.3.rest_8_ = f32[512,768]{1,0:T(8,128)S(1)} custom-call(s32[5]{0:T(128)S(1)} %copy-done.2, bf16[3072,768]{1,0:T(8,128)(2,1)S(1)} %copy-done, bf16[512,256]{1,0:T(8,128)(2,1)S(1)} %get-tuple-element.35.rest_0_, bf16[512,256]{1,0:T(8,128)(2,1)S(1)} %collective-permute-done.29.rest_1_, bf16[512,256]{1,0:T(8,128)(2,1)S(1)} %collective-permute-done.30.rest_2_, ...), custom_call_target="tpu_custom_call" | custom-call | tf_op jit(solution)/shard_map/project/pallas_call | solution.py:321
  128.5 1.5 %project.4.rest_8_ = f32[512,768]{1,0:T(8,128)S(1)} custom-call(s32[5]{0:T(128)S(1)} %copy-done.2, bf16[3072,768]{1,0:T(8,128)(2,1)S(1)} %copy-done, bf16[512,128]{1,0:T(8,128)(2,1)S(1)} %collective-permute-done.23.rest_0_, bf16[512,128]{1,0:T(8,128)(2,1)S(1)} %collective-permute-done.24.rest_1_, bf16[512,128]{1,0:T(8,128)(2,1)S(1)} %collective-permute-done.25.rest_2_, ...), custom_call_target="tpu_custom_call" | custom-call | tf_op jit(solution)/shard_map/project/pallas_call | solution.py:321
  130.0 1.8 %collective-permute-done.22.rest_7_ = bf16[512,128]{1,0:T(8,128)(2,1)S(1)} collective-permute-done((bf16[512,128]{1,0:T(8,128)(2,1)S(1)}, bf16[512,128]{1,0:T(8,128)(2,1)S(1)}, u32[]{:S(2)}, u32[]{:S(2)}) %collective-permute-start.22) | collective-permute-done | bytes 131104 | tf_op jit(solution)/shard_map/ppermute | solution.py:42
  131.9 2.4 %project.5 = bf16[512,768]{1,0:T(8,128)(2,1)} custom-call(s32[5]{0:T(128)S(1)} %copy-done.2, bf16[3072,768]{1,0:T(8,128)(2,1)S(1)} %copy-done, bf16[512,128]{1,0:T(8,128)(2,1)S(1)} %collective-permute-done.9.rest_0_, bf16[512,128]{1,0:T(8,128)(2,1)S(1)} %collective-permute-done.10.rest_1_, bf16[512,128]{1,0:T(8,128)(2,1)S(1)} %collective-permute-done.11.rest_2_, ...), custom_call_target="tpu_custom_call" | custom-call | tf_op jit(solution)/shard_map/project/pallas_call | solution.py:321
  (43 shorter events, 0.3 us)
Async XLA Ops:
  5.9 23.1 %collective-permute-start.2 = (bf16[448,384]{1,0:T(8,128)(2,1)}, bf16[448,384]{1,0:T(8,128)(2,1)S(1)}, u32[]{:S(2)}, u32[]{:S(2)}) collective-permute-start(bf16[448,384]{1,0:T(8,128)(2,1)} %get-tuple-element.24), channel_id=1, source_target_pairs={{0,3},{1,2},{2,1},{3,0},{4,7},{5,6},{6,5},{7,4},{8,11},{9,10},{10,... | collective-permute-start | bytes 1032200 | tf_op jit(solution)/shard_map/ppermute | solution.py:42
  9.9 25.7 %collective-permute-start.1 = (bf16[448,384]{1,0:T(8,128)(2,1)}, bf16[448,384]{1,0:T(8,128)(2,1)S(1)}, u32[]{:S(2)}, u32[]{:S(2)}) collective-permute-start(bf16[448,384]{1,0:T(8,128)(2,1)} %get-tuple-element.23), channel_id=1, source_target_pairs={{0,2},{1,3},{2,0},{3,1},{4,6},{5,7},{6,4},{7,5},{8,10},{9,11},{10,... | collective-permute-start | bytes 1032200 | tf_op jit(solution)/shard_map/ppermute | solution.py:42
  10.4 6.6 %copy-start.1 = (bf16[448,384]{1,0:T(8,128)(2,1)S(1)}, bf16[448,384]{1,0:T(8,128)(2,1)}, u32[]{:S(2)}) copy-start(bf16[448,384]{1,0:T(8,128)(2,1)} %get-tuple-element.21.rest_0_) | copy-start | bytes 1032196
  10.4 28.2 %collective-permute-start = (bf16[448,384]{1,0:T(8,128)(2,1)}, bf16[448,384]{1,0:T(8,128)(2,1)S(1)}, u32[]{:S(2)}, u32[]{:S(2)}) collective-permute-start(bf16[448,384]{1,0:T(8,128)(2,1)} %get-tuple-element.22), channel_id=1, source_target_pairs={{0,1},{1,0},{2,3},{3,2},{4,5},{5,4},{6,7},{7,6},{8,9},{9,8},{10,11... | collective-permute-start | bytes 1032200 | tf_op jit(solution)/shard_map/ppermute | solution.py:42
  12.7 34.9 %collective-permute-start.3 = (bf16[448,256]{1,0:T(8,128)(2,1)}, bf16[448,256]{1,0:T(8,128)(2,1)S(1)}, u32[]{:S(2)}, u32[]{:S(2)}) collective-permute-start(bf16[448,256]{1,0:T(8,128)(2,1)} %get-tuple-element.25), channel_id=1, source_target_pairs={{0,4},{1,5},{2,6},{3,7},{4,0},{5,1},{6,2},{7,3},{8,12},{9,13},{10,... | collective-permute-start | bytes 688136 | tf_op jit(solution)/shard_map/ppermute | solution.py:42
  15.7 31.9 %collective-permute-start.4 = (bf16[448,256]{1,0:T(8,128)(2,1)}, bf16[448,256]{1,0:T(8,128)(2,1)S(1)}, u32[]{:S(2)}, u32[]{:S(2)}) collective-permute-start(bf16[448,256]{1,0:T(8,128)(2,1)} %get-tuple-element.26), channel_id=1, source_target_pairs={{0,5},{1,4},{2,7},{3,6},{4,1},{5,0},{6,3},{7,2},{8,13},{9,12},{10,... | collective-permute-start | bytes 688136 | tf_op jit(solution)/shard_map/ppermute | solution.py:42
  29.0 18.6 %collective-permute-start.5 = (bf16[448,256]{1,0:T(8,128)(2,1)}, bf16[448,256]{1,0:T(8,128)(2,1)S(1)}, u32[]{:S(2)}, u32[]{:S(2)}) collective-permute-start(bf16[448,256]{1,0:T(8,128)(2,1)} %get-tuple-element.27), channel_id=1, source_target_pairs={{0,6},{1,7},{2,4},{3,5},{4,2},{5,3},{6,0},{7,1},{8,14},{9,15},{10,... | collective-permute-start | bytes 688136 | tf_op jit(solution)/shard_map/ppermute | solution.py:42
  35.7 11.9 %collective-permute-start.6 = (bf16[448,256]{1,0:T(8,128)(2,1)}, bf16[448,256]{1,0:T(8,128)(2,1)S(1)}, u32[]{:S(2)}, u32[]{:S(2)}) collective-permute-start(bf16[448,256]{1,0:T(8,128)(2,1)} %get-tuple-element.28), channel_id=1, source_target_pairs={{0,7},{1,6},{2,5},{3,4},{4,3},{5,2},{6,1},{7,0},{8,15},{9,14},{10,... | collective-permute-start | bytes 688136 | tf_op jit(solution)/shard_map/ppermute | solution.py:42
  38.6 9.2 %copy-start.8 = (bf16[448,128]{1,0:T(8,128)(2,1)S(1)}, bf16[448,128]{1,0:T(8,128)(2,1)}, u32[]{:S(2)}) copy-start(bf16[448,128]{1,0:T(8,128)(2,1)} %get-tuple-element.33) | copy-start | bytes 344068
  38.6 11.6 %copy-start.7 = (bf16[448,128]{1,0:T(8,128)(2,1)S(1)}, bf16[448,128]{1,0:T(8,128)(2,1)}, u32[]{:S(2)}) copy-start(bf16[448,128]{1,0:T(8,128)(2,1)} %get-tuple-element.32) | copy-start | bytes 344068
  38.7 19.9 %copy-start.6 = (bf16[448,128]{1,0:T(8,128)(2,1)S(1)}, bf16[448,128]{1,0:T(8,128)(2,1)}, u32[]{:S(2)}) copy-start(bf16[448,128]{1,0:T(8,128)(2,1)} %get-tuple-element.31) | copy-start | bytes 344068
  38.7 24.4 %copy-start.5 = (bf16[448,128]{1,0:T(8,128)(2,1)S(1)}, bf16[448,128]{1,0:T(8,128)(2,1)}, u32[]{:S(2)}) copy-start(bf16[448,128]{1,0:T(8,128)(2,1)} %get-tuple-element.30) | copy-start | bytes 344068
  38.8 41.5 %collective-permute-start.7 = (bf16[1536,384]{1,0:T(8,128)(2,1)S(1)}, bf16[1536,384]{1,0:T(8,128)(2,1)S(1)}, u32[]{:S(2)}, u32[]{:S(2)}) collective-permute-start(bf16[1536,384]{1,0:T(8,128)(2,1)S(1)} %pad_maximum_fusion), channel_id=1, source_target_pairs={{0,8},{8,0},{1,9},{9,1},{2,10},{10,2},{3,11},{11,3},{4,12},{12,4},... | collective-permute-start | bytes 3538952 | tf_op jit(solution)/shard_map/ppermute | solution.py:84
  47.5 32.7 %copy-start = (bf16[3072,768]{1,0:T(8,128)(2,1)S(1)}, bf16[3072,768]{1,0:T(8,128)(2,1)}, u32[]{:S(2)}) copy-start(bf16[3072,768]{1,0:T(8,128)(2,1)} %weight.5) | copy-start | bytes 14155780
  47.6 31.9 %copy-start.2 = (s32[5]{0:T(128)S(1)}, s32[5]{0:T(128)}, u32[]{:S(2)}) copy-start(s32[5]{0:T(128)} %stack.16.place.rest_0_) | copy-start | bytes 64
  47.7 31.9 %copy-start.4 = (s32[1,4,8]{2,1,0:T(4,128)S(1)}, s32[1,4,8]{2,1,0:T(4,128)}, u32[]{:S(2)}) copy-start(s32[1,4,8]{2,1,0:T(4,128)} %param.11) | copy-start | bytes 388
  47.7 32.5 %collective-permute-start.8 = (bf16[1536,256]{1,0:T(8,128)(2,1)S(1)}, bf16[1536,256]{1,0:T(8,128)(2,1)S(1)}, u32[]{:S(2)}, u32[]{:S(2)}) collective-permute-start(bf16[1536,256]{1,0:T(8,128)(2,1)S(1)} %pad_maximum_fusion.1), channel_id=1, source_target_pairs={{0,8},{8,0},{1,9},{9,1},{2,10},{10,2},{3,11},{11,3},{4,12},{12,4},... | collective-permute-start | bytes 2359304 | tf_op jit(solution)/shard_map/ppermute | solution.py:84
  47.8 15.3 %collective-permute-start.16 = (bf16[448,128]{1,0:T(8,128)(2,1)S(1)}, bf16[448,128]{1,0:T(8,128)(2,1)S(1)}, u32[]{:S(2)}, u32[]{:S(2)}) collective-permute-start(bf16[448,128]{1,0:T(8,128)(2,1)S(1)} %copy-done.8), channel_id=1, source_target_pairs={{0,7},{1,6},{2,5},{3,4},{4,3},{5,2},{6,1},{7,0},{8,15},{9,14},{10,... | collective-permute-start | bytes 344072 | tf_op jit(solution)/shard_map/ppermute | solution.py:42
  50.3 23.0 %collective-permute-start.15 = (bf16[448,128]{1,0:T(8,128)(2,1)S(1)}, bf16[448,128]{1,0:T(8,128)(2,1)S(1)}, u32[]{:S(2)}, u32[]{:S(2)}) collective-permute-start(bf16[448,128]{1,0:T(8,128)(2,1)S(1)} %copy-done.7), channel_id=1, source_target_pairs={{0,6},{1,7},{2,4},{3,5},{4,2},{5,3},{6,0},{7,1},{8,14},{9,15},{10,... | collective-permute-start | bytes 344072 | tf_op jit(solution)/shard_map/ppermute | solution.py:42
  58.6 20.1 %collective-permute-start.14 = (bf16[448,128]{1,0:T(8,128)(2,1)S(1)}, bf16[448,128]{1,0:T(8,128)(2,1)S(1)}, u32[]{:S(2)}, u32[]{:S(2)}) collective-permute-start(bf16[448,128]{1,0:T(8,128)(2,1)S(1)} %copy-done.6), channel_id=1, source_target_pairs={{0,5},{1,4},{2,7},{3,6},{4,1},{5,0},{6,3},{7,2},{8,13},{9,12},{10,... | collective-permute-start | bytes 344072 | tf_op jit(solution)/shard_map/ppermute | solution.py:42
  63.1 16.4 %collective-permute-start.13 = (bf16[448,128]{1,0:T(8,128)(2,1)S(1)}, bf16[448,128]{1,0:T(8,128)(2,1)S(1)}, u32[]{:S(2)}, u32[]{:S(2)}) collective-permute-start(bf16[448,128]{1,0:T(8,128)(2,1)S(1)} %copy-done.5), channel_id=1, source_target_pairs={{0,4},{1,5},{2,6},{3,7},{4,0},{5,1},{6,2},{7,3},{8,12},{9,13},{10,... | collective-permute-start | bytes 344072 | tf_op jit(solution)/shard_map/ppermute | solution.py:42
  79.5 8.9 %collective-permute-start.17 = (bf16[1536,128]{1,0:T(8,128)(2,1)S(1)}, bf16[1536,128]{1,0:T(8,128)(2,1)S(1)}, u32[]{:S(2)}, u32[]{:S(2)}) collective-permute-start(bf16[1536,128]{1,0:T(8,128)(2,1)S(1)} %pad_maximum_fusion.2), channel_id=1, source_target_pairs={{0,8},{8,0},{1,9},{9,1},{2,10},{10,2},{3,11},{11,3},{4,12},{12,4},... | collective-permute-start | bytes 1179656 | tf_op jit(solution)/shard_map/ppermute | solution.py:84
  85.6 22.5 %collective-permute-start.30 = (bf16[512,256]{1,0:T(8,128)(2,1)S(1)}, bf16[512,256]{1,0:T(8,128)(2,1)S(1)}, u32[]{:S(2)}, u32[]{:S(2)}) collective-permute-start(bf16[512,256]{1,0:T(8,128)(2,1)S(1)} %get-tuple-element.35.rest_0_), channel_id=1, source_target_pairs={{0,2},{1,3},{2,0},{3,1},{4,6},{5,7},{6,4},{7,5},{8,10},{9,11},{10,... | collective-permute-start | bytes 786440 | tf_op jit(solution)/shard_map/ppermute | solution.py:42
  85.7 9.5 %collective-permute-start.9 = (bf16[512,128]{1,0:T(8,128)(2,1)S(1)}, bf16[512,128]{1,0:T(8,128)(2,1)S(1)}, u32[]{:S(2)}, u32[]{:S(2)}) collective-permute-start(bf16[512,128]{1,0:T(8,128)(2,1)S(1)} %get-tuple-element.29), channel_id=1, source_target_pairs={{0,4},{1,5},{2,6},{3,7},{4,0},{5,1},{6,2},{7,3},{8,12},{9,13},{10,... | collective-permute-start | bytes 393224 | tf_op jit(solution)/shard_map/ppermute | solution.py:42
  91.4 14.7 %collective-permute-start.18 = (bf16[512,128]{1,0:T(8,128)(2,1)S(1)}, bf16[512,128]{1,0:T(8,128)(2,1)S(1)}, u32[]{:S(2)}, u32[]{:S(2)}) collective-permute-start(bf16[512,128]{1,0:T(8,128)(2,1)S(1)} %attend.3.rest_4_), channel_id=1, source_target_pairs={{0,4},{1,5},{2,6},{3,7},{4,0},{5,1},{6,2},{7,3},{8,12},{9,13},{10,... | collective-permute-start | bytes 393224 | tf_op jit(solution)/shard_map/ppermute | solution.py:42
  91.8 20.9 %collective-permute-start.29 = (bf16[512,256]{1,0:T(8,128)(2,1)S(1)}, bf16[512,256]{1,0:T(8,128)(2,1)S(1)}, u32[]{:S(2)}, u32[]{:S(2)}) collective-permute-start(bf16[512,256]{1,0:T(8,128)(2,1)S(1)} %get-tuple-element.35.rest_0_), channel_id=1, source_target_pairs={{0,1},{1,0},{2,3},{3,2},{4,5},{5,4},{6,7},{7,6},{8,9},{9,8},{10,11... | collective-permute-start | bytes 786440 | tf_op jit(solution)/shard_map/ppermute | solution.py:42
  94.2 11.9 %collective-permute-start.19 = (bf16[512,128]{1,0:T(8,128)(2,1)S(1)}, bf16[512,128]{1,0:T(8,128)(2,1)S(1)}, u32[]{:S(2)}, u32[]{:S(2)}) collective-permute-start(bf16[512,128]{1,0:T(8,128)(2,1)S(1)} %attend.3.rest_4_), channel_id=1, source_target_pairs={{0,1},{1,0},{2,3},{3,2},{4,5},{5,4},{6,7},{7,6},{8,9},{9,8},{10,11... | collective-permute-start | bytes 393224 | tf_op jit(solution)/shard_map/ppermute | solution.py:42
  95.2 15.5 %collective-permute-start.23 = (bf16[512,128]{1,0:T(8,128)(2,1)S(1)}, bf16[512,128]{1,0:T(8,128)(2,1)S(1)}, u32[]{:S(2)}, u32[]{:S(2)}) collective-permute-start(bf16[512,128]{1,0:T(8,128)(2,1)S(1)} %get-tuple-element.34), channel_id=1, source_target_pairs={{0,4},{1,5},{2,6},{3,7},{4,0},{5,1},{6,2},{7,3},{8,12},{9,13},{10,... | collective-permute-start | bytes 393224 | tf_op jit(solution)/shard_map/ppermute | solution.py:42
  106.1 6.4 %collective-permute-start.27 = (bf16[512,128]{1,0:T(8,128)(2,1)S(1)}, bf16[512,128]{1,0:T(8,128)(2,1)S(1)}, u32[]{:S(2)}, u32[]{:S(2)}) collective-permute-start(bf16[512,128]{1,0:T(8,128)(2,1)S(1)} %attend.3.rest_4_), channel_id=1, source_target_pairs={{0,2},{1,3},{2,0},{3,1},{4,6},{5,7},{6,4},{7,5},{8,10},{9,11},{10,... | collective-permute-start | bytes 393224 | tf_op jit(solution)/shard_map/ppermute | solution.py:42
  106.1 10.1 %collective-permute-start.11 = (bf16[512,128]{1,0:T(8,128)(2,1)S(1)}, bf16[512,128]{1,0:T(8,128)(2,1)S(1)}, u32[]{:S(2)}, u32[]{:S(2)}) collective-permute-start(bf16[512,128]{1,0:T(8,128)(2,1)S(1)} %collective-permute-done.9.rest_0_), channel_id=1, source_target_pairs={{0,2},{1,3},{2,0},{3,1},{4,6},{5,7},{6,4},{7,5},{8,10},{9,11},{10,... | collective-permute-start | bytes 393224 | tf_op jit(solution)/shard_map/ppermute | solution.py:42
  108.1 18.8 %collective-permute-start.31 = (bf16[512,256]{1,0:T(8,128)(2,1)S(1)}, bf16[512,256]{1,0:T(8,128)(2,1)S(1)}, u32[]{:S(2)}, u32[]{:S(2)}) collective-permute-start(bf16[512,256]{1,0:T(8,128)(2,1)S(1)} %collective-permute-done.30.rest_2_), channel_id=1, source_target_pairs={{0,1},{1,0},{2,3},{3,2},{4,5},{5,4},{6,7},{7,6},{8,9},{9,8},{10,11... | collective-permute-start | bytes 786440 | tf_op jit(solution)/shard_map/ppermute | solution.py:42
  110.8 8.2 %collective-permute-start.20 = (bf16[512,128]{1,0:T(8,128)(2,1)S(1)}, bf16[512,128]{1,0:T(8,128)(2,1)S(1)}, u32[]{:S(2)}, u32[]{:S(2)}) collective-permute-start(bf16[512,128]{1,0:T(8,128)(2,1)S(1)} %collective-permute-done.19.rest_5_), channel_id=1, source_target_pairs={{0,4},{1,5},{2,6},{3,7},{4,0},{5,1},{6,2},{7,3},{8,12},{9,13},{10,... | collective-permute-start | bytes 393224 | tf_op jit(solution)/shard_map/ppermute | solution.py:42
  112.4 8.4 %collective-permute-start.25 = (bf16[512,128]{1,0:T(8,128)(2,1)S(1)}, bf16[512,128]{1,0:T(8,128)(2,1)S(1)}, u32[]{:S(2)}, u32[]{:S(2)}) collective-permute-start(bf16[512,128]{1,0:T(8,128)(2,1)S(1)} %collective-permute-done.23.rest_0_), channel_id=1, source_target_pairs={{0,2},{1,3},{2,0},{3,1},{4,6},{5,7},{6,4},{7,5},{8,10},{9,11},{10,... | collective-permute-start | bytes 393224 | tf_op jit(solution)/shard_map/ppermute | solution.py:42
  112.7 10.9 %collective-permute-start.24 = (bf16[512,128]{1,0:T(8,128)(2,1)S(1)}, bf16[512,128]{1,0:T(8,128)(2,1)S(1)}, u32[]{:S(2)}, u32[]{:S(2)}) collective-permute-start(bf16[512,128]{1,0:T(8,128)(2,1)S(1)} %collective-permute-done.23.rest_0_), channel_id=1, source_target_pairs={{0,1},{1,0},{2,3},{3,2},{4,5},{5,4},{6,7},{7,6},{8,9},{9,8},{10,11... | collective-permute-start | bytes 393224 | tf_op jit(solution)/shard_map/ppermute | solution.py:42
  116.2 7.4 %collective-permute-start.28 = (bf16[512,128]{1,0:T(8,128)(2,1)S(1)}, bf16[512,128]{1,0:T(8,128)(2,1)S(1)}, u32[]{:S(2)}, u32[]{:S(2)}) collective-permute-start(bf16[512,128]{1,0:T(8,128)(2,1)S(1)} %collective-permute-done.19.rest_5_), channel_id=1, source_target_pairs={{0,2},{1,3},{2,0},{3,1},{4,6},{5,7},{6,4},{7,5},{8,10},{9,11},{10,... | collective-permute-start | bytes 393224 | tf_op jit(solution)/shard_map/ppermute | solution.py:42
  119.0 11.0 %collective-permute-start.10 = (bf16[512,128]{1,0:T(8,128)(2,1)S(1)}, bf16[512,128]{1,0:T(8,128)(2,1)S(1)}, u32[]{:S(2)}, u32[]{:S(2)}) collective-permute-start(bf16[512,128]{1,0:T(8,128)(2,1)S(1)} %collective-permute-done.9.rest_0_), channel_id=1, source_target_pairs={{0,1},{1,0},{2,3},{3,2},{4,5},{5,4},{6,7},{7,6},{8,9},{9,8},{10,11... | collective-permute-start | bytes 393224 | tf_op jit(solution)/shard_map/ppermute | solution.py:42
  120.9 7.6 %collective-permute-start.26 = (bf16[512,128]{1,0:T(8,128)(2,1)S(1)}, bf16[512,128]{1,0:T(8,128)(2,1)S(1)}, u32[]{:S(2)}, u32[]{:S(2)}) collective-permute-start(bf16[512,128]{1,0:T(8,128)(2,1)S(1)} %collective-permute-done.25.rest_2_), channel_id=1, source_target_pairs={{0,1},{1,0},{2,3},{3,2},{4,5},{5,4},{6,7},{7,6},{8,9},{9,8},{10,11... | collective-permute-start | bytes 393224 | tf_op jit(solution)/shard_map/ppermute | solution.py:42
  123.5 6.5 %collective-permute-start.21 = (bf16[512,128]{1,0:T(8,128)(2,1)S(1)}, bf16[512,128]{1,0:T(8,128)(2,1)S(1)}, u32[]{:S(2)}, u32[]{:S(2)}) collective-permute-start(bf16[512,128]{1,0:T(8,128)(2,1)S(1)} %collective-permute-done.18.rest_4_), channel_id=1, source_target_pairs={{0,2},{1,3},{2,0},{3,1},{4,6},{5,7},{6,4},{7,5},{8,10},{9,11},{10,... | collective-permute-start | bytes 393224 | tf_op jit(solution)/shard_map/ppermute | solution.py:42
  123.6 6.5 %collective-permute-start.12 = (bf16[512,128]{1,0:T(8,128)(2,1)S(1)}, bf16[512,128]{1,0:T(8,128)(2,1)S(1)}, u32[]{:S(2)}, u32[]{:S(2)}) collective-permute-start(bf16[512,128]{1,0:T(8,128)(2,1)S(1)} %collective-permute-done.11.rest_2_), channel_id=1, source_target_pairs={{0,1},{1,0},{2,3},{3,2},{4,5},{5,4},{6,7},{7,6},{8,9},{9,8},{10,11... | collective-permute-start | bytes 393224 | tf_op jit(solution)/shard_map/ppermute | solution.py:42
  126.9 5.0 %collective-permute-start.22 = (bf16[512,128]{1,0:T(8,128)(2,1)S(1)}, bf16[512,128]{1,0:T(8,128)(2,1)S(1)}, u32[]{:S(2)}, u32[]{:S(2)}) collective-permute-start(bf16[512,128]{1,0:T(8,128)(2,1)S(1)} %collective-permute-done.20.rest_5_), channel_id=1, source_target_pairs={{0,2},{1,3},{2,0},{3,1},{4,6},{5,7},{6,4},{7,5},{8,10},{9,11},{10,... | collective-permute-start | bytes 393224 | tf_op jit(solution)/shard_map/ppermute | solution.py:42
  128.4 3.4 %copy-start.3 = (f32[8,768]{1,0:T(8,128)S(1)}, f32[8,768]{1,0:T(8,128)}, u32[]{:S(2)}) copy-start(f32[8,768]{1,0:T(8,128)} %get-tuple-element.36.rest_9_) | copy-start | bytes 73732

commit v5 on v4

--- a/solution.py
+++ b/solution.py
@@ -53,11 +53,7 @@
         return [(value, 0)], [[] for _ in heads]
     near = both(value, 0)
     if group == 8:
-        pair = send(value, 2)
-        if across_first:
-            near += [(pair, 2), (send(near[1][0], 2), 3)]
-        else:
-            near += both(pair, 2)
+        near += both(send(value, 2), 2)
     far = []
     for head, block in enumerate(heads):
         pieces = []
@@ -470,8 +466,11 @@
         close, distant = spread(attended, singles, group, index == len(chunks) - 1)
         groups[index] += [(value, step, low) for value, step in close]
         for head, pieces in enumerate(distant):
-            late = min(index + (1 if head < len(distant) - 1 else 2), len(chunks))
-            groups[late] += [(value, step, low + head * HD) for value, step in pieces]
+            for number, (value, step) in enumerate(pieces):
+                ended = number == len(pieces) - 1
+                late = len(chunks) if ended and index >= len(chunks) - 2 else index + 1
+                late = late if ended else min(late, len(chunks) - 1)
+                groups[late].append((value, step, low + head * HD))
 
     groups = [entries for entries in groups if entries]
     result = None

time: 135 us -> 129 us (0.956)
  waiting for transfers between devices: 43.8 us -> 40.1 us
  starting transfers between devices: 67.2 us -> 65.5 us
    ppermute x29, waiting for transfers between devices: 43.7 us -> 40.1 us  [xor_permute(): return lax.ppermute(value, 'tp', pairs)]
    ppermute x29, starting transfers between devices: 67 us -> 65.3 us  [xor_permute(): return lax.ppermute(value, 'tp', pairs)]
  transfers between devices with their start and end apart: 32 -> 32, of which waited for: 12 -> 9; matrix products, arithmetic and copies ran while one was open for 0% -> 0% of each run, Pallas kernels for 11% -> 11%
where the time goes in v5:
time: 129 us
  starting transfers between devices  65.5 us (51%)
  waiting for transfers between devices  40.1 us (31%)
  Pallas kernels  20.7 us (16%)
  between operations  1.7 us (1%)
    ppermute x29, starting transfers between devices, xor_permute(): return lax.ppermute(value, 'tp', pairs)  65.3 us
    ppermute x29, waiting for transfers between devices, xor_permute(): return lax.ppermute(value, 'tp', pairs)  40.1 us
    pallas_call x2, Pallas kernels, attention(): pl.pallas_call(body, out_shape=outs, in_specs=[SMEM] + [VMEM] * (1 + len(...  8.4 us
    pallas_call x2, Pallas kernels, pack(): pl.pallas_call(functools.partial(pack_body, half=half, rows=rows, width=w...  6.04 us
    pallas_call x3, Pallas kernels, project(): pl.pallas_call(functools.partial(project_body, rows=rows, last=last, firs...  5.67 us
  transfers between devices with their start and end apart: 32, of which 9 were waited for; matrix products, arithmetic and copies ran while one was open for 0% of the time, Pallas kernels for 11%

profile of v5, /device:TPU:0, one launch (start us, length us, event | category | flops | bytes accessed | tf_op | source)
XLA Modules:
  0.0 129.2 jit_solution(738048782063128692)
XLA Ops:
  1.3 0.6 stack.16.place.rest_0_
  1.9 4.0 %pack.2 = (f32[8,768]{1,0:T(8,128)}, bf16[448,384]{1,0:T(8,128)(2,1)}, bf16[448,384]{1,0:T(8,128)(2,1)}, bf16[448,384]{1,0:T(8,128)(2,1)}, bf16[448,384]{1,0:T(8...) custom-call(s32[5]{0:T(128)} %stack.16.place.rest_0_, ...), custom_call_target="tpu_custom_call" | custom-call | tf_op jit(solution)/shard_map/pack/pallas_call | solution.py:144
  5.9 4.1 %collective-permute-start.2 = (bf16[448,384]{1,0:T(8,128)(2,1)}, bf16[448,384]{1,0:T(8,128)(2,1)S(1)}, u32[]{:S(2)}, u32[]{:S(2)}) collective-permute-start(bf16[448,384]{1,0:T(8,128)(2,1)} %get-tuple-element.24), channel_id=1, source_target_pairs={{0,3},{1,2},{2,1},{3,0},{4,7},{5,6},{6,5},{7,4},{8,11},{9,10},{10,... | collective-permute-start | bytes 1032200 | tf_op jit(solution)/shard_map/ppermute | solution.py:42
  9.9 0.4 collective-permute-start.1
  10.4 0.2 collective-permute-start
  10.6 2.1 %pack.3 = (bf16[448,256]{1,0:T(8,128)(2,1)}, bf16[448,256]{1,0:T(8,128)(2,1)}, bf16[448,256]{1,0:T(8,128)(2,1)}, bf16[448,256]{1,0:T(8,128)(2,1)}) custom-call(bf16[64,3072]{1,0:T(8,128)(2,1)} %bitcast.11, bf16[2,64,3072]{2,1,0:T(8,128)(2,1)} %bitcast.9, bf16[2,256,3072]{2,1,0:T(8,128)(2,1)} %rest_2_.1), custom_call_target="tpu_custom_call" | custom-call | tf_op jit(solution)/shard_map/pack/pallas_call | solution.py:144
  12.7 3.0 %collective-permute-start.3 = (bf16[448,256]{1,0:T(8,128)(2,1)}, bf16[448,256]{1,0:T(8,128)(2,1)S(1)}, u32[]{:S(2)}, u32[]{:S(2)}) collective-permute-start(bf16[448,256]{1,0:T(8,128)(2,1)} %get-tuple-element.25), channel_id=1, source_target_pairs={{0,4},{1,5},{2,6},{3,7},{4,0},{5,1},{6,2},{7,3},{8,12},{9,13},{10,... | collective-permute-start | bytes 688136 | tf_op jit(solution)/shard_map/ppermute | solution.py:42
  15.7 1.3 collective-permute-start.4
  17.0 12.0 %collective-permute-done.2.rest_3_ = bf16[448,384]{1,0:T(8,128)(2,1)S(1)} collective-permute-done((bf16[448,384]{1,0:T(8,128)(2,1)}, bf16[448,384]{1,0:T(8,128)(2,1)S(1)}, u32[]{:S(2)}, u32[]{:S(2)}) %collective-permute-start.2) | collective-permute-done | bytes 344096 | tf_op jit(solution)/shard_map/ppermute | solution.py:42
  29.0 3.0 %collective-permute-start.5 = (bf16[448,256]{1,0:T(8,128)(2,1)}, bf16[448,256]{1,0:T(8,128)(2,1)S(1)}, u32[]{:S(2)}, u32[]{:S(2)}) collective-permute-start(bf16[448,256]{1,0:T(8,128)(2,1)} %get-tuple-element.27), channel_id=1, source_target_pairs={{0,6},{1,7},{2,4},{3,5},{4,2},{5,3},{6,0},{7,1},{8,14},{9,15},{10,... | collective-permute-start | bytes 688136 | tf_op jit(solution)/shard_map/ppermute | solution.py:42
  32.0 3.6 %collective-permute-done.1.rest_2_ = bf16[448,384]{1,0:T(8,128)(2,1)S(1)} collective-permute-done((bf16[448,384]{1,0:T(8,128)(2,1)}, bf16[448,384]{1,0:T(8,128)(2,1)S(1)}, u32[]{:S(2)}, u32[]{:S(2)}) %collective-permute-start.1) | collective-permute-done | bytes 344096 | tf_op jit(solution)/shard_map/ppermute | solution.py:42
  35.7 2.9 %collective-permute-start.6 = (bf16[448,256]{1,0:T(8,128)(2,1)}, bf16[448,256]{1,0:T(8,128)(2,1)S(1)}, u32[]{:S(2)}, u32[]{:S(2)}) collective-permute-start(bf16[448,256]{1,0:T(8,128)(2,1)} %get-tuple-element.28), channel_id=1, source_target_pairs={{0,7},{1,6},{2,5},{3,4},{4,3},{5,2},{6,1},{7,0},{8,15},{9,14},{10,... | collective-permute-start | bytes 688136 | tf_op jit(solution)/shard_map/ppermute | solution.py:42
  38.7 0.1 pad_maximum_fusion
  38.8 0.1 collective-permute-start.7
  38.9 8.6 %collective-permute-done.6.rest_7_ = bf16[448,256]{1,0:T(8,128)(2,1)S(1)} collective-permute-done((bf16[448,256]{1,0:T(8,128)(2,1)}, bf16[448,256]{1,0:T(8,128)(2,1)S(1)}, u32[]{:S(2)}, u32[]{:S(2)}) %collective-permute-start.6) | collective-permute-done | bytes 229408 | tf_op jit(solution)/shard_map/ppermute | solution.py:42
  47.6 0.0 collective-permute-done.4.rest_5_
  47.6 0.0 collective-permute-done.3.rest_4_
  47.7 0.0 copy-start.4
  47.7 0.1 pad_maximum_fusion.1
  47.7 0.1 collective-permute-start.8
  47.8 2.5 %collective-permute-start.18 = (bf16[448,128]{1,0:T(8,128)(2,1)S(1)}, bf16[448,128]{1,0:T(8,128)(2,1)S(1)}, u32[]{:S(2)}, u32[]{:S(2)}) collective-permute-start(bf16[448,128]{1,0:T(8,128)(2,1)S(1)} %copy-done.8), channel_id=1, source_target_pairs={{0,7},{1,6},{2,5},{3,4},{4,3},{5,2},{6,1},{7,0},{8,15},{9,14},{10,... | collective-permute-start | bytes 344072 | tf_op jit(solution)/shard_map/ppermute | solution.py:42
  50.3 8.3 %collective-permute-start.17 = (bf16[448,128]{1,0:T(8,128)(2,1)S(1)}, bf16[448,128]{1,0:T(8,128)(2,1)S(1)}, u32[]{:S(2)}, u32[]{:S(2)}) collective-permute-start(bf16[448,128]{1,0:T(8,128)(2,1)S(1)} %copy-done.7), channel_id=1, source_target_pairs={{0,6},{1,7},{2,4},{3,5},{4,2},{5,3},{6,0},{7,1},{8,14},{9,15},{10,... | collective-permute-start | bytes 344072 | tf_op jit(solution)/shard_map/ppermute | solution.py:42
  58.6 4.5 %collective-permute-start.16 = (bf16[448,128]{1,0:T(8,128)(2,1)S(1)}, bf16[448,128]{1,0:T(8,128)(2,1)S(1)}, u32[]{:S(2)}, u32[]{:S(2)}) collective-permute-start(bf16[448,128]{1,0:T(8,128)(2,1)S(1)} %copy-done.6), channel_id=1, source_target_pairs={{0,5},{1,4},{2,7},{3,6},{4,1},{5,0},{6,3},{7,2},{8,13},{9,12},{10,... | collective-permute-start | bytes 344072 | tf_op jit(solution)/shard_map/ppermute | solution.py:42
  63.1 0.0 collective-permute-done.18.rest_7_
  63.1 10.2 %collective-permute-start.15 = (bf16[448,128]{1,0:T(8,128)(2,1)S(1)}, bf16[448,128]{1,0:T(8,128)(2,1)S(1)}, u32[]{:S(2)}, u32[]{:S(2)}) collective-permute-start(bf16[448,128]{1,0:T(8,128)(2,1)S(1)} %copy-done.5), channel_id=1, source_target_pairs={{0,4},{1,5},{2,6},{3,7},{4,0},{5,1},{6,2},{7,3},{8,12},{9,13},{10,... | collective-permute-start | bytes 344072 | tf_op jit(solution)/shard_map/ppermute | solution.py:42
  73.3 5.5 %collective-permute-done.16.rest_5_ = bf16[448,128]{1,0:T(8,128)(2,1)S(1)} collective-permute-done((bf16[448,128]{1,0:T(8,128)(2,1)S(1)}, bf16[448,128]{1,0:T(8,128)(2,1)S(1)}, u32[]{:S(2)}, u32[]{:S(2)}) %collective-permute-start.16) | collective-permute-done | bytes 114720 | tf_op jit(solution)/shard_map/ppermute | solution.py:42
  78.7 0.7 collective-permute-done.15.rest_4_
  79.5 0.1 collective-permute-start.19
  79.6 0.6 bias.1.bias_ref
  80.2 0.0 collective-permute-done.8.rest_9_
  80.3 0.0 collective-permute-done.7.rest_8_
  80.3 5.4 %attend.2 = (bf16[512,256]{1,0:T(8,128)(2,1)S(1)}, bf16[512,128]{1,0:T(8,128)(2,1)S(1)}, bf16[512,128]{1,0:T(8,128)(2,1)S(1)}) custom-call(s32[5]{0:T(128)S(1)} %copy-done.2, f32[4,1,3072]{2,1,0:T(1,128)S(1)} %bias.1.bias_ref, bf16[448,384]{1,0:T(8,128)(2,1)S(1)} %copy-done.1, bf16[448,384]{1,0:T(8,128)(2,1)S(1)} %collective-permute-done.rest_1_, ...), custom_call_target="tpu_custom_call" | custom-call | tf_op jit(solution)/shard_map/attend/pallas_call | solution.py:275
  85.6 0.1 collective-permute-start.30
  85.7 2.6 %collective-permute-start.9 = (bf16[512,128]{1,0:T(8,128)(2,1)S(1)}, bf16[512,128]{1,0:T(8,128)(2,1)S(1)}, u32[]{:S(2)}, u32[]{:S(2)}) collective-permute-start(bf16[512,128]{1,0:T(8,128)(2,1)S(1)} %get-tuple-element.29), channel_id=1, source_target_pairs={{0,4},{1,5},{2,6},{3,7},{4,0},{5,1},{6,2},{7,3},{8,12},{9,13},{10,... | collective-permute-start | bytes 393224 | tf_op jit(solution)/shard_map/ppermute | solution.py:42
  88.4 0.3 collective-permute-start.12
  88.7 2.3 %collective-permute-start.29 = (bf16[512,256]{1,0:T(8,128)(2,1)S(1)}, bf16[512,256]{1,0:T(8,128)(2,1)S(1)}, u32[]{:S(2)}, u32[]{:S(2)}) collective-permute-start(bf16[512,256]{1,0:T(8,128)(2,1)S(1)} %get-tuple-element.35.rest_0_), channel_id=1, source_target_pairs={{0,1},{1,0},{2,3},{3,2},{4,5},{5,4},{6,7},{7,6},{8,9},{9,8},{10,11... | collective-permute-start | bytes 786440 | tf_op jit(solution)/shard_map/ppermute | solution.py:42
  91.0 0.0 collective-permute-done.19.rest_9_
  91.1 3.0 %attend.3.rest_6_ = bf16[512,128]{1,0:T(8,128)(2,1)S(1)} custom-call(s32[5]{0:T(128)S(1)} %copy-done.2, f32[4,1,3072]{2,1,0:T(1,128)S(1)} %bias.1.bias_ref, bf16[448,384]{1,0:T(8,128)(2,1)S(1)} %copy-done.1, bf16[448,384]{1,0:T(8,128)(2,1)S(1)} %collective-permute-done.rest_1_, bf16[448,384]{1,0:T(8,128)(2,1)S(1)} %collective-permute-done.1.rest_2_, ...), custom_call_target="tpu_custom_call" | custom-call | tf_op jit(solution)/shard_map/attend/pallas_call | solution.py:275
  94.1 0.1 collective-permute-start.20
  94.2 1.1 collective-permute-done.9.rest_0_
  95.3 3.2 %collective-permute-start.25 = (bf16[512,128]{1,0:T(8,128)(2,1)S(1)}, bf16[512,128]{1,0:T(8,128)(2,1)S(1)}, u32[]{:S(2)}, u32[]{:S(2)}) collective-permute-start(bf16[512,128]{1,0:T(8,128)(2,1)S(1)} %attend.3.rest_6_), channel_id=1, source_target_pairs={{0,2},{1,3},{2,0},{3,1},{4,6},{5,7},{6,4},{7,5},{8,10},{9,11},{10,... | collective-permute-start | bytes 393224 | tf_op jit(solution)/shard_map/ppermute | solution.py:42
  98.4 2.7 %collective-permute-done.12.rest_3_ = bf16[512,128]{1,0:T(8,128)(2,1)S(1)} collective-permute-done((bf16[512,128]{1,0:T(8,128)(2,1)S(1)}, bf16[512,128]{1,0:T(8,128)(2,1)S(1)}, u32[]{:S(2)}, u32[]{:S(2)}) %collective-permute-start.12) | collective-permute-done | bytes 131104 | tf_op jit(solution)/shard_map/ppermute | solution.py:42
  101.1 0.2 collective-permute-start.27
  101.3 2.5 %collective-permute-start.10 = (bf16[512,128]{1,0:T(8,128)(2,1)S(1)}, bf16[512,128]{1,0:T(8,128)(2,1)S(1)}, u32[]{:S(2)}, u32[]{:S(2)}) collective-permute-start(bf16[512,128]{1,0:T(8,128)(2,1)S(1)} %collective-permute-done.9.rest_0_), channel_id=1, source_target_pairs={{0,2},{1,3},{2,0},{3,1},{4,6},{5,7},{6,4},{7,5},{8,10},{9,11},{10,... | collective-permute-start | bytes 393224 | tf_op jit(solution)/shard_map/ppermute | solution.py:42
  103.8 2.7 %collective-permute-start.31 = (bf16[512,256]{1,0:T(8,128)(2,1)S(1)}, bf16[512,256]{1,0:T(8,128)(2,1)S(1)}, u32[]{:S(2)}, u32[]{:S(2)}) collective-permute-start(bf16[512,256]{1,0:T(8,128)(2,1)S(1)} %collective-permute-done.30.rest_2_), channel_id=1, source_target_pairs={{0,1},{1,0},{2,3},{3,2},{4,5},{5,4},{6,7},{7,6},{8,9},{9,8},{10,11... | collective-permute-start | bytes 786440 | tf_op jit(solution)/shard_map/ppermute | solution.py:42
  106.5 0.0 collective-permute-done.25.rest_8_
  106.5 0.1 collective-permute-start.13
  106.5 3.0 %collective-permute-done.27.rest_10_ = bf16[512,128]{1,0:T(8,128)(2,1)S(1)} collective-permute-done((bf16[512,128]{1,0:T(8,128)(2,1)S(1)}, bf16[512,128]{1,0:T(8,128)(2,1)S(1)}, u32[]{:S(2)}, u32[]{:S(2)}) %collective-permute-start.27) | collective-permute-done | bytes 131104 | tf_op jit(solution)/shard_map/ppermute | solution.py:42
  109.5 1.8 %collective-permute-start.23 = (bf16[512,128]{1,0:T(8,128)(2,1)S(1)}, bf16[512,128]{1,0:T(8,128)(2,1)S(1)}, u32[]{:S(2)}, u32[]{:S(2)}) collective-permute-start(bf16[512,128]{1,0:T(8,128)(2,1)S(1)} %collective-permute-done.9.rest_0_), channel_id=1, source_target_pairs={{0,1},{1,0},{2,3},{3,2},{4,5},{5,4},{6,7},{7,6},{8,9},{9,8},{10,11... | collective-permute-start | bytes 393224 | tf_op jit(solution)/shard_map/ppermute | solution.py:42
  111.3 2.0 %collective-permute-start.24 = (bf16[512,128]{1,0:T(8,128)(2,1)S(1)}, bf16[512,128]{1,0:T(8,128)(2,1)S(1)}, u32[]{:S(2)}, u32[]{:S(2)}) collective-permute-start(bf16[512,128]{1,0:T(8,128)(2,1)S(1)} %collective-permute-done.12.rest_3_), channel_id=1, source_target_pairs={{0,1},{1,0},{2,3},{3,2},{4,5},{5,4},{6,7},{7,6},{8,9},{9,8},{10,11... | collective-permute-start | bytes 393224 | tf_op jit(solution)/shard_map/ppermute | solution.py:42
  113.3 1.7 %collective-permute-start.26 = (bf16[512,128]{1,0:T(8,128)(2,1)S(1)}, bf16[512,128]{1,0:T(8,128)(2,1)S(1)}, u32[]{:S(2)}, u32[]{:S(2)}) collective-permute-start(bf16[512,128]{1,0:T(8,128)(2,1)S(1)} %collective-permute-done.25.rest_8_), channel_id=1, source_target_pairs={{0,1},{1,0},{2,3},{3,2},{4,5},{5,4},{6,7},{7,6},{8,9},{9,8},{10,11... | collective-permute-start | bytes 393224 | tf_op jit(solution)/shard_map/ppermute | solution.py:42
  115.0 2.8 %collective-permute-done.21.rest_11_ = bf16[512,128]{1,0:T(8,128)(2,1)S(1)} collective-permute-done((bf16[512,128]{1,0:T(8,128)(2,1)S(1)}, bf16[512,128]{1,0:T(8,128)(2,1)S(1)}, u32[]{:S(2)}, u32[]{:S(2)}) %collective-permute-start.21) | collective-permute-done | bytes 131104 | tf_op jit(solution)/shard_map/ppermute | solution.py:42
  117.9 0.0 collective-permute-start.28
  117.9 1.3 collective-permute-start.11
  119.1 0.0 collective-permute-done.24.rest_4_
  119.1 1.4 %collective-permute-start.14 = (bf16[512,128]{1,0:T(8,128)(2,1)S(1)}, bf16[512,128]{1,0:T(8,128)(2,1)S(1)}, u32[]{:S(2)}, u32[]{:S(2)}) collective-permute-start(bf16[512,128]{1,0:T(8,128)(2,1)S(1)} %collective-permute-done.13.rest_5_), channel_id=1, source_target_pairs={{0,1},{1,0},{2,3},{3,2},{4,5},{5,4},{6,7},{7,6},{8,9},{9,8},{10,11... | collective-permute-start | bytes 393224 | tf_op jit(solution)/shard_map/ppermute | solution.py:42
  120.5 0.0 collective-permute-done.31.rest_3_
  120.5 2.9 %collective-permute-start.22 = (bf16[512,128]{1,0:T(8,128)(2,1)S(1)}, bf16[512,128]{1,0:T(8,128)(2,1)S(1)}, u32[]{:S(2)}, u32[]{:S(2)}) collective-permute-start(bf16[512,128]{1,0:T(8,128)(2,1)S(1)} %collective-permute-done.21.rest_11_), channel_id=1, source_target_pairs={{0,2},{1,3},{2,0},{3,1},{4,6},{5,7},{6,4},{7,5},{8,10},{9,11},{10,... | collective-permute-start | bytes 393224 | tf_op jit(solution)/shard_map/ppermute | solution.py:42
  123.4 1.5 %project.3.rest_13_ = f32[512,768]{1,0:T(8,128)S(1)} custom-call(s32[5]{0:T(128)S(1)} %copy-done.2, bf16[3072,768]{1,0:T(8,128)(2,1)S(1)} %copy-done, bf16[512,256]{1,0:T(8,128)(2,1)S(1)} %get-tuple-element.35.rest_0_, bf16[512,256]{1,0:T(8,128)(2,1)S(1)} %collective-permute-done.29.rest_1_, bf16[512,256]{1,0:T(8,128)(2,1)S(1)} %collective-permute-done.30.rest_2_, ...), custom_call_target="tpu_custom_call" | custom-call | tf_op jit(solution)/shard_map/project/pallas_call | solution.py:317
  125.0 0.0 collective-permute-done.28.rest_12_
  125.0 2.1 %project.4.rest_3_ = f32[512,768]{1,0:T(8,128)S(1)} custom-call(s32[5]{0:T(128)S(1)} %copy-done.2, bf16[3072,768]{1,0:T(8,128)(2,1)S(1)} %copy-done, bf16[512,128]{1,0:T(8,128)(2,1)S(1)} %collective-permute-done.9.rest_0_, bf16[512,128]{1,0:T(8,128)(2,1)S(1)} %collective-permute-done.23.rest_1_, bf16[512,128]{1,0:T(8,128)(2,1)S(1)} %collective-permute-done.10.rest_2_, ...), custom_call_target="tpu_custom_call" | custom-call | tf_op jit(solution)/shard_map/project/pallas_call | solution.py:317
  127.1 0.0 collective-permute-done.11.rest_0_
  127.1 0.0 collective-permute-done.22.rest_2_
  127.2 2.0 %project.5 = bf16[512,768]{1,0:T(8,128)(2,1)} custom-call(s32[5]{0:T(128)S(1)} %copy-done.2, bf16[3072,768]{1,0:T(8,128)(2,1)S(1)} %copy-done, bf16[512,128]{1,0:T(8,128)(2,1)S(1)} %collective-permute-done.11.rest_0_, bf16[512,128]{1,0:T(8,128)(2,1)S(1)} %collective-permute-done.14.rest_1_, bf16[512,128]{1,0:T(8,128)(2,1)S(1)} %collective-permute-done.22.rest_2_, ...), custom_call_target="tpu_custom_call" | custom-call | tf_op jit(solution)/shard_map/project/pallas_call | solution.py:317
  (43 shorter events, 0.3 us)
Async XLA Ops:
  5.9 23.1 %collective-permute-start.2 = (bf16[448,384]{1,0:T(8,128)(2,1)}, bf16[448,384]{1,0:T(8,128)(2,1)S(1)}, u32[]{:S(2)}, u32[]{:S(2)}) collective-permute-start(bf16[448,384]{1,0:T(8,128)(2,1)} %get-tuple-element.24), channel_id=1, source_target_pairs={{0,3},{1,2},{2,1},{3,0},{4,7},{5,6},{6,5},{7,4},{8,11},{9,10},{10,... | collective-permute-start | bytes 1032200 | tf_op jit(solution)/shard_map/ppermute | solution.py:42
  9.9 25.7 %collective-permute-start.1 = (bf16[448,384]{1,0:T(8,128)(2,1)}, bf16[448,384]{1,0:T(8,128)(2,1)S(1)}, u32[]{:S(2)}, u32[]{:S(2)}) collective-permute-start(bf16[448,384]{1,0:T(8,128)(2,1)} %get-tuple-element.23), channel_id=1, source_target_pairs={{0,2},{1,3},{2,0},{3,1},{4,6},{5,7},{6,4},{7,5},{8,10},{9,11},{10,... | collective-permute-start | bytes 1032200 | tf_op jit(solution)/shard_map/ppermute | solution.py:42
  10.4 6.6 %copy-start.1 = (bf16[448,384]{1,0:T(8,128)(2,1)S(1)}, bf16[448,384]{1,0:T(8,128)(2,1)}, u32[]{:S(2)}) copy-start(bf16[448,384]{1,0:T(8,128)(2,1)} %get-tuple-element.21.rest_0_) | copy-start | bytes 1032196
  10.4 28.2 %collective-permute-start = (bf16[448,384]{1,0:T(8,128)(2,1)}, bf16[448,384]{1,0:T(8,128)(2,1)S(1)}, u32[]{:S(2)}, u32[]{:S(2)}) collective-permute-start(bf16[448,384]{1,0:T(8,128)(2,1)} %get-tuple-element.22), channel_id=1, source_target_pairs={{0,1},{1,0},{2,3},{3,2},{4,5},{5,4},{6,7},{7,6},{8,9},{9,8},{10,11... | collective-permute-start | bytes 1032200 | tf_op jit(solution)/shard_map/ppermute | solution.py:42
  12.7 34.9 %collective-permute-start.3 = (bf16[448,256]{1,0:T(8,128)(2,1)}, bf16[448,256]{1,0:T(8,128)(2,1)S(1)}, u32[]{:S(2)}, u32[]{:S(2)}) collective-permute-start(bf16[448,256]{1,0:T(8,128)(2,1)} %get-tuple-element.25), channel_id=1, source_target_pairs={{0,4},{1,5},{2,6},{3,7},{4,0},{5,1},{6,2},{7,3},{8,12},{9,13},{10,... | collective-permute-start | bytes 688136 | tf_op jit(solution)/shard_map/ppermute | solution.py:42
  15.7 31.9 %collective-permute-start.4 = (bf16[448,256]{1,0:T(8,128)(2,1)}, bf16[448,256]{1,0:T(8,128)(2,1)S(1)}, u32[]{:S(2)}, u32[]{:S(2)}) collective-permute-start(bf16[448,256]{1,0:T(8,128)(2,1)} %get-tuple-element.26), channel_id=1, source_target_pairs={{0,5},{1,4},{2,7},{3,6},{4,1},{5,0},{6,3},{7,2},{8,13},{9,12},{10,... | collective-permute-start | bytes 688136 | tf_op jit(solution)/shard_map/ppermute | solution.py:42
  29.0 18.6 %collective-permute-start.5 = (bf16[448,256]{1,0:T(8,128)(2,1)}, bf16[448,256]{1,0:T(8,128)(2,1)S(1)}, u32[]{:S(2)}, u32[]{:S(2)}) collective-permute-start(bf16[448,256]{1,0:T(8,128)(2,1)} %get-tuple-element.27), channel_id=1, source_target_pairs={{0,6},{1,7},{2,4},{3,5},{4,2},{5,3},{6,0},{7,1},{8,14},{9,15},{10,... | collective-permute-start | bytes 688136 | tf_op jit(solution)/shard_map/ppermute | solution.py:42
  35.7 11.9 %collective-permute-start.6 = (bf16[448,256]{1,0:T(8,128)(2,1)}, bf16[448,256]{1,0:T(8,128)(2,1)S(1)}, u32[]{:S(2)}, u32[]{:S(2)}) collective-permute-start(bf16[448,256]{1,0:T(8,128)(2,1)} %get-tuple-element.28), channel_id=1, source_target_pairs={{0,7},{1,6},{2,5},{3,4},{4,3},{5,2},{6,1},{7,0},{8,15},{9,14},{10,... | collective-permute-start | bytes 688136 | tf_op jit(solution)/shard_map/ppermute | solution.py:42
  38.6 9.2 %copy-start.8 = (bf16[448,128]{1,0:T(8,128)(2,1)S(1)}, bf16[448,128]{1,0:T(8,128)(2,1)}, u32[]{:S(2)}) copy-start(bf16[448,128]{1,0:T(8,128)(2,1)} %get-tuple-element.34) | copy-start | bytes 344068
  38.6 11.6 %copy-start.7 = (bf16[448,128]{1,0:T(8,128)(2,1)S(1)}, bf16[448,128]{1,0:T(8,128)(2,1)}, u32[]{:S(2)}) copy-start(bf16[448,128]{1,0:T(8,128)(2,1)} %get-tuple-element.33) | copy-start | bytes 344068
  38.7 19.9 %copy-start.6 = (bf16[448,128]{1,0:T(8,128)(2,1)S(1)}, bf16[448,128]{1,0:T(8,128)(2,1)}, u32[]{:S(2)}) copy-start(bf16[448,128]{1,0:T(8,128)(2,1)} %get-tuple-element.32) | copy-start | bytes 344068
  38.7 24.4 %copy-start.5 = (bf16[448,128]{1,0:T(8,128)(2,1)S(1)}, bf16[448,128]{1,0:T(8,128)(2,1)}, u32[]{:S(2)}) copy-start(bf16[448,128]{1,0:T(8,128)(2,1)} %get-tuple-element.31) | copy-start | bytes 344068
  38.8 41.5 %collective-permute-start.7 = (bf16[1536,384]{1,0:T(8,128)(2,1)S(1)}, bf16[1536,384]{1,0:T(8,128)(2,1)S(1)}, u32[]{:S(2)}, u32[]{:S(2)}) collective-permute-start(bf16[1536,384]{1,0:T(8,128)(2,1)S(1)} %pad_maximum_fusion), channel_id=1, source_target_pairs={{0,8},{8,0},{1,9},{9,1},{2,10},{10,2},{3,11},{11,3},{4,12},{12,4},... | collective-permute-start | bytes 3538952 | tf_op jit(solution)/shard_map/ppermute | solution.py:80
  47.5 32.7 %copy-start = (bf16[3072,768]{1,0:T(8,128)(2,1)S(1)}, bf16[3072,768]{1,0:T(8,128)(2,1)}, u32[]{:S(2)}) copy-start(bf16[3072,768]{1,0:T(8,128)(2,1)} %weight.5) | copy-start | bytes 14155780
  47.6 31.9 %copy-start.2 = (s32[5]{0:T(128)S(1)}, s32[5]{0:T(128)}, u32[]{:S(2)}) copy-start(s32[5]{0:T(128)} %stack.16.place.rest_0_) | copy-start | bytes 64
  47.7 31.9 %copy-start.4 = (s32[1,4,8]{2,1,0:T(4,128)S(1)}, s32[1,4,8]{2,1,0:T(4,128)}, u32[]{:S(2)}) copy-start(s32[1,4,8]{2,1,0:T(4,128)} %param.11) | copy-start | bytes 388
  47.7 32.5 %collective-permute-start.8 = (bf16[1536,256]{1,0:T(8,128)(2,1)S(1)}, bf16[1536,256]{1,0:T(8,128)(2,1)S(1)}, u32[]{:S(2)}, u32[]{:S(2)}) collective-permute-start(bf16[1536,256]{1,0:T(8,128)(2,1)S(1)} %pad_maximum_fusion.1), channel_id=1, source_target_pairs={{0,8},{8,0},{1,9},{9,1},{2,10},{10,2},{3,11},{11,3},{4,12},{12,4},... | collective-permute-start | bytes 2359304 | tf_op jit(solution)/shard_map/ppermute | solution.py:80
  47.8 15.3 %collective-permute-start.18 = (bf16[448,128]{1,0:T(8,128)(2,1)S(1)}, bf16[448,128]{1,0:T(8,128)(2,1)S(1)}, u32[]{:S(2)}, u32[]{:S(2)}) collective-permute-start(bf16[448,128]{1,0:T(8,128)(2,1)S(1)} %copy-done.8), channel_id=1, source_target_pairs={{0,7},{1,6},{2,5},{3,4},{4,3},{5,2},{6,1},{7,0},{8,15},{9,14},{10,... | collective-permute-start | bytes 344072 | tf_op jit(solution)/shard_map/ppermute | solution.py:42
  50.3 23.0 %collective-permute-start.17 = (bf16[448,128]{1,0:T(8,128)(2,1)S(1)}, bf16[448,128]{1,0:T(8,128)(2,1)S(1)}, u32[]{:S(2)}, u32[]{:S(2)}) collective-permute-start(bf16[448,128]{1,0:T(8,128)(2,1)S(1)} %copy-done.7), channel_id=1, source_target_pairs={{0,6},{1,7},{2,4},{3,5},{4,2},{5,3},{6,0},{7,1},{8,14},{9,15},{10,... | collective-permute-start | bytes 344072 | tf_op jit(solution)/shard_map/ppermute | solution.py:42
  58.6 20.1 %collective-permute-start.16 = (bf16[448,128]{1,0:T(8,128)(2,1)S(1)}, bf16[448,128]{1,0:T(8,128)(2,1)S(1)}, u32[]{:S(2)}, u32[]{:S(2)}) collective-permute-start(bf16[448,128]{1,0:T(8,128)(2,1)S(1)} %copy-done.6), channel_id=1, source_target_pairs={{0,5},{1,4},{2,7},{3,6},{4,1},{5,0},{6,3},{7,2},{8,13},{9,12},{10,... | collective-permute-start | bytes 344072 | tf_op jit(solution)/shard_map/ppermute | solution.py:42
  63.1 16.4 %collective-permute-start.15 = (bf16[448,128]{1,0:T(8,128)(2,1)S(1)}, bf16[448,128]{1,0:T(8,128)(2,1)S(1)}, u32[]{:S(2)}, u32[]{:S(2)}) collective-permute-start(bf16[448,128]{1,0:T(8,128)(2,1)S(1)} %copy-done.5), channel_id=1, source_target_pairs={{0,4},{1,5},{2,6},{3,7},{4,0},{5,1},{6,2},{7,3},{8,12},{9,13},{10,... | collective-permute-start | bytes 344072 | tf_op jit(solution)/shard_map/ppermute | solution.py:42
  79.5 11.6 %collective-permute-start.19 = (bf16[1536,128]{1,0:T(8,128)(2,1)S(1)}, bf16[1536,128]{1,0:T(8,128)(2,1)S(1)}, u32[]{:S(2)}, u32[]{:S(2)}) collective-permute-start(bf16[1536,128]{1,0:T(8,128)(2,1)S(1)} %pad_maximum_fusion.2), channel_id=1, source_target_pairs={{0,8},{8,0},{1,9},{9,1},{2,10},{10,2},{3,11},{11,3},{4,12},{12,4},... | collective-permute-start | bytes 1179656 | tf_op jit(solution)/shard_map/ppermute | solution.py:80
  85.6 18.2 %collective-permute-start.30 = (bf16[512,256]{1,0:T(8,128)(2,1)S(1)}, bf16[512,256]{1,0:T(8,128)(2,1)S(1)}, u32[]{:S(2)}, u32[]{:S(2)}) collective-permute-start(bf16[512,256]{1,0:T(8,128)(2,1)S(1)} %get-tuple-element.35.rest_0_), channel_id=1, source_target_pairs={{0,2},{1,3},{2,0},{3,1},{4,6},{5,7},{6,4},{7,5},{8,10},{9,11},{10,... | collective-permute-start | bytes 786440 | tf_op jit(solution)/shard_map/ppermute | solution.py:42
  85.7 9.5 %collective-permute-start.9 = (bf16[512,128]{1,0:T(8,128)(2,1)S(1)}, bf16[512,128]{1,0:T(8,128)(2,1)S(1)}, u32[]{:S(2)}, u32[]{:S(2)}) collective-permute-start(bf16[512,128]{1,0:T(8,128)(2,1)S(1)} %get-tuple-element.29), channel_id=1, source_target_pairs={{0,4},{1,5},{2,6},{3,7},{4,0},{5,1},{6,2},{7,3},{8,12},{9,13},{10,... | collective-permute-start | bytes 393224 | tf_op jit(solution)/shard_map/ppermute | solution.py:42
  88.4 12.8 %collective-permute-start.12 = (bf16[512,128]{1,0:T(8,128)(2,1)S(1)}, bf16[512,128]{1,0:T(8,128)(2,1)S(1)}, u32[]{:S(2)}, u32[]{:S(2)}) collective-permute-start(bf16[512,128]{1,0:T(8,128)(2,1)S(1)} %get-tuple-element.30), channel_id=1, source_target_pairs={{0,4},{1,5},{2,6},{3,7},{4,0},{5,1},{6,2},{7,3},{8,12},{9,13},{10,... | collective-permute-start | bytes 393224 | tf_op jit(solution)/shard_map/ppermute | solution.py:42
  88.7 20.8 %collective-permute-start.29 = (bf16[512,256]{1,0:T(8,128)(2,1)S(1)}, bf16[512,256]{1,0:T(8,128)(2,1)S(1)}, u32[]{:S(2)}, u32[]{:S(2)}) collective-permute-start(bf16[512,256]{1,0:T(8,128)(2,1)S(1)} %get-tuple-element.35.rest_0_), channel_id=1, source_target_pairs={{0,1},{1,0},{2,3},{3,2},{4,5},{5,4},{6,7},{7,6},{8,9},{9,8},{10,11... | collective-permute-start | bytes 786440 | tf_op jit(solution)/shard_map/ppermute | solution.py:42
  94.1 7.2 %collective-permute-start.20 = (bf16[512,128]{1,0:T(8,128)(2,1)S(1)}, bf16[512,128]{1,0:T(8,128)(2,1)S(1)}, u32[]{:S(2)}, u32[]{:S(2)}) collective-permute-start(bf16[512,128]{1,0:T(8,128)(2,1)S(1)} %attend.3.rest_6_), channel_id=1, source_target_pairs={{0,1},{1,0},{2,3},{3,2},{4,5},{5,4},{6,7},{7,6},{8,9},{9,8},{10,11... | collective-permute-start | bytes 393224 | tf_op jit(solution)/shard_map/ppermute | solution.py:42
  95.3 11.2 %collective-permute-start.25 = (bf16[512,128]{1,0:T(8,128)(2,1)S(1)}, bf16[512,128]{1,0:T(8,128)(2,1)S(1)}, u32[]{:S(2)}, u32[]{:S(2)}) collective-permute-start(bf16[512,128]{1,0:T(8,128)(2,1)S(1)} %attend.3.rest_6_), channel_id=1, source_target_pairs={{0,2},{1,3},{2,0},{3,1},{4,6},{5,7},{6,4},{7,5},{8,10},{9,11},{10,... | collective-permute-start | bytes 393224 | tf_op jit(solution)/shard_map/ppermute | solution.py:42
  101.1 8.4 %collective-permute-start.27 = (bf16[512,128]{1,0:T(8,128)(2,1)S(1)}, bf16[512,128]{1,0:T(8,128)(2,1)S(1)}, u32[]{:S(2)}, u32[]{:S(2)}) collective-permute-start(bf16[512,128]{1,0:T(8,128)(2,1)S(1)} %attend.3.rest_6_), channel_id=1, source_target_pairs={{0,4},{1,5},{2,6},{3,7},{4,0},{5,1},{6,2},{7,3},{8,12},{9,13},{10,... | collective-permute-start | bytes 393224 | tf_op jit(solution)/shard_map/ppermute | solution.py:42
  101.3 10.0 %collective-permute-start.10 = (bf16[512,128]{1,0:T(8,128)(2,1)S(1)}, bf16[512,128]{1,0:T(8,128)(2,1)S(1)}, u32[]{:S(2)}, u32[]{:S(2)}) collective-permute-start(bf16[512,128]{1,0:T(8,128)(2,1)S(1)} %collective-permute-done.9.rest_0_), channel_id=1, source_target_pairs={{0,2},{1,3},{2,0},{3,1},{4,6},{5,7},{6,4},{7,5},{8,10},{9,11},{10,... | collective-permute-start | bytes 393224 | tf_op jit(solution)/shard_map/ppermute | solution.py:42
  103.8 16.7 %collective-permute-start.31 = (bf16[512,256]{1,0:T(8,128)(2,1)S(1)}, bf16[512,256]{1,0:T(8,128)(2,1)S(1)}, u32[]{:S(2)}, u32[]{:S(2)}) collective-permute-start(bf16[512,256]{1,0:T(8,128)(2,1)S(1)} %collective-permute-done.30.rest_2_), channel_id=1, source_target_pairs={{0,1},{1,0},{2,3},{3,2},{4,5},{5,4},{6,7},{7,6},{8,9},{9,8},{10,11... | collective-permute-start | bytes 786440 | tf_op jit(solution)/shard_map/ppermute | solution.py:42
  106.5 6.8 %collective-permute-start.13 = (bf16[512,128]{1,0:T(8,128)(2,1)S(1)}, bf16[512,128]{1,0:T(8,128)(2,1)S(1)}, u32[]{:S(2)}, u32[]{:S(2)}) collective-permute-start(bf16[512,128]{1,0:T(8,128)(2,1)S(1)} %collective-permute-done.12.rest_3_), channel_id=1, source_target_pairs={{0,2},{1,3},{2,0},{3,1},{4,6},{5,7},{6,4},{7,5},{8,10},{9,11},{10,... | collective-permute-start | bytes 393224 | tf_op jit(solution)/shard_map/ppermute | solution.py:42
  109.5 8.3 %collective-permute-start.21 = (bf16[512,128]{1,0:T(8,128)(2,1)S(1)}, bf16[512,128]{1,0:T(8,128)(2,1)S(1)}, u32[]{:S(2)}, u32[]{:S(2)}) collective-permute-start(bf16[512,128]{1,0:T(8,128)(2,1)S(1)} %collective-permute-done.20.rest_7_), channel_id=1, source_target_pairs={{0,4},{1,5},{2,6},{3,7},{4,0},{5,1},{6,2},{7,3},{8,12},{9,13},{10,... | collective-permute-start | bytes 393224 | tf_op jit(solution)/shard_map/ppermute | solution.py:42
  109.5 8.3 %collective-permute-start.23 = (bf16[512,128]{1,0:T(8,128)(2,1)S(1)}, bf16[512,128]{1,0:T(8,128)(2,1)S(1)}, u32[]{:S(2)}, u32[]{:S(2)}) collective-permute-start(bf16[512,128]{1,0:T(8,128)(2,1)S(1)} %collective-permute-done.9.rest_0_), channel_id=1, source_target_pairs={{0,1},{1,0},{2,3},{3,2},{4,5},{5,4},{6,7},{7,6},{8,9},{9,8},{10,11... | collective-permute-start | bytes 393224 | tf_op jit(solution)/shard_map/ppermute | solution.py:42
  111.3 7.8 %collective-permute-start.24 = (bf16[512,128]{1,0:T(8,128)(2,1)S(1)}, bf16[512,128]{1,0:T(8,128)(2,1)S(1)}, u32[]{:S(2)}, u32[]{:S(2)}) collective-permute-start(bf16[512,128]{1,0:T(8,128)(2,1)S(1)} %collective-permute-done.12.rest_3_), channel_id=1, source_target_pairs={{0,1},{1,0},{2,3},{3,2},{4,5},{5,4},{6,7},{7,6},{8,9},{9,8},{10,11... | collective-permute-start | bytes 393224 | tf_op jit(solution)/shard_map/ppermute | solution.py:42
  113.3 11.7 %collective-permute-start.26 = (bf16[512,128]{1,0:T(8,128)(2,1)S(1)}, bf16[512,128]{1,0:T(8,128)(2,1)S(1)}, u32[]{:S(2)}, u32[]{:S(2)}) collective-permute-start(bf16[512,128]{1,0:T(8,128)(2,1)S(1)} %collective-permute-done.25.rest_8_), channel_id=1, source_target_pairs={{0,1},{1,0},{2,3},{3,2},{4,5},{5,4},{6,7},{7,6},{8,9},{9,8},{10,11... | collective-permute-start | bytes 393224 | tf_op jit(solution)/shard_map/ppermute | solution.py:42
  117.9 7.1 %collective-permute-start.28 = (bf16[512,128]{1,0:T(8,128)(2,1)S(1)}, bf16[512,128]{1,0:T(8,128)(2,1)S(1)}, u32[]{:S(2)}, u32[]{:S(2)}) collective-permute-start(bf16[512,128]{1,0:T(8,128)(2,1)S(1)} %collective-permute-done.27.rest_10_), channel_id=1, source_target_pairs={{0,2},{1,3},{2,0},{3,1},{4,6},{5,7},{6,4},{7,5},{8,10},{9,11},{10,... | collective-permute-start | bytes 393224 | tf_op jit(solution)/shard_map/ppermute | solution.py:42
  117.9 9.3 %collective-permute-start.11 = (bf16[512,128]{1,0:T(8,128)(2,1)S(1)}, bf16[512,128]{1,0:T(8,128)(2,1)S(1)}, u32[]{:S(2)}, u32[]{:S(2)}) collective-permute-start(bf16[512,128]{1,0:T(8,128)(2,1)S(1)} %collective-permute-done.10.rest_2_), channel_id=1, source_target_pairs={{0,1},{1,0},{2,3},{3,2},{4,5},{5,4},{6,7},{7,6},{8,9},{9,8},{10,11... | collective-permute-start | bytes 393224 | tf_op jit(solution)/shard_map/ppermute | solution.py:42
  119.1 8.0 %collective-permute-start.14 = (bf16[512,128]{1,0:T(8,128)(2,1)S(1)}, bf16[512,128]{1,0:T(8,128)(2,1)S(1)}, u32[]{:S(2)}, u32[]{:S(2)}) collective-permute-start(bf16[512,128]{1,0:T(8,128)(2,1)S(1)} %collective-permute-done.13.rest_5_), channel_id=1, source_target_pairs={{0,1},{1,0},{2,3},{3,2},{4,5},{5,4},{6,7},{7,6},{8,9},{9,8},{10,11... | collective-permute-start | bytes 393224 | tf_op jit(solution)/shard_map/ppermute | solution.py:42
  120.5 6.6 %collective-permute-start.22 = (bf16[512,128]{1,0:T(8,128)(2,1)S(1)}, bf16[512,128]{1,0:T(8,128)(2,1)S(1)}, u32[]{:S(2)}, u32[]{:S(2)}) collective-permute-start(bf16[512,128]{1,0:T(8,128)(2,1)S(1)} %collective-permute-done.21.rest_11_), channel_id=1, source_target_pairs={{0,2},{1,3},{2,0},{3,1},{4,6},{5,7},{6,4},{7,5},{8,10},{9,11},{10,... | collective-permute-start | bytes 393224 | tf_op jit(solution)/shard_map/ppermute | solution.py:42
  124.9 2.2 %copy-start.3 = (f32[8,768]{1,0:T(8,128)S(1)}, f32[8,768]{1,0:T(8,128)}, u32[]{:S(2)}) copy-start(f32[8,768]{1,0:T(8,128)} %get-tuple-element.36.rest_4_) | copy-start | bytes 73732
